TPU v7x, 256 devices: a whole 4x4x8 slice. The times are simulated.
256 devices in a mesh: section: 8 (over x, core), wide: 32 (over z, y).
Axes of the slice: x: 4, y: 4, z: 8, core: 2. Of those that a mesh axis runs over, the one named last changes fastest.
Arguments:
- stream: bfloat16 [8, 2048, 2048], P('section', 'wide'), may hold values from -3 to 3
- mixer_gain: float32 [8, 2048], P('section'), may hold values from 0.1 to 1.9
- ssm_weight: bfloat16 [8, 2048, 160], P('section'), may hold values from -0.125 to 0.125
- decay_rate: float32 [8, 32], P('section'), may hold values from 2.4414063e-05 to 0.04
- skip_gain: float32 [8, 32], P('section'), may hold values from 0.5 to 1.5
- mixed_gain: float32 [8, 2048], P('section'), may hold values from 0.1 to 1.9
- ffn_gain: float32 [8, 2048], P('section'), may hold values from 0.1 to 1.9
- router_weight: bfloat16 [8, 2048, 4], P('section'), may hold values from -0.125 to 0.125
- expert_ids: int32 [8, 2048, 2], P('section', 'wide'), may hold values from 0 to 3, all different within a row; in each aligned block of 64 rows (0 to 63, 64 to 127, ..., all dimensions but the last counted through in order) at most 40 rows name the same one
- gate_weight: bfloat16 [8, 2048, 28672], P('section', None, 'wide'), may hold values from -0.125 to 0.125
- up_weight: bfloat16 [8, 2048, 28672], P('section', None, 'wide'), may hold values from -0.125 to 0.125
- down_weight: bfloat16 [8, 28672, 2048], P('section', 'wide'), may hold values from -0.0625 to 0.0625
Outputs:
- carried: bfloat16 [8, 2048, 2048], P('section', 'wide')
Inputs may be any that keep to these rules, and one draw needn't show every extreme that they name: `expert_ids`: A token's 2 experts differ. Among the tokens of one device, no expert is named by more than 40 of them, a bound that some block reaches.
All inputs are finite; a program needn't handle non-finite values.
Results may differ from a plain program's by a relative error of at most 0.0085.
Values may be sent and summed in bfloat16 or wider, within the bound.
No kernel may reach another device: no remote copies, remote signals or barrier semaphores. Data moves between devices by JAX's collectives and lax.ppermute only.
A program may use at most 128 MiB of HBM per device.

v0:
```python
import functools
import math

import jax
import jax.numpy as jnp
from jax import lax
from jax.experimental import pallas as pl
from jax.experimental.pallas import tpu as pltpu
from jax.sharding import Mesh
from jax.sharding import PartitionSpec as P

HEADS = 32
HEAD_DIM = 64
STATE = 64
EXPERTS = 4
TOP = 2
CAP = 40
NZ = 8
NY = 4
WIDE = ("wide_0", "wide_1")
EPSILON = 1e-05
CHUNKS = ((0, 1, 7, 4), (2, 6, 3, 5))


def passed_along(value, axis, by):
    length = lax.axis_size(axis)
    return lax.ppermute(value, axis, [(i, (i + by) % length) for i in range(length)])


def rms_scale(values, gain_row):
    mean_sq = jnp.mean(values * values, axis=-1, keepdims=True)
    return values * lax.rsqrt(mean_sq + EPSILON) * gain_row


def route_slots(id_rows):
    flat_ids = id_rows.reshape(-1)
    one_hot = (
        flat_ids[:, None] == lax.broadcasted_iota(jnp.int32, (flat_ids.shape[0], EXPERTS), 1)
    ).astype(jnp.int32)
    running = jnp.cumsum(one_hot, axis=0) - 1
    slot_ids = jnp.sum(one_hot * running, axis=1)
    return slot_ids


def prefix_kernel(arrived_ref, out_ref):
    def step(k, carry):
        out_ref[k] = carry.astype(jnp.bfloat16)
        block = arrived_ref[k].astype(jnp.float32)
        decay = block[32:33] + block[33:34] + block[34:35]
        return carry * decay + block[:32]

    lax.fori_loop(0, NZ * NY, step, jnp.zeros((32, 128), jnp.float32))


def prefix_states(arrived):
    return pl.pallas_call(
        prefix_kernel,
        out_shape=jax.ShapeDtypeStruct((NZ * NY, 32, 128), jnp.bfloat16),
        in_specs=[pl.BlockSpec(memory_space=pltpu.VMEM)],
        out_specs=pl.BlockSpec(memory_space=pltpu.VMEM),
        name="prefix_states",
    )(arrived)


def carried_states(payload):
    arrived = lax.all_to_all(payload, WIDE, split_axis=0, concat_axis=0, tiled=True)
    back = lax.all_to_all(
        prefix_states(arrived), WIDE, split_axis=0, concat_axis=0, tiled=True
    )
    return back.reshape(16, 2, 32, 128).transpose(1, 2, 0, 3).reshape(STATE, -1)


def head_column(values, head):
    lanes = lax.broadcasted_iota(jnp.int32, values.shape, 1)
    return jnp.sum(jnp.where(lanes == head, values, 0.0), axis=1, keepdims=True)


def pair_columns(values, pair):
    shape = (values.shape[0], 2 * HEAD_DIM)
    lanes = lax.broadcasted_iota(jnp.int32, shape, 1)
    return jnp.where(
        lanes < HEAD_DIM, head_column(values, 2 * pair), head_column(values, 2 * pair + 1)
    )


def ordered(seq_len):
    rows = lax.broadcasted_iota(jnp.int32, (seq_len, seq_len), 0)
    return rows >= lax.broadcasted_iota(jnp.int32, (seq_len, seq_len), 1)


def front_kernel(
    inputs_ref, gain_ref, ssm_ref, rate_ref, payload_ref, normed_ref, maps_ref, step_ref, cum_ref
):
    values = inputs_ref[...].astype(jnp.float32)
    normed = rms_scale(values, gain_ref[...]).astype(jnp.bfloat16)
    normed_ref[...] = normed
    projected = lax.dot_general(
        normed, ssm_ref[...], (((1,), (1,)), ((), ())), preferred_element_type=jnp.float32
    )
    maps_ref[...] = projected[:, : 2 * STATE]
    raw = projected[:, 2 * STATE :]
    step_size = jnp.maximum(raw, 0.0) + jnp.log1p(jnp.exp(-jnp.abs(raw)))
    step_ref[...] = step_size
    seq_len = values.shape[0]
    cumulative = jnp.dot(
        ordered(seq_len).astype(jnp.float32),
        -step_size * rate_ref[...],
        precision=lax.Precision.HIGHEST,
        preferred_element_type=jnp.float32,
    )
    cum_ref[...] = cumulative
    total = cumulative[seq_len - 1 :]
    tail = jnp.exp(total - cumulative) * step_size
    decay = jnp.exp(total)
    b_rows = (projected[:, :STATE] / float(STATE)).astype(jnp.bfloat16)
    row = lax.broadcasted_iota(jnp.int32, (8, 2 * HEAD_DIM), 0)

    def pair_step(pair, carry):
        lanes = pl.ds(pl.multiple_of(pair * 2 * HEAD_DIM, 2 * HEAD_DIM), 2 * HEAD_DIM)
        here = normed_ref[:, lanes].astype(jnp.float32)
        weighted = (pair_columns(tail, pair) * here).astype(jnp.bfloat16)
        state = lax.dot_general(
            b_rows, weighted, (((0,), (0,)), ((), ())), preferred_element_type=jnp.float32
        )
        cols = pair_columns(decay, pair)
        high = cols.astype(jnp.bfloat16).astype(jnp.float32)
        mid = (cols - high).astype(jnp.bfloat16).astype(jnp.float32)
        low = cols - high - mid
        extra = jnp.where(
            row == 0, high, jnp.where(row == 1, mid, jnp.where(row == 2, low, 0.0))
        )
        for half in range(2):
            block = jnp.concatenate([state[half * 32 : half * 32 + 32], extra], axis=0)
            payload_ref[2 * pair + half] = block.astype(jnp.bfloat16)
        return carry

    lax.fori_loop(0, HEADS // 2, pair_step, 0)


def within_kernel(normed_ref, maps_ref, step_ref, cum_ref, skip_ref, out_ref, cum_t, step_t):
    cumulative = cum_ref[...]
    cum_t[...] = cumulative.T
    step_t[...] = step_ref[...].T
    seq_len = cumulative.shape[0]
    mask = ordered(seq_len)
    b_rows = (maps_ref[:, :STATE] / float(STATE)).astype(jnp.bfloat16)
    c_rows = (maps_ref[:, STATE:] / math.sqrt(STATE)).astype(jnp.bfloat16)
    meets = lax.dot_general(
        c_rows, b_rows, (((1,), (1,)), ((), ())), preferred_element_type=jnp.float32
    )

    def pair_step(pair, carry):
        lanes = pl.ds(pl.multiple_of(pair * 2 * HEAD_DIM, 2 * HEAD_DIM), 2 * HEAD_DIM)
        here = normed_ref[:, lanes]
        results = []
        for side in range(2):
            head = 2 * pair + side
            gaps = head_column(cumulative, head) - cum_t[pl.ds(head, 1), :]
            kernel = jnp.where(mask, jnp.exp(jnp.where(mask, gaps, 0.0)), 0.0)
            mixing = (meets * kernel * step_t[pl.ds(head, 1), :]).astype(jnp.bfloat16)
            results.append(jnp.dot(mixing, here, preferred_element_type=jnp.float32))
        left = lax.broadcasted_iota(jnp.int32, results[0].shape, 1) < HEAD_DIM
        skip = pair_columns(skip_ref[...], pair)
        out_ref[:, lanes] = (
            jnp.where(left, results[0], results[1]) + here.astype(jnp.float32) * skip
        )
        return carry

    lax.fori_loop(0, HEADS // 2, pair_step, 0)


def mixer_block(inputs, mixer_gain, ssm_weight, decay_rate, skip_gain, mixed_gain):
    seq_len, features = inputs.shape
    here = pl.BlockSpec(memory_space=pltpu.VMEM)
    payload, normed, maps, step_size, cumulative = pl.pallas_call(
        front_kernel,
        out_shape=[
            jax.ShapeDtypeStruct((NZ * NY, 40, 2 * HEAD_DIM), jnp.bfloat16),
            jax.ShapeDtypeStruct((seq_len, features), jnp.bfloat16),
            jax.ShapeDtypeStruct((seq_len, 2 * STATE), jnp.float32),
            jax.ShapeDtypeStruct((seq_len, HEADS), jnp.float32),
            jax.ShapeDtypeStruct((seq_len, HEADS), jnp.float32),
        ],
        in_specs=[here] * 4,
        out_specs=[here] * 5,
        name="front",
    )(inputs, mixer_gain[None], ssm_weight.T, decay_rate[None])
    carried_in = carried_states(payload)
    within = pl.pallas_call(
        within_kernel,
        out_shape=jax.ShapeDtypeStruct((seq_len, features), jnp.float32),
        in_specs=[here] * 5,
        out_specs=here,
        scratch_shapes=[
            pltpu.VMEM((HEADS, seq_len), jnp.float32),
            pltpu.VMEM((HEADS, seq_len), jnp.float32),
        ],
        cost_estimate=pl.CostEstimate(
            flops=10 * seq_len * seq_len * features,
            transcendentals=seq_len * seq_len * HEADS,
            bytes_accessed=8 * seq_len * features,
        ),
        name="within",
    )(normed, maps, step_size, cumulative, skip_gain[None])
    c_rows = maps[:, STATE:] / math.sqrt(STATE)
    carried_part = jnp.dot(
        c_rows.astype(jnp.bfloat16), carried_in, preferred_element_type=jnp.float32
    ) * jnp.repeat(jnp.exp(cumulative), HEAD_DIM, axis=1)
    return inputs.astype(jnp.float32) + rms_scale(within + carried_part, mixed_gain)


def expert_kernel(sizes, tile, out_tile, *refs):
    n = len(sizes)
    pieces, (gate, up, down), outs = refs[:n], refs[n : n + 3], refs[n + 3 : 2 * n + 3]
    rows, gate_up, downs, hidden, sem_in, sem_down = refs[2 * n + 3 :]
    tiles, out_tiles = gate_up.shape[0], downs.shape[0]

    def copies(i):
        cols = pl.ds(pl.multiple_of(i * tile, tile), tile)
        return (
            pltpu.make_async_copy(
                gate.at[:, cols], gate_up.at[i, :, pl.ds(0, tile)], sem_in.at[i, 0]
            ),
            pltpu.make_async_copy(
                up.at[:, cols], gate_up.at[i, :, pl.ds(tile, tile)], sem_in.at[i, 1]
            ),
        )

    def down_copy(j):
        return pltpu.make_async_copy(
            down.at[:, pl.ds(pl.multiple_of(j * out_tile, out_tile), out_tile)],
            downs.at[j],
            sem_down.at[j],
        )

    for i in range(tiles):
        for copy in copies(i):
            copy.start()
    for j in range(out_tiles):
        down_copy(j).start()
    at = 0
    for piece, size in zip(pieces, sizes):

        def gather(i, carry, piece=piece, at=at):
            rows[pl.ds(pl.multiple_of(at + i * 16, 16), 16)] = piece[
                pl.ds(pl.multiple_of(i * 16, 16), 16)
            ]
            return carry

        lax.fori_loop(0, size // 16, gather, 0)
        at += size

    def first(i, carry):
        for copy in copies(i):
            copy.wait()
        both = jnp.dot(rows[...], gate_up[i], preferred_element_type=jnp.float32)
        gate_pre, up_pre = both[:, :tile], both[:, tile:]
        hidden[:, pl.ds(pl.multiple_of(i * tile, tile), tile)] = (
            jax.nn.silu(gate_pre) * up_pre
        ).astype(jnp.bfloat16)
        return carry

    lax.fori_loop(0, tiles, first, 0)

    def second(j, carry):
        down_copy(j).wait()
        result = jnp.dot(hidden[...], downs[j], preferred_element_type=jnp.float32)
        result = result.astype(jnp.bfloat16)
        at = 0
        for out, size in zip(outs, sizes):
            out[:, pl.ds(pl.multiple_of(j * out_tile, out_tile), out_tile)] = result[at : at + size]
            at += size
        return carry

    lax.fori_loop(0, out_tiles, second, 0)


def expert_rows(pieces, gate_part, up_part, down_part):
    features, width = gate_part.shape
    tile, out_tile = 128, 512
    sizes = tuple(piece.shape[0] for piece in pieces)
    total = sum(sizes)
    here = pl.BlockSpec(memory_space=pltpu.VMEM)
    away = pl.BlockSpec(memory_space=pltpu.HBM)
    return pl.pallas_call(
        functools.partial(expert_kernel, sizes, tile, out_tile),
        out_shape=[jax.ShapeDtypeStruct((size, features), jnp.bfloat16) for size in sizes],
        in_specs=[here] * len(sizes) + [away] * 3,
        out_specs=[here] * len(sizes),
        scratch_shapes=[
            pltpu.VMEM((total, features), jnp.bfloat16),
            pltpu.VMEM((width // tile, features, 2 * tile), jnp.bfloat16),
            pltpu.VMEM((features // out_tile, width, out_tile), jnp.bfloat16),
            pltpu.VMEM((total, width), jnp.bfloat16),
            pltpu.SemaphoreType.DMA((width // tile, 2)),
            pltpu.SemaphoreType.DMA((features // out_tile,)),
        ],
        compiler_params=pltpu.CompilerParams(vmem_limit_bytes=40 * 2**20),
        cost_estimate=pl.CostEstimate(
            flops=6 * total * features * width,
            transcendentals=total * width,
            bytes_accessed=6 * features * width + 4 * total * features,
        ),
        name="expert_rows",
    )(*pieces, gate_part, up_part, down_part)


def join_kernel(*refs):
    blocks, out = refs[:-1], refs[-1]
    rows = blocks[0].shape[0]
    for number, block in enumerate(blocks):

        def copy(i, carry, block=block, at=number * rows):
            out[pl.ds(pl.multiple_of(at + i * 8, 8), 8)] = block[pl.ds(pl.multiple_of(i * 8, 8), 8)]
            return carry

        lax.fori_loop(0, rows // 8, copy, 0)


def joined(blocks):
    rows, features = blocks[0].shape
    here = pl.BlockSpec(memory_space=pltpu.VMEM)
    return pl.pallas_call(
        join_kernel,
        out_shape=jax.ShapeDtypeStruct((rows * len(blocks), features), blocks[0].dtype),
        in_specs=[here] * len(blocks),
        out_specs=here,
        name="join",
    )(*blocks)


def added(one, other):
    return (one.astype(jnp.float32) + other.astype(jnp.float32)).astype(jnp.bfloat16)


def onward(value, back):
    sections = lax.axis_size("section")
    pairs = [
        (s * NZ + z, (s + 1) % sections * NZ + (z - back) % NZ)
        for s in range(sections)
        for z in range(NZ)
    ]
    return lax.ppermute(value, ("section", "wide_0"), pairs)


def homeward(number, o_own, to_left, to_right):
    from_left = passed_along(to_left, "wide_1", -1)
    from_right = passed_along(to_right, "wide_1", 1)
    summed = (
        o_own.astype(jnp.float32) + from_left.astype(jnp.float32) + from_right.astype(jnp.float32)
    ).astype(jnp.bfloat16)
    return {k: summed[i * CAP : (i + 1) * CAP] for i, k in enumerate(CHUNKS[number])}


def weighted_rows(weights, rows):
    high = lax.reduce_precision(weights, 8, 7)
    both = [high.astype(jnp.bfloat16), (weights - high).astype(jnp.bfloat16)]
    return sum(jnp.dot(part, rows, preferred_element_type=jnp.float32) for part in both)


def expert_layer(residual, ffn_gain, router_weight, id_rows, gate_part, up_part, down_part):
    tok_rows = residual.shape[0]
    features = residual.shape[1]
    zi = lax.axis_index("wide_0")
    slots = route_slots(id_rows).reshape(tok_rows, TOP)
    routed = rms_scale(residual, ffn_gain).astype(jnp.bfloat16)
    logits = jnp.dot(routed, router_weight, preferred_element_type=jnp.float32)
    experts = lax.broadcasted_iota(jnp.int32, (tok_rows, EXPERTS), 1)
    signs = (experts == id_rows[:, :1]).astype(jnp.float32) - (
        experts == id_rows[:, 1:]
    ).astype(jnp.float32)
    first_share = jax.nn.sigmoid(jnp.sum(logits * signs, axis=1))
    shares = jnp.stack([first_share, 1.0 - first_share], axis=1)

    col_expert = ((zi + lax.broadcasted_iota(jnp.int32, (NZ, CAP), 0)) % NZ // 2).reshape(-1)
    col_slot = lax.broadcasted_iota(jnp.int32, (NZ, CAP), 1).reshape(-1)
    hits = [
        (id_rows[:, k][:, None] == col_expert[None, :]) & (slots[:, k][:, None] == col_slot[None, :])
        for k in range(TOP)
    ]
    placing = (hits[0] | hits[1]).astype(jnp.bfloat16)
    combine = jnp.where(hits[0], shares[:, 0:1], 0.0) + jnp.where(hits[1], shares[:, 1:2], 0.0)
    packed = lax.dot_general(
        placing, routed, (((0,), (0,)), ((), ())), preferred_element_type=jnp.float32
    ).astype(jnp.bfloat16).reshape(NZ, CAP, features)

    arrived = {}
    for chunk in CHUNKS:
        for k in chunk:
            arrived[k] = packed[0] if k == 0 else passed_along(packed[k], "wide_0", k)
    answers, kept = {}, []

    def finish(number, *sums):
        for k, block in homeward(number, *sums).items():
            if k:
                answers[k] = onward(block, k)
                continue
            own_part = residual + weighted_rows(combine[:, :CAP], block)
            wide = jnp.concatenate(
                [own_part, combine[:, CAP:], jnp.zeros((tok_rows, 104), jnp.float32)], axis=1
            )
            kept.append(onward(wide, 0))

    ahead = None
    for number, chunk in enumerate(CHUNKS):
        own = joined([arrived[k] for k in chunk])
        half = own.shape[0] // 2
        left = passed_along(own, "wide_1", 1)
        right = passed_along(own, "wide_1", -1)
        far_a = passed_along(left[:half], "wide_1", 1)
        far_b = passed_along(right[half:], "wide_1", -1)
        if ahead is not None:
            finish(number - 1, *ahead)
        o_own, o_left, o_right, o_far_a, o_far_b = expert_rows(
            (own, left, right, far_a, far_b), gate_part, up_part, down_part
        )
        mid_a = passed_along(o_far_a, "wide_1", -1)
        mid_b = passed_along(o_far_b, "wide_1", 1)
        to_left = jnp.concatenate([added(o_left[:half], mid_a), o_left[half:]], axis=0)
        to_right = jnp.concatenate([o_right[:half], added(o_right[half:], mid_b)], axis=0)
        ahead = (o_own, to_left, to_right)
    finish(len(CHUNKS) - 1, *ahead)
    stacked = joined([answers[k] for k in range(1, NZ)])
    kept = kept[0]
    rest = kept[:, features : features + (NZ - 1) * CAP]
    return (kept[:, :features] + weighted_rows(rest, stacked)).astype(jnp.bfloat16)


def local(
    stream,
    mixer_gain,
    ssm_weight,
    decay_rate,
    skip_gain,
    mixed_gain,
    ffn_gain,
    router_weight,
    expert_ids,
    gate_weight,
    up_weight,
    down_weight,
):
    residual = mixer_block(
        stream[0], mixer_gain[0], ssm_weight[0], decay_rate[0], skip_gain[0], mixed_gain[0]
    )
    finished = expert_layer(
        residual,
        ffn_gain[0],
        router_weight[0],
        expert_ids[0],
        gate_weight[0],
        up_weight[0],
        down_weight[0],
    )
    return finished[None]


def solution(mesh):
    finer = Mesh(
        mesh.devices.reshape(mesh.shape["section"], NZ, NY), ("section", "wide_0", "wide_1")
    )
    placed = (
        P("section", WIDE, None),
        P("section", None),
        P("section", None, None),
        P("section", None),
        P("section", None),
        P("section", None),
        P("section", None),
        P("section", None, None),
        P("section", WIDE, None),
        P("section", None, WIDE),
        P("section", None, WIDE),
        P("section", WIDE, None),
    )
    return jax.shard_map(
        local, mesh=finer, in_specs=placed, out_specs=P("section", WIDE, None), check_vma=False
    )
```

profile of v0, /device:TPU:24, one launch (start us, length us, event | category | flops | bytes accessed | tf_op | source)
XLA Modules:
  0.0 223.1 jit_solution(13734330650417477688)
XLA Ops:
  0.0 6.0 %front.1 = (bf16[32,40,128]{2,1,0:T(8,128)(2,1)}, bf16[64,2048]{1,0:T(8,128)(2,1)}, f32[64,128]{1,0:T(8,128)}, f32[64,32]{1,0:T(8,128)}, f32[64,32]{1,0:T(8,128)}) custom-call(bf16[64,2048]{1,0:T(8,128)(2,1)} %bitcast.45, f32[1,2048]{1,0:T(1,128)} %gain_ref.1, bf16[160,2048]{1,0:T(8,128)(2,1)} %bitcast.48, f32[1,32]{1,0:T(1,128)} %rate_ref.1), custom_call_target="tpu_custom_call" | custom-call | tf_op jit(solution)/shard_map/front/pallas_call | solution.py:175
  6.1 11.6 %all-to-all-start = ((bf16[32,40,128]{2,1,0:T(8,128)(2,1)}), bf16[32,40,128]{2,1,0:T(8,128)(2,1)S(1)}, u32[]{:S(2)}, u32[]{:S(2)}) async-start(bf16[32,40,128]{2,1,0:T(8,128)(2,1)} %get-tuple-element.24), calls=%async_computation | async-start | bytes 655360 | tf_op jit(solution)/shard_map/all_to_all | solution.py:66
  18.7 11.6 %all-to-all-done.arrived_ref = bf16[32,40,128]{2,1,0:T(8,128)(2,1)S(1)} async-done(((bf16[32,40,128]{2,1,0:T(8,128)(2,1)}), bf16[32,40,128]{2,1,0:T(8,128)(2,1)S(1)}, u32[]{:S(2)}, u32[]{:S(2)}) %all-to-all-start) | async-done | bytes 327712 | tf_op jit(solution)/shard_map/all_to_all | solution.py:66
  31.0 2.0 prefix_states.1
  33.0 5.6 %all-to-all-start.1 = ((bf16[32,32,128]{2,1,0:T(8,128)(2,1)}), bf16[32,32,128]{2,1,0:T(8,128)(2,1)S(1)}, u32[]{:S(2)}, u32[]{:S(2)}) async-start(bf16[32,32,128]{2,1,0:T(8,128)(2,1)} %prefix_states.1), calls=%async_computation.1 | async-start | bytes 524288 | tf_op jit(solution)/shard_map/all_to_all | solution.py:67
  39.5 5.5 %within.1 = f32[64,2048]{1,0:T(8,128)} custom-call(bf16[64,2048]{1,0:T(8,128)(2,1)} %get-tuple-element.20.normed_ref, f32[64,128]{1,0:T(8,128)} %get-tuple-element.21.maps_ref, f32[64,32]{1,0:T(8,128)} %get-tuple-element.22.step_ref, f32[64,32]{1,0:T(8,128)} %get-tuple-element.23.cum_ref, f32[1,32]{1,0:T(1,128)} %skip_ref.1), custom_call_target="tpu_custom_call" | custom-call | flops 83886080 | bytes 1048576 | tf_op jit(solution)/shard_map/within/pallas_call | solution.py:189
  45.1 4.1 %all-to-all-done.1 = bf16[32,32,128]{2,1,0:T(8,128)(2,1)S(1)} async-done(((bf16[32,32,128]{2,1,0:T(8,128)(2,1)}), bf16[32,32,128]{2,1,0:T(8,128)(2,1)S(1)}, u32[]{:S(2)}, u32[]{:S(2)}) %all-to-all-start.1) | async-done | bytes 262176 | tf_op jit(solution)/shard_map/all_to_all | solution.py:67
  49.4 1.4 multiply_reduce_fusion.1
  51.8 0.8 fusion.29
  53.3 3.5 %collective-permute-start.14 = (bf16[40,2048]{1,0:T(8,128)(2,1)S(1)}, bf16[40,2048]{1,0:T(8,128)(2,1)S(1)}, u32[]{:S(2)}, u32[]{:S(2)}) collective-permute-start(bf16[40,2048]{1,0:T(8,128)(2,1)S(1)} %get-tuple-element.41), channel_id=1, source_target_pairs={{0,24},{4,28},{8,0},{12,4},{16,8},{20,12},{24,16},{28,20},{1,25},{... | collective-permute-start | bytes 491528 | tf_op jit(solution)/shard_map/ppermute | solution.py:27
  56.7 5.0 %collective-permute-start.16 = (bf16[40,2048]{1,0:T(8,128)(2,1)S(1)}, bf16[40,2048]{1,0:T(8,128)(2,1)S(1)}, u32[]{:S(2)}, u32[]{:S(2)}) collective-permute-start(bf16[40,2048]{1,0:T(8,128)(2,1)S(1)} %get-tuple-element.39), channel_id=1, source_target_pairs={{0,20},{4,24},{8,28},{12,0},{16,4},{20,8},{24,12},{28,16},{1,21},{... | collective-permute-start | bytes 491528 | tf_op jit(solution)/shard_map/ppermute | solution.py:27
  61.8 3.6 %collective-permute-done.13.refs_0_ = bf16[40,2048]{1,0:T(8,128)(2,1)S(1)} collective-permute-done((bf16[40,2048]{1,0:T(8,128)(2,1)S(1)}, bf16[40,2048]{1,0:T(8,128)(2,1)S(1)}, u32[]{:S(2)}, u32[]{:S(2)}) %collective-permute-start.13) | collective-permute-done | bytes 163872 | tf_op jit(solution)/shard_map/ppermute | solution.py:27
  65.4 3.1 %collective-permute-done.14.refs_1_ = bf16[40,2048]{1,0:T(8,128)(2,1)S(1)} collective-permute-done((bf16[40,2048]{1,0:T(8,128)(2,1)S(1)}, bf16[40,2048]{1,0:T(8,128)(2,1)S(1)}, u32[]{:S(2)}, u32[]{:S(2)}) %collective-permute-start.14) | collective-permute-done | bytes 163872 | tf_op jit(solution)/shard_map/ppermute | solution.py:27
  68.5 3.5 %collective-permute-done.15.refs_2_ = bf16[40,2048]{1,0:T(8,128)(2,1)S(1)} collective-permute-done((bf16[40,2048]{1,0:T(8,128)(2,1)S(1)}, bf16[40,2048]{1,0:T(8,128)(2,1)S(1)}, u32[]{:S(2)}, u32[]{:S(2)}) %collective-permute-start.15) | collective-permute-done | bytes 163872 | tf_op jit(solution)/shard_map/ppermute | solution.py:27
  73.2 2.1 join.4.refs_0_
  75.4 1.3 collective-permute-start.17
  77.4 1.5 collective-permute-start
  78.9 1.7 collective-permute-start.1
  80.6 3.1 %collective-permute-start.2 = (bf16[40,2048]{1,0:T(8,128)(2,1)S(1)}, bf16[40,2048]{1,0:T(8,128)(2,1)S(1)}, u32[]{:S(2)}, u32[]{:S(2)}) collective-permute-start(bf16[40,2048]{1,0:T(8,128)(2,1)S(1)} %get-tuple-element.43), channel_id=1, source_target_pairs={{0,16},{4,20},{8,24},{12,28},{16,0},{20,4},{24,8},{28,12},{1,17},{... | collective-permute-start | bytes 491528 | tf_op jit(solution)/shard_map/ppermute | solution.py:27
  83.9 2.4 %collective-permute-done.1.refs_2_ = bf16[40,2048]{1,0:T(8,128)(2,1)S(1)} collective-permute-done((bf16[40,2048]{1,0:T(8,128)(2,1)S(1)}, bf16[40,2048]{1,0:T(8,128)(2,1)S(1)}, u32[]{:S(2)}, u32[]{:S(2)}) %collective-permute-start.1) | collective-permute-done | bytes 163872 | tf_op jit(solution)/shard_map/ppermute | solution.py:27
  86.4 7.0 %collective-permute-done.2.refs_3_ = bf16[40,2048]{1,0:T(8,128)(2,1)S(1)} collective-permute-done((bf16[40,2048]{1,0:T(8,128)(2,1)S(1)}, bf16[40,2048]{1,0:T(8,128)(2,1)S(1)}, u32[]{:S(2)}, u32[]{:S(2)}) %collective-permute-start.2) | collective-permute-done | bytes 163872 | tf_op jit(solution)/shard_map/ppermute | solution.py:27
  94.0 2.1 join.3.refs_0_
  96.1 3.0 %collective-permute-start.3 = (bf16[160,2048]{1,0:T(8,128)(2,1)}, bf16[160,2048]{1,0:T(8,128)(2,1)S(1)}, u32[]{:S(2)}, u32[]{:S(2)}) collective-permute-start(bf16[160,2048]{1,0:T(8,128)(2,1)} %join.3.refs_0_), channel_id=1, source_target_pairs={{0,1},{1,2},{2,3},{3,0},{4,5},{5,6},{6,7},{7,4},{8,9},{9,10},{10,1... | collective-permute-start | bytes 1966088 | tf_op jit(solution)/shard_map/ppermute | solution.py:27
  99.4 3.3 %collective-permute-start.19 = (bf16[80,2048]{1,0:T(8,128)(2,1)S(1)}, bf16[80,2048]{1,0:T(8,128)(2,1)S(1)}, u32[]{:S(2)}, u32[]{:S(2)}) collective-permute-start(bf16[80,2048]{1,0:T(8,128)(2,1)S(1)} %slice.176), channel_id=1, source_target_pairs={{0,1},{1,2},{2,3},{3,0},{4,5},{5,6},{6,7},{7,4},{8,9},{9,10},{10,1... | collective-permute-start | bytes 983048 | tf_op jit(solution)/shard_map/ppermute | solution.py:27
  103.1 11.4 %collective-permute-done.3.refs_1_ = bf16[160,2048]{1,0:T(8,128)(2,1)S(1)} collective-permute-done((bf16[160,2048]{1,0:T(8,128)(2,1)}, bf16[160,2048]{1,0:T(8,128)(2,1)S(1)}, u32[]{:S(2)}, u32[]{:S(2)}) %collective-permute-start.3) | collective-permute-done | bytes 655392 | tf_op jit(solution)/shard_map/ppermute | solution.py:27
  114.5 3.7 %collective-permute-start.5 = (bf16[80,2048]{1,0:T(8,128)(2,1)S(1)}, bf16[80,2048]{1,0:T(8,128)(2,1)S(1)}, u32[]{:S(2)}, u32[]{:S(2)}) collective-permute-start(bf16[80,2048]{1,0:T(8,128)(2,1)S(1)} %slice.165), channel_id=1, source_target_pairs={{0,1},{1,2},{2,3},{3,0},{4,5},{5,6},{6,7},{7,4},{8,9},{9,10},{10,1... | collective-permute-start | bytes 983048 | tf_op jit(solution)/shard_map/ppermute | solution.py:27
  118.5 2.9 %collective-permute-done.20.refs_4_ = bf16[80,2048]{1,0:T(8,128)(2,1)S(1)} collective-permute-done((bf16[80,2048]{1,0:T(8,128)(2,1)S(1)}, bf16[80,2048]{1,0:T(8,128)(2,1)S(1)}, u32[]{:S(2)}, u32[]{:S(2)}) %collective-permute-start.20) | collective-permute-done | bytes 327712 | tf_op jit(solution)/shard_map/ppermute | solution.py:27
  121.4 2.0 copy-done.3
  123.5 2.0 copy-done.4
  125.5 11.1 %expert_rows.3 = (bf16[160,2048]{1,0:T(8,128)(2,1)S(1)}, bf16[160,2048]{1,0:T(8,128)(2,1)S(1)}, bf16[160,2048]{1,0:T(8,128)(2,1)S(1)}, bf16[80,2048]{1,0:T(8,128)(2,1)S(1)}, bf16[80,2048]{1,0:T(8,128)(2,1)S(1)}) custom-call(bf16[160,2048]{1,0:T(8,128)(2,1)S(1)} %copy-done.1, bf16[160,2048]{1,0:T(8,128)(2,1)S(1)} %collective-permute-done.17.refs_1_, ...), custom_call_target="tpu_custom_call" | custom-call | flops 7046430720 | bytes 16252928 | tf_op jit(solution)/shard_map/expert_rows/pallas_call | solution.py:285
  136.8 3.3 %collective-permute-start.23 = (bf16[80,2048]{1,0:T(8,128)(2,1)S(1)}, bf16[80,2048]{1,0:T(8,128)(2,1)S(1)}, u32[]{:S(2)}, u32[]{:S(2)}) collective-permute-start(bf16[80,2048]{1,0:T(8,128)(2,1)S(1)} %get-tuple-element.34), channel_id=1, source_target_pairs={{0,1},{1,2},{2,3},{3,0},{4,5},{5,6},{6,7},{7,4},{8,9},{9,10},{10,1... | collective-permute-start | bytes 983048 | tf_op jit(solution)/shard_map/ppermute | solution.py:27
  140.1 11.1 %expert_rows.2 = (bf16[160,2048]{1,0:T(8,128)(2,1)S(1)}, bf16[160,2048]{1,0:T(8,128)(2,1)S(1)}, bf16[160,2048]{1,0:T(8,128)(2,1)S(1)}, bf16[80,2048]{1,0:T(8,128)(2,1)S(1)}, bf16[80,2048]{1,0:T(8,128)(2,1)S(1)}) custom-call(bf16[160,2048]{1,0:T(8,128)(2,1)S(1)} %copy-done.2, bf16[160,2048]{1,0:T(8,128)(2,1)S(1)} %collective-permute-done.3.refs_1_, ...), custom_call_target="tpu_custom_call" | custom-call | flops 7046430720 | bytes 16252928 | tf_op jit(solution)/shard_map/expert_rows/pallas_call | solution.py:285
  151.3 3.3 %collective-permute-start.9 = (bf16[80,2048]{1,0:T(8,128)(2,1)S(1)}, bf16[80,2048]{1,0:T(8,128)(2,1)S(1)}, u32[]{:S(2)}, u32[]{:S(2)}) collective-permute-start(bf16[80,2048]{1,0:T(8,128)(2,1)S(1)} %get-tuple-element.29), channel_id=1, source_target_pairs={{0,1},{1,2},{2,3},{3,0},{4,5},{5,6},{6,7},{7,4},{8,9},{9,10},{10,1... | collective-permute-start | bytes 983048 | tf_op jit(solution)/shard_map/ppermute | solution.py:27
  155.3 3.3 %collective-permute-start.24 = (bf16[160,2048]{1,0:T(8,128)(2,1)S(1)}, bf16[160,2048]{1,0:T(8,128)(2,1)S(1)}, u32[]{:S(2)}, u32[]{:S(2)}) collective-permute-start(bf16[160,2048]{1,0:T(8,128)(2,1)S(1)} %pad_maximum_fusion.3), channel_id=1, source_target_pairs={{0,1},{1,2},{2,3},{3,0},{4,5},{5,6},{6,7},{7,4},{8,9},{9,10},{10,1... | collective-permute-start | bytes 1966088 | tf_op jit(solution)/shard_map/ppermute | solution.py:27
  158.6 4.5 %collective-permute-done.7 = bf16[80,2048]{1,0:T(8,128)(2,1)S(1)} collective-permute-done((bf16[80,2048]{1,0:T(8,128)(2,1)S(1)}, bf16[80,2048]{1,0:T(8,128)(2,1)S(1)}, u32[]{:S(2)}, u32[]{:S(2)}) %collective-permute-start.7) | collective-permute-done | bytes 327712 | tf_op jit(solution)/shard_map/ppermute | solution.py:27
  163.5 3.3 %collective-permute-start.10 = (bf16[160,2048]{1,0:T(8,128)(2,1)S(1)}, bf16[160,2048]{1,0:T(8,128)(2,1)S(1)}, u32[]{:S(2)}, u32[]{:S(2)}) collective-permute-start(bf16[160,2048]{1,0:T(8,128)(2,1)S(1)} %pad_maximum_fusion.1), channel_id=1, source_target_pairs={{0,1},{1,2},{2,3},{3,0},{4,5},{5,6},{6,7},{7,4},{8,9},{9,10},{10,1... | collective-permute-start | bytes 1966088 | tf_op jit(solution)/shard_map/ppermute | solution.py:27
  166.8 6.3 %collective-permute-done.22 = bf16[160,2048]{1,0:T(8,128)(2,1)S(1)} collective-permute-done((bf16[160,2048]{1,0:T(8,128)(2,1)S(1)}, bf16[160,2048]{1,0:T(8,128)(2,1)S(1)}, u32[]{:S(2)}, u32[]{:S(2)}) %collective-permute-start.22) | collective-permute-done | bytes 655392 | tf_op jit(solution)/shard_map/ppermute | solution.py:27
  173.6 6.7 %collective-permute-start.26 = (bf16[40,2048]{1,0:T(8,128)(2,1)S(1)}, bf16[40,2048]{1,0:T(8,128)(2,1)S(1)}, u32[]{:S(2)}, u32[]{:S(2)}) collective-permute-start(bf16[40,2048]{1,0:T(8,128)(2,1)S(1)} %get-tuple-element.52), channel_id=1, source_target_pairs={{0,52},{4,56},{8,60},{12,32},{16,36},{20,40},{24,44},{28,48},{32,8... | collective-permute-start | bytes 491528 | tf_op jit(solution)/shard_map/ppermute | solution.py:343
  181.1 3.6 %collective-permute-start.11 = (f32[64,2432]{1,0:T(8,128)S(1)}, f32[64,2432]{1,0:T(8,128)}, u32[]{:S(2)}, u32[]{:S(2)}) collective-permute-start(f32[64,2432]{1,0:T(8,128)S(1)} %concatenate.17), channel_id=1, source_target_pairs={{0,32},{4,36},{8,40},{12,44},{16,48},{20,52},{24,56},{28,60},{32,6... | collective-permute-start | bytes 1867784 | tf_op jit(solution)/shard_map/ppermute | solution.py:343
  184.7 6.0 %collective-permute-start.29 = (bf16[40,2048]{1,0:T(8,128)(2,1)S(1)}, bf16[40,2048]{1,0:T(8,128)(2,1)S(1)}, u32[]{:S(2)}, u32[]{:S(2)}) collective-permute-start(bf16[40,2048]{1,0:T(8,128)(2,1)S(1)} %get-tuple-element.50), channel_id=1, source_target_pairs={{0,40},{4,44},{8,48},{12,52},{16,56},{20,60},{24,32},{28,36},{32,7... | collective-permute-start | bytes 491528 | tf_op jit(solution)/shard_map/ppermute | solution.py:343
  190.7 1.9 collective-permute-start.12
  192.7 6.3 %collective-permute-start.27 = (bf16[40,2048]{1,0:T(8,128)(2,1)S(1)}, bf16[40,2048]{1,0:T(8,128)(2,1)S(1)}, u32[]{:S(2)}, u32[]{:S(2)}) collective-permute-start(bf16[40,2048]{1,0:T(8,128)(2,1)S(1)} %get-tuple-element.48), channel_id=1, source_target_pairs={{0,48},{4,52},{8,56},{12,60},{16,32},{20,36},{24,40},{28,44},{32,8... | collective-permute-start | bytes 491528 | tf_op jit(solution)/shard_map/ppermute | solution.py:343
  199.0 4.6 %collective-permute-done.29.refs_5_ = bf16[40,2048]{1,0:T(8,128)(2,1)S(1)} collective-permute-done((bf16[40,2048]{1,0:T(8,128)(2,1)S(1)}, bf16[40,2048]{1,0:T(8,128)(2,1)S(1)}, u32[]{:S(2)}, u32[]{:S(2)}) %collective-permute-start.29) | collective-permute-done | bytes 163872 | tf_op jit(solution)/shard_map/ppermute | solution.py:343
  203.6 5.2 %collective-permute-done.27.refs_3_ = bf16[40,2048]{1,0:T(8,128)(2,1)S(1)} collective-permute-done((bf16[40,2048]{1,0:T(8,128)(2,1)S(1)}, bf16[40,2048]{1,0:T(8,128)(2,1)S(1)}, u32[]{:S(2)}, u32[]{:S(2)}) %collective-permute-start.27) | collective-permute-done | bytes 163872 | tf_op jit(solution)/shard_map/ppermute | solution.py:343
  208.9 6.8 %collective-permute-done.30.refs_6_ = bf16[40,2048]{1,0:T(8,128)(2,1)S(1)} collective-permute-done((bf16[40,2048]{1,0:T(8,128)(2,1)S(1)}, bf16[40,2048]{1,0:T(8,128)(2,1)S(1)}, u32[]{:S(2)}, u32[]{:S(2)}) %collective-permute-start.30) | collective-permute-done | bytes 163872 | tf_op jit(solution)/shard_map/ppermute | solution.py:343
  216.4 2.6 %join.5 = bf16[280,2048]{1,0:T(8,128)(2,1)} custom-call(bf16[40,2048]{1,0:T(8,128)(2,1)} %copy-done.12, bf16[40,2048]{1,0:T(8,128)(2,1)} %copy-done.8, bf16[40,2048]{1,0:T(8,128)(2,1)} %copy-done.9, bf16[40,2048]{1,0:T(8,128)(2,1)} %copy-done.13, bf16[40,2048]{1,0:T(8,128)(2,1)} %copy-done.10, bf16[40,2048]{1,0:T(8,128)(2,1)} %copy-done.11, ...), custom_call_target="tpu_custom_call" | custom-call | tf_op jit(solution)/shard_map/join/pallas_call | solution.py:323
  219.0 1.8 fusion.13
  220.8 2.2 %fusion.4 = bf16[1,64,2048]{2,1,0:T(8,128)(2,1)} fusion(f32[64,2432]{1,0:T(8,128)} %collective-permute-done.11, f32[64,2048]{1,0:T(8,128)S(1)} %fusion.13, bf16[280,2048]{1,0:T(8,128)(2,1)S(1)} %copy-done.5), kind=kOutput, calls=%fused_computation.24 | convolution fusion | flops 73829376 | bytes 2555904 | tf_op jit(solution)/shard_map/dot_general | solution.py:358
  (134 shorter events, 11.7 us)
Async XLA Ops:
  0.0 99.1 %copy-start = (bf16[1,2048,4]{1,2,0:T(4,128)(2,1)S(1)}, bf16[1,2048,4]{1,2,0:T(4,128)(2,1)}, u32[]{:S(2)}) copy-start(bf16[1,2048,4]{1,2,0:T(4,128)(2,1)} %param.19) | copy-start | bytes 49156
  0.0 17.7 %copy-start.26 = (s32[1,64,2]{1,2,0:T(2,128)S(1)}, s32[1,64,2]{1,2,0:T(2,128)}, u32[]{:S(2)}) copy-start(s32[1,64,2]{1,2,0:T(2,128)} %param.20) | copy-start | bytes 1540
  6.1 32.5 %copy-start.23 = (f32[64,32]{1,0:T(8,128)S(1)}, f32[64,32]{1,0:T(8,128)}, u32[]{:S(2)}) copy-start(f32[64,32]{1,0:T(8,128)} %get-tuple-element.23.cum_ref) | copy-start | bytes 24580
  6.1 24.2 %all-to-all-start = ((bf16[32,40,128]{2,1,0:T(8,128)(2,1)}), bf16[32,40,128]{2,1,0:T(8,128)(2,1)S(1)}, u32[]{:S(2)}, u32[]{:S(2)}) async-start(bf16[32,40,128]{2,1,0:T(8,128)(2,1)} %get-tuple-element.24), calls=%async_computation | async-start | bytes 655360 | tf_op jit(solution)/shard_map/all_to_all | solution.py:66
  33.0 16.2 %all-to-all-start.1 = ((bf16[32,32,128]{2,1,0:T(8,128)(2,1)}), bf16[32,32,128]{2,1,0:T(8,128)(2,1)S(1)}, u32[]{:S(2)}, u32[]{:S(2)}) async-start(bf16[32,32,128]{2,1,0:T(8,128)(2,1)} %prefix_states.1), calls=%async_computation.1 | async-start | bytes 524288 | tf_op jit(solution)/shard_map/all_to_all | solution.py:67
  38.9 10.4 %copy-start.22 = (f32[64,128]{1,0:T(8,128)S(1)}, f32[64,128]{1,0:T(8,128)}, u32[]{:S(2)}) copy-start(f32[64,128]{1,0:T(8,128)} %get-tuple-element.21.maps_ref) | copy-start | bytes 98308
  52.6 12.8 %collective-permute-start.13 = (bf16[40,2048]{1,0:T(8,128)(2,1)S(1)}, bf16[40,2048]{1,0:T(8,128)(2,1)S(1)}, u32[]{:S(2)}, u32[]{:S(2)}) collective-permute-start(bf16[40,2048]{1,0:T(8,128)(2,1)S(1)} %get-tuple-element.42), channel_id=1, source_target_pairs={{0,8},{4,12},{8,16},{12,20},{16,24},{20,28},{24,0},{28,4},{1,9},{5... | collective-permute-start | bytes 491528 | tf_op jit(solution)/shard_map/ppermute | solution.py:27
  53.3 15.2 %collective-permute-start.14 = (bf16[40,2048]{1,0:T(8,128)(2,1)S(1)}, bf16[40,2048]{1,0:T(8,128)(2,1)S(1)}, u32[]{:S(2)}, u32[]{:S(2)}) collective-permute-start(bf16[40,2048]{1,0:T(8,128)(2,1)S(1)} %get-tuple-element.41), channel_id=1, source_target_pairs={{0,24},{4,28},{8,0},{12,4},{16,8},{20,12},{24,16},{28,20},{1,25},{... | collective-permute-start | bytes 491528 | tf_op jit(solution)/shard_map/ppermute | solution.py:27
  56.7 15.2 %collective-permute-start.15 = (bf16[40,2048]{1,0:T(8,128)(2,1)S(1)}, bf16[40,2048]{1,0:T(8,128)(2,1)S(1)}, u32[]{:S(2)}, u32[]{:S(2)}) collective-permute-start(bf16[40,2048]{1,0:T(8,128)(2,1)S(1)} %get-tuple-element.40), channel_id=1, source_target_pairs={{0,12},{4,16},{8,20},{12,24},{16,28},{20,0},{24,4},{28,8},{1,13},{... | collective-permute-start | bytes 491528 | tf_op jit(solution)/shard_map/ppermute | solution.py:27
  56.7 15.2 %collective-permute-start.16 = (bf16[40,2048]{1,0:T(8,128)(2,1)S(1)}, bf16[40,2048]{1,0:T(8,128)(2,1)S(1)}, u32[]{:S(2)}, u32[]{:S(2)}) collective-permute-start(bf16[40,2048]{1,0:T(8,128)(2,1)S(1)} %get-tuple-element.39), channel_id=1, source_target_pairs={{0,20},{4,24},{8,28},{12,0},{16,4},{20,8},{24,12},{28,16},{1,21},{... | collective-permute-start | bytes 491528 | tf_op jit(solution)/shard_map/ppermute | solution.py:27
  65.4 6.6 %copy-start.15 = (bf16[40,2048]{1,0:T(8,128)(2,1)}, bf16[40,2048]{1,0:T(8,128)(2,1)S(1)}, u32[]{:S(2)}) copy-start(bf16[40,2048]{1,0:T(8,128)(2,1)S(1)} %collective-permute-done.13.refs_0_) | copy-start | bytes 491524
  75.4 24.0 %collective-permute-start.17 = (bf16[160,2048]{1,0:T(8,128)(2,1)}, bf16[160,2048]{1,0:T(8,128)(2,1)S(1)}, u32[]{:S(2)}, u32[]{:S(2)}) collective-permute-start(bf16[160,2048]{1,0:T(8,128)(2,1)} %join.4.refs_0_), channel_id=1, source_target_pairs={{0,1},{1,2},{2,3},{3,0},{4,5},{5,6},{6,7},{7,4},{8,9},{9,10},{10,1... | collective-permute-start | bytes 1966088 | tf_op jit(solution)/shard_map/ppermute | solution.py:27
  76.6 26.1 %collective-permute-start.18 = (bf16[160,2048]{1,0:T(8,128)(2,1)}, bf16[160,2048]{1,0:T(8,128)(2,1)S(1)}, u32[]{:S(2)}, u32[]{:S(2)}) collective-permute-start(bf16[160,2048]{1,0:T(8,128)(2,1)} %join.4.refs_0_), channel_id=1, source_target_pairs={{0,3},{1,0},{2,1},{3,2},{4,7},{5,4},{6,5},{7,6},{8,11},{9,8},{10,9... | collective-permute-start | bytes 1966088 | tf_op jit(solution)/shard_map/ppermute | solution.py:27
  77.4 6.5 %collective-permute-start = (bf16[40,2048]{1,0:T(8,128)(2,1)S(1)}, bf16[40,2048]{1,0:T(8,128)(2,1)S(1)}, u32[]{:S(2)}, u32[]{:S(2)}) collective-permute-start(bf16[40,2048]{1,0:T(8,128)(2,1)S(1)} %get-tuple-element.45), channel_id=1, source_target_pairs={{0,4},{4,8},{8,12},{12,16},{16,20},{20,24},{24,28},{28,0},{1,5},{5... | collective-permute-start | bytes 491528 | tf_op jit(solution)/shard_map/ppermute | solution.py:27
  78.9 7.5 %collective-permute-start.1 = (bf16[40,2048]{1,0:T(8,128)(2,1)S(1)}, bf16[40,2048]{1,0:T(8,128)(2,1)S(1)}, u32[]{:S(2)}, u32[]{:S(2)}) collective-permute-start(bf16[40,2048]{1,0:T(8,128)(2,1)S(1)} %get-tuple-element.44), channel_id=1, source_target_pairs={{0,28},{4,0},{8,4},{12,8},{16,12},{20,16},{24,20},{28,24},{1,29},{... | collective-permute-start | bytes 491528 | tf_op jit(solution)/shard_map/ppermute | solution.py:27
  80.6 12.7 %collective-permute-start.2 = (bf16[40,2048]{1,0:T(8,128)(2,1)S(1)}, bf16[40,2048]{1,0:T(8,128)(2,1)S(1)}, u32[]{:S(2)}, u32[]{:S(2)}) collective-permute-start(bf16[40,2048]{1,0:T(8,128)(2,1)S(1)} %get-tuple-element.43), channel_id=1, source_target_pairs={{0,16},{4,20},{8,24},{12,28},{16,0},{20,4},{24,8},{28,12},{1,17},{... | collective-permute-start | bytes 491528 | tf_op jit(solution)/shard_map/ppermute | solution.py:27
  83.9 9.4 %copy-start.18 = (bf16[40,2048]{1,0:T(8,128)(2,1)}, bf16[40,2048]{1,0:T(8,128)(2,1)S(1)}, u32[]{:S(2)}) copy-start(bf16[40,2048]{1,0:T(8,128)(2,1)S(1)} %collective-permute-done.refs_1_) | copy-start | bytes 491524
  86.3 7.0 %copy-start.20 = (bf16[40,2048]{1,0:T(8,128)(2,1)}, bf16[40,2048]{1,0:T(8,128)(2,1)S(1)}, u32[]{:S(2)}) copy-start(bf16[40,2048]{1,0:T(8,128)(2,1)S(1)} %collective-permute-done.1.refs_2_) | copy-start | bytes 491524
  96.1 18.4 %collective-permute-start.3 = (bf16[160,2048]{1,0:T(8,128)(2,1)}, bf16[160,2048]{1,0:T(8,128)(2,1)S(1)}, u32[]{:S(2)}, u32[]{:S(2)}) collective-permute-start(bf16[160,2048]{1,0:T(8,128)(2,1)} %join.3.refs_0_), channel_id=1, source_target_pairs={{0,1},{1,2},{2,3},{3,0},{4,5},{5,6},{6,7},{7,4},{8,9},{9,10},{10,1... | collective-permute-start | bytes 1966088 | tf_op jit(solution)/shard_map/ppermute | solution.py:27
  99.1 19.1 %collective-permute-start.4 = (bf16[160,2048]{1,0:T(8,128)(2,1)}, bf16[160,2048]{1,0:T(8,128)(2,1)S(1)}, u32[]{:S(2)}, u32[]{:S(2)}) collective-permute-start(bf16[160,2048]{1,0:T(8,128)(2,1)} %join.3.refs_0_), channel_id=1, source_target_pairs={{0,3},{1,0},{2,1},{3,2},{4,7},{5,4},{6,5},{7,6},{8,11},{9,8},{10,9... | collective-permute-start | bytes 1966088 | tf_op jit(solution)/shard_map/ppermute | solution.py:27
  99.4 22.0 %copy-start.1 = (bf16[160,2048]{1,0:T(8,128)(2,1)S(1)}, bf16[160,2048]{1,0:T(8,128)(2,1)}, u32[]{:S(2)}) copy-start(bf16[160,2048]{1,0:T(8,128)(2,1)} %join.4.refs_0_) | copy-start | bytes 1966084
  99.4 19.1 %collective-permute-start.19 = (bf16[80,2048]{1,0:T(8,128)(2,1)S(1)}, bf16[80,2048]{1,0:T(8,128)(2,1)S(1)}, u32[]{:S(2)}, u32[]{:S(2)}) collective-permute-start(bf16[80,2048]{1,0:T(8,128)(2,1)S(1)} %slice.176), channel_id=1, source_target_pairs={{0,1},{1,2},{2,3},{3,0},{4,5},{5,6},{6,7},{7,4},{8,9},{9,10},{10,1... | collective-permute-start | bytes 983048 | tf_op jit(solution)/shard_map/ppermute | solution.py:27
  102.8 18.7 %collective-permute-start.20 = (bf16[80,2048]{1,0:T(8,128)(2,1)S(1)}, bf16[80,2048]{1,0:T(8,128)(2,1)S(1)}, u32[]{:S(2)}, u32[]{:S(2)}) collective-permute-start(bf16[80,2048]{1,0:T(8,128)(2,1)S(1)} %slice.177), channel_id=1, source_target_pairs={{0,3},{1,0},{2,1},{3,2},{4,7},{5,4},{6,5},{7,6},{8,11},{9,8},{10,9... | collective-permute-start | bytes 983048 | tf_op jit(solution)/shard_map/ppermute | solution.py:27
  114.5 25.5 %collective-permute-start.5 = (bf16[80,2048]{1,0:T(8,128)(2,1)S(1)}, bf16[80,2048]{1,0:T(8,128)(2,1)S(1)}, u32[]{:S(2)}, u32[]{:S(2)}) collective-permute-start(bf16[80,2048]{1,0:T(8,128)(2,1)S(1)} %slice.165), channel_id=1, source_target_pairs={{0,1},{1,2},{2,3},{3,0},{4,5},{5,6},{6,7},{7,4},{8,9},{9,10},{10,1... | collective-permute-start | bytes 983048 | tf_op jit(solution)/shard_map/ppermute | solution.py:27
  118.2 21.8 %collective-permute-start.6 = (bf16[80,2048]{1,0:T(8,128)(2,1)S(1)}, bf16[80,2048]{1,0:T(8,128)(2,1)S(1)}, u32[]{:S(2)}, u32[]{:S(2)}) collective-permute-start(bf16[80,2048]{1,0:T(8,128)(2,1)S(1)} %slice.166), channel_id=1, source_target_pairs={{0,3},{1,0},{2,1},{3,2},{4,7},{5,4},{6,5},{7,6},{8,11},{9,8},{10,9... | collective-permute-start | bytes 983048 | tf_op jit(solution)/shard_map/ppermute | solution.py:27
  125.5 14.5 %copy-start.2 = (bf16[160,2048]{1,0:T(8,128)(2,1)S(1)}, bf16[160,2048]{1,0:T(8,128)(2,1)}, u32[]{:S(2)}) copy-start(bf16[160,2048]{1,0:T(8,128)(2,1)} %join.3.refs_0_) | copy-start | bytes 1966084
  136.6 18.0 %collective-permute-start.21 = (bf16[80,2048]{1,0:T(8,128)(2,1)S(1)}, bf16[80,2048]{1,0:T(8,128)(2,1)S(1)}, u32[]{:S(2)}, u32[]{:S(2)}) collective-permute-start(bf16[80,2048]{1,0:T(8,128)(2,1)S(1)} %get-tuple-element.32), channel_id=1, source_target_pairs={{0,3},{1,0},{2,1},{3,2},{4,7},{5,4},{6,5},{7,6},{8,11},{9,8},{10,9... | collective-permute-start | bytes 983048 | tf_op jit(solution)/shard_map/ppermute | solution.py:27
  136.8 18.4 %collective-permute-start.23 = (bf16[80,2048]{1,0:T(8,128)(2,1)S(1)}, bf16[80,2048]{1,0:T(8,128)(2,1)S(1)}, u32[]{:S(2)}, u32[]{:S(2)}) collective-permute-start(bf16[80,2048]{1,0:T(8,128)(2,1)S(1)} %get-tuple-element.34), channel_id=1, source_target_pairs={{0,1},{1,2},{2,3},{3,0},{4,5},{5,6},{6,7},{7,4},{8,9},{9,10},{10,1... | collective-permute-start | bytes 983048 | tf_op jit(solution)/shard_map/ppermute | solution.py:27
  151.2 11.9 %collective-permute-start.7 = (bf16[80,2048]{1,0:T(8,128)(2,1)S(1)}, bf16[80,2048]{1,0:T(8,128)(2,1)S(1)}, u32[]{:S(2)}, u32[]{:S(2)}) collective-permute-start(bf16[80,2048]{1,0:T(8,128)(2,1)S(1)} %get-tuple-element.27), channel_id=1, source_target_pairs={{0,3},{1,0},{2,1},{3,2},{4,7},{5,4},{6,5},{7,6},{8,11},{9,8},{10,9... | collective-permute-start | bytes 983048 | tf_op jit(solution)/shard_map/ppermute | solution.py:27
  151.3 12.0 %collective-permute-start.9 = (bf16[80,2048]{1,0:T(8,128)(2,1)S(1)}, bf16[80,2048]{1,0:T(8,128)(2,1)S(1)}, u32[]{:S(2)}, u32[]{:S(2)}) collective-permute-start(bf16[80,2048]{1,0:T(8,128)(2,1)S(1)} %get-tuple-element.29), channel_id=1, source_target_pairs={{0,1},{1,2},{2,3},{3,0},{4,5},{5,6},{6,7},{7,4},{8,9},{9,10},{10,1... | collective-permute-start | bytes 983048 | tf_op jit(solution)/shard_map/ppermute | solution.py:27
  154.8 18.3 %collective-permute-start.22 = (bf16[160,2048]{1,0:T(8,128)(2,1)S(1)}, bf16[160,2048]{1,0:T(8,128)(2,1)S(1)}, u32[]{:S(2)}, u32[]{:S(2)}) collective-permute-start(bf16[160,2048]{1,0:T(8,128)(2,1)S(1)} %pad_maximum_fusion.2), channel_id=1, source_target_pairs={{0,3},{1,0},{2,1},{3,2},{4,7},{5,4},{6,5},{7,6},{8,11},{9,8},{10,9... | collective-permute-start | bytes 1966088 | tf_op jit(solution)/shard_map/ppermute | solution.py:27
  155.3 17.8 %collective-permute-start.24 = (bf16[160,2048]{1,0:T(8,128)(2,1)S(1)}, bf16[160,2048]{1,0:T(8,128)(2,1)S(1)}, u32[]{:S(2)}, u32[]{:S(2)}) collective-permute-start(bf16[160,2048]{1,0:T(8,128)(2,1)S(1)} %pad_maximum_fusion.3), channel_id=1, source_target_pairs={{0,1},{1,2},{2,3},{3,0},{4,5},{5,6},{6,7},{7,4},{8,9},{9,10},{10,1... | collective-permute-start | bytes 1966088 | tf_op jit(solution)/shard_map/ppermute | solution.py:27
  163.2 17.0 %collective-permute-start.8 = (bf16[160,2048]{1,0:T(8,128)(2,1)S(1)}, bf16[160,2048]{1,0:T(8,128)(2,1)S(1)}, u32[]{:S(2)}, u32[]{:S(2)}) collective-permute-start(bf16[160,2048]{1,0:T(8,128)(2,1)S(1)} %pad_maximum_fusion), channel_id=1, source_target_pairs={{0,3},{1,0},{2,1},{3,2},{4,7},{5,4},{6,5},{7,6},{8,11},{9,8},{10,9... | collective-permute-start | bytes 1966088 | tf_op jit(solution)/shard_map/ppermute | solution.py:27
  163.5 16.8 %collective-permute-start.10 = (bf16[160,2048]{1,0:T(8,128)(2,1)S(1)}, bf16[160,2048]{1,0:T(8,128)(2,1)S(1)}, u32[]{:S(2)}, u32[]{:S(2)}) collective-permute-start(bf16[160,2048]{1,0:T(8,128)(2,1)S(1)} %pad_maximum_fusion.1), channel_id=1, source_target_pairs={{0,1},{1,2},{2,3},{3,0},{4,5},{5,6},{6,7},{7,4},{8,9},{9,10},{10,1... | collective-permute-start | bytes 1966088 | tf_op jit(solution)/shard_map/ppermute | solution.py:27
  173.5 17.2 %collective-permute-start.25 = (bf16[40,2048]{1,0:T(8,128)(2,1)S(1)}, bf16[40,2048]{1,0:T(8,128)(2,1)S(1)}, u32[]{:S(2)}, u32[]{:S(2)}) collective-permute-start(bf16[40,2048]{1,0:T(8,128)(2,1)S(1)} %get-tuple-element.53), channel_id=1, source_target_pairs={{0,56},{4,60},{8,32},{12,36},{16,40},{20,44},{24,48},{28,52},{32,8... | collective-permute-start | bytes 491528 | tf_op jit(solution)/shard_map/ppermute | solution.py:343
  173.6 19.1 %collective-permute-start.26 = (bf16[40,2048]{1,0:T(8,128)(2,1)S(1)}, bf16[40,2048]{1,0:T(8,128)(2,1)S(1)}, u32[]{:S(2)}, u32[]{:S(2)}) collective-permute-start(bf16[40,2048]{1,0:T(8,128)(2,1)S(1)} %get-tuple-element.52), channel_id=1, source_target_pairs={{0,52},{4,56},{8,60},{12,32},{16,36},{20,40},{24,44},{28,48},{32,8... | collective-permute-start | bytes 491528 | tf_op jit(solution)/shard_map/ppermute | solution.py:343
  180.2 18.8 %collective-permute-start.28 = (bf16[40,2048]{1,0:T(8,128)(2,1)S(1)}, bf16[40,2048]{1,0:T(8,128)(2,1)S(1)}, u32[]{:S(2)}, u32[]{:S(2)}) collective-permute-start(bf16[40,2048]{1,0:T(8,128)(2,1)S(1)} %get-tuple-element.51), channel_id=1, source_target_pairs={{0,44},{4,48},{8,52},{12,56},{16,60},{20,32},{24,36},{28,40},{32,7... | collective-permute-start | bytes 491528 | tf_op jit(solution)/shard_map/ppermute | solution.py:343
  181.1 37.9 %collective-permute-start.11 = (f32[64,2432]{1,0:T(8,128)S(1)}, f32[64,2432]{1,0:T(8,128)}, u32[]{:S(2)}, u32[]{:S(2)}) collective-permute-start(f32[64,2432]{1,0:T(8,128)S(1)} %concatenate.17), channel_id=1, source_target_pairs={{0,32},{4,36},{8,40},{12,44},{16,48},{20,52},{24,56},{28,60},{32,6... | collective-permute-start | bytes 1867784 | tf_op jit(solution)/shard_map/ppermute | solution.py:343
  184.7 18.9 %collective-permute-start.29 = (bf16[40,2048]{1,0:T(8,128)(2,1)S(1)}, bf16[40,2048]{1,0:T(8,128)(2,1)S(1)}, u32[]{:S(2)}, u32[]{:S(2)}) collective-permute-start(bf16[40,2048]{1,0:T(8,128)(2,1)S(1)} %get-tuple-element.50), channel_id=1, source_target_pairs={{0,40},{4,44},{8,48},{12,52},{16,56},{20,60},{24,32},{28,36},{32,7... | collective-permute-start | bytes 491528 | tf_op jit(solution)/shard_map/ppermute | solution.py:343
  190.7 25.0 %copy-start.8 = (bf16[40,2048]{1,0:T(8,128)(2,1)}, bf16[40,2048]{1,0:T(8,128)(2,1)S(1)}, u32[]{:S(2)}) copy-start(bf16[40,2048]{1,0:T(8,128)(2,1)S(1)} %collective-permute-done.25.refs_1_) | copy-start | bytes 491524
  190.7 12.9 %collective-permute-start.12 = (bf16[40,2048]{1,0:T(8,128)(2,1)S(1)}, bf16[40,2048]{1,0:T(8,128)(2,1)S(1)}, u32[]{:S(2)}, u32[]{:S(2)}) collective-permute-start(bf16[40,2048]{1,0:T(8,128)(2,1)S(1)} %get-tuple-element.49), channel_id=1, source_target_pairs={{0,60},{4,32},{8,36},{12,40},{16,44},{20,48},{24,52},{28,56},{32,9... | collective-permute-start | bytes 491528 | tf_op jit(solution)/shard_map/ppermute | solution.py:343
  192.6 23.0 %copy-start.9 = (bf16[40,2048]{1,0:T(8,128)(2,1)}, bf16[40,2048]{1,0:T(8,128)(2,1)S(1)}, u32[]{:S(2)}) copy-start(bf16[40,2048]{1,0:T(8,128)(2,1)S(1)} %collective-permute-done.26.refs_2_) | copy-start | bytes 491524
  192.7 16.2 %collective-permute-start.27 = (bf16[40,2048]{1,0:T(8,128)(2,1)S(1)}, bf16[40,2048]{1,0:T(8,128)(2,1)S(1)}, u32[]{:S(2)}, u32[]{:S(2)}) collective-permute-start(bf16[40,2048]{1,0:T(8,128)(2,1)S(1)} %get-tuple-element.48), channel_id=1, source_target_pairs={{0,48},{4,52},{8,56},{12,60},{16,32},{20,36},{24,40},{28,44},{32,8... | collective-permute-start | bytes 491528 | tf_op jit(solution)/shard_map/ppermute | solution.py:343
  199.0 16.7 %copy-start.10 = (bf16[40,2048]{1,0:T(8,128)(2,1)}, bf16[40,2048]{1,0:T(8,128)(2,1)S(1)}, u32[]{:S(2)}) copy-start(bf16[40,2048]{1,0:T(8,128)(2,1)S(1)} %collective-permute-done.28.refs_4_) | copy-start | bytes 491524
  199.0 16.7 %collective-permute-start.30 = (bf16[40,2048]{1,0:T(8,128)(2,1)S(1)}, bf16[40,2048]{1,0:T(8,128)(2,1)S(1)}, u32[]{:S(2)}, u32[]{:S(2)}) collective-permute-start(bf16[40,2048]{1,0:T(8,128)(2,1)S(1)} %get-tuple-element.47), channel_id=1, source_target_pairs={{0,36},{4,40},{8,44},{12,48},{16,52},{20,56},{24,60},{28,32},{32,6... | collective-permute-start | bytes 491528 | tf_op jit(solution)/shard_map/ppermute | solution.py:343
  203.6 12.0 %copy-start.11 = (bf16[40,2048]{1,0:T(8,128)(2,1)}, bf16[40,2048]{1,0:T(8,128)(2,1)S(1)}, u32[]{:S(2)}) copy-start(bf16[40,2048]{1,0:T(8,128)(2,1)S(1)} %collective-permute-done.29.refs_5_) | copy-start | bytes 491524
  203.6 12.0 %copy-start.12 = (bf16[40,2048]{1,0:T(8,128)(2,1)}, bf16[40,2048]{1,0:T(8,128)(2,1)S(1)}, u32[]{:S(2)}) copy-start(bf16[40,2048]{1,0:T(8,128)(2,1)S(1)} %collective-permute-done.12.refs_0_) | copy-start | bytes 491524
  208.9 6.8 %copy-start.13 = (bf16[40,2048]{1,0:T(8,128)(2,1)}, bf16[40,2048]{1,0:T(8,128)(2,1)S(1)}, u32[]{:S(2)}) copy-start(bf16[40,2048]{1,0:T(8,128)(2,1)S(1)} %collective-permute-done.27.refs_3_) | copy-start | bytes 491524
  (12 other events, 26.1 us)
where the time goes:
time: 225 us; the launch traced here: 223 us
  starting transfers between devices  83.1 us (37%)
  waiting for transfers between devices  77.5 us (34%)
  Pallas kernels  42.6 us (19%)
  local copies, waits for them, and re-layouts  10.4 us (5%)
  matrix products  6.86 us (3%)
    ppermute x23, waiting for transfers between devices, passed_along(): lax.ppermute(value, axis, [(i, (i + by) % length) for i in range(length)])  45.2 us
    ppermute x23, starting transfers between devices, passed_along(): lax.ppermute(value, axis, [(i, (i + by) % length) for i in range(length)])  41.3 us
    ppermute x8, starting transfers between devices, onward(): return lax.ppermute(value, ('section', 'wide_0'), pairs)  24.6 us
    pallas_call x2, Pallas kernels, expert_rows(): pl.pallas_call(functools.partial(expert_kernel, sizes, tile, out_tile), o...  22.2 us
    ppermute x8, waiting for transfers between devices, onward(): return lax.ppermute(value, ('section', 'wide_0'), pairs)  16.7 us
    all_to_all x1, starting transfers between devices, carried_states(): lax.all_to_all(payload, WIDE, split_axis=0, concat_axis=0, tiled=True)  11.6 us
    all_to_all x1, waiting for transfers between devices, carried_states(): lax.all_to_all(payload, WIDE, split_axis=0, concat_axis=0, tiled=True)  11.6 us
    unnamed x55, local copies, waits for them, and re-layouts  7.58 us
  transfers between devices with their start and end apart: 33, of which 16 were waited for; matrix products, arithmetic and copies ran while one was open for 2% of the time, Pallas kernels for 15%

commit v1 on v0

--- a/solution.py
+++ b/solution.py
@@ -19,12 +19,15 @@
 NY = 4
 WIDE = ("wide_0", "wide_1")
 EPSILON = 1e-05
-CHUNKS = ((0, 1, 7, 4), (2, 6, 3, 5))
-
-
-def passed_along(value, axis, by):
-    length = lax.axis_size(axis)
-    return lax.ppermute(value, axis, [(i, (i + by) % length) for i in range(length)])
+SHIFTS = (0, 2, 6, 4)
+
+
+def along_y(value, by):
+    return lax.ppermute(value, "wide_1", [(y, (y + by) % NY) for y in range(NY)])
+
+
+def along_z(value, target):
+    return lax.ppermute(value, "wide_0", [(z, target(z) % NZ) for z in range(NZ)])
 
 
 def rms_scale(values, gain_row):
@@ -49,7 +52,7 @@
         decay = block[32:33] + block[33:34] + block[34:35]
         return carry * decay + block[:32]
 
-    lax.fori_loop(0, NZ * NY, step, jnp.zeros((32, 128), jnp.float32))
+    lax.fori_loop(0, NZ * NY, step, jnp.zeros((32, 128), jnp.float32), unroll=8)
 
 
 def prefix_states(arrived):
@@ -59,7 +62,7 @@
         in_specs=[pl.BlockSpec(memory_space=pltpu.VMEM)],
         out_specs=pl.BlockSpec(memory_space=pltpu.VMEM),
         name="prefix_states",
-    )(arrived)
+    )(pltpu.with_memory_space_constraint(arrived, pltpu.VMEM))
 
 
 def carried_states(payload):
@@ -134,7 +137,7 @@
             payload_ref[2 * pair + half] = block.astype(jnp.bfloat16)
         return carry
 
-    lax.fori_loop(0, HEADS // 2, pair_step, 0)
+    lax.fori_loop(0, HEADS // 2, pair_step, 0, unroll=4)
 
 
 def within_kernel(normed_ref, maps_ref, step_ref, cum_ref, skip_ref, out_ref, cum_t, step_t):
@@ -275,8 +278,8 @@
     lax.fori_loop(0, out_tiles, second, 0)
 
 
-def expert_rows(pieces, gate_part, up_part, down_part):
-    features, width = gate_part.shape
+def expert_rows(pieces, *weights):
+    features, width = weights[0].shape
     tile, out_tile = 128, 512
     sizes = tuple(piece.shape[0] for piece in pieces)
     total = sum(sizes)
@@ -295,14 +298,14 @@
             pltpu.SemaphoreType.DMA((width // tile, 2)),
             pltpu.SemaphoreType.DMA((features // out_tile,)),
         ],
-        compiler_params=pltpu.CompilerParams(vmem_limit_bytes=40 * 2**20),
+        compiler_params=pltpu.CompilerParams(vmem_limit_bytes=24 * 2**20),
         cost_estimate=pl.CostEstimate(
             flops=6 * total * features * width,
             transcendentals=total * width,
             bytes_accessed=6 * features * width + 4 * total * features,
         ),
         name="expert_rows",
-    )(*pieces, gate_part, up_part, down_part)
+    )(*pieces, *(pltpu.with_memory_space_constraint(w, pltpu.HBM) for w in weights))
 
 
 def join_kernel(*refs):
@@ -326,30 +329,62 @@
         in_specs=[here] * len(blocks),
         out_specs=here,
         name="join",
-    )(*blocks)
+    )(*(pltpu.with_memory_space_constraint(block, pltpu.VMEM) for block in blocks))
 
 
 def added(one, other):
     return (one.astype(jnp.float32) + other.astype(jnp.float32)).astype(jnp.bfloat16)
 
 
-def onward(value, back):
+def onward(value, target):
     sections = lax.axis_size("section")
     pairs = [
-        (s * NZ + z, (s + 1) % sections * NZ + (z - back) % NZ)
+        (s * NZ + z, (s + 1) % sections * NZ + target(z) % NZ)
         for s in range(sections)
         for z in range(NZ)
     ]
     return lax.ppermute(value, ("section", "wide_0"), pairs)
 
 
-def homeward(number, o_own, to_left, to_right):
-    from_left = passed_along(to_left, "wide_1", -1)
-    from_right = passed_along(to_right, "wide_1", 1)
-    summed = (
-        o_own.astype(jnp.float32) + from_left.astype(jnp.float32) + from_right.astype(jnp.float32)
-    ).astype(jnp.bfloat16)
-    return {k: summed[i * CAP : (i + 1) * CAP] for i, k in enumerate(CHUNKS[number])}
+def finish_kernel(kept_ref, *refs):
+    answers, out_ref, stacked = refs[:-2], refs[-2], refs[-1]
+    for number, answer in enumerate(answers):
+
+        def copy(i, carry, answer=answer, at=number * CAP):
+            stacked[pl.ds(pl.multiple_of(at + i * 8, 8), 8)] = answer[
+                pl.ds(pl.multiple_of(i * 8, 8), 8)
+            ]
+            return carry
+
+        lax.fori_loop(0, CAP // 8, copy, 0, unroll=True)
+    features = out_ref.shape[1]
+    weights = kept_ref[:, features : features + len(SHIFTS) * CAP]
+    parts = [weights[:, :CAP]]
+    for i in range(1, len(SHIFTS)):
+        parts += [weights[:, i * CAP : (i + 1) * CAP]] * 2
+    weights = jnp.concatenate(parts, axis=1)
+    high = weights.astype(jnp.bfloat16)
+    low = (weights - high.astype(jnp.float32)).astype(jnp.bfloat16)
+    for at in range(0, features, 512):
+        rows = stacked[:, at : at + 512]
+        result = kept_ref[:, at : at + 512] + jnp.dot(
+            high, rows, preferred_element_type=jnp.float32
+        )
+        result += jnp.dot(low, rows, preferred_element_type=jnp.float32)
+        out_ref[:, at : at + 512] = result.astype(jnp.bfloat16)
+
+
+def finished(kept, answers):
+    rows, features = kept.shape[0], answers[0].shape[1]
+    here = pl.BlockSpec(memory_space=pltpu.VMEM)
+    return pl.pallas_call(
+        finish_kernel,
+        out_shape=jax.ShapeDtypeStruct((rows, features), jnp.bfloat16),
+        in_specs=[here] * (1 + len(answers)),
+        out_specs=here,
+        scratch_shapes=[pltpu.VMEM((len(answers) * CAP, features), jnp.bfloat16)],
+        name="finish",
+    )(*(pltpu.with_memory_space_constraint(value, pltpu.VMEM) for value in (kept, *answers)))
 
 
 def weighted_rows(weights, rows):
@@ -372,8 +407,9 @@
     first_share = jax.nn.sigmoid(jnp.sum(logits * signs, axis=1))
     shares = jnp.stack([first_share, 1.0 - first_share], axis=1)
 
-    col_expert = ((zi + lax.broadcasted_iota(jnp.int32, (NZ, CAP), 0)) % NZ // 2).reshape(-1)
-    col_slot = lax.broadcasted_iota(jnp.int32, (NZ, CAP), 1).reshape(-1)
+    shifts = [jnp.full((CAP,), shift, jnp.int32) for shift in SHIFTS]
+    col_expert = (zi + jnp.concatenate(shifts)) % NZ // 2
+    col_slot = lax.broadcasted_iota(jnp.int32, (len(SHIFTS), CAP), 1).reshape(-1)
     hits = [
         (id_rows[:, k][:, None] == col_expert[None, :]) & (slots[:, k][:, None] == col_slot[None, :])
         for k in range(TOP)
@@ -382,48 +418,43 @@
     combine = jnp.where(hits[0], shares[:, 0:1], 0.0) + jnp.where(hits[1], shares[:, 1:2], 0.0)
     packed = lax.dot_general(
         placing, routed, (((0,), (0,)), ((), ())), preferred_element_type=jnp.float32
-    ).astype(jnp.bfloat16).reshape(NZ, CAP, features)
-
-    arrived = {}
-    for chunk in CHUNKS:
-        for k in chunk:
-            arrived[k] = packed[0] if k == 0 else passed_along(packed[k], "wide_0", k)
-    answers, kept = {}, []
-
-    def finish(number, *sums):
-        for k, block in homeward(number, *sums).items():
-            if k:
-                answers[k] = onward(block, k)
-                continue
-            own_part = residual + weighted_rows(combine[:, :CAP], block)
-            wide = jnp.concatenate(
-                [own_part, combine[:, CAP:], jnp.zeros((tok_rows, 104), jnp.float32)], axis=1
-            )
-            kept.append(onward(wide, 0))
-
-    ahead = None
-    for number, chunk in enumerate(CHUNKS):
-        own = joined([arrived[k] for k in chunk])
+    ).astype(jnp.bfloat16).reshape(len(SHIFTS), CAP, features)
+
+    blocks = [packed[0]]
+    for shift, block in zip(SHIFTS[1:], packed[1:]):
+        blocks.append(along_z(block, lambda z, by=shift: z + by))
+    even = joined(blocks)
+    odd = along_z(even, lambda z: z ^ 1)
+
+    sums = []
+    for own in (even, odd):
         half = own.shape[0] // 2
-        left = passed_along(own, "wide_1", 1)
-        right = passed_along(own, "wide_1", -1)
-        far_a = passed_along(left[:half], "wide_1", 1)
-        far_b = passed_along(right[half:], "wide_1", -1)
-        if ahead is not None:
-            finish(number - 1, *ahead)
+        left = along_y(own, 1)
+        right = along_y(own, -1)
+        far_a = along_y(left[:half], 1)
+        far_b = along_y(right[half:], -1)
         o_own, o_left, o_right, o_far_a, o_far_b = expert_rows(
             (own, left, right, far_a, far_b), gate_part, up_part, down_part
         )
-        mid_a = passed_along(o_far_a, "wide_1", -1)
-        mid_b = passed_along(o_far_b, "wide_1", 1)
+        mid_a = along_y(o_far_a, -1)
+        mid_b = along_y(o_far_b, 1)
         to_left = jnp.concatenate([added(o_left[:half], mid_a), o_left[half:]], axis=0)
         to_right = jnp.concatenate([o_right[:half], added(o_right[half:], mid_b)], axis=0)
-        ahead = (o_own, to_left, to_right)
-    finish(len(CHUNKS) - 1, *ahead)
-    stacked = joined([answers[k] for k in range(1, NZ)])
-    kept = kept[0]
-    rest = kept[:, features : features + (NZ - 1) * CAP]
-    return (kept[:, :features] + weighted_rows(rest, stacked)).astype(jnp.bfloat16)
+        from_left = along_y(to_left, -1)
+        from_right = along_y(to_right, 1)
+        total = o_own.astype(jnp.float32) + from_left.astype(jnp.float32)
+        sums.append((total + from_right.astype(jnp.float32)).astype(jnp.bfloat16))
+
+    own_part = residual + weighted_rows(combine[:, :CAP], sums[0][:CAP])
+    spare = jnp.zeros((tok_rows, 96), jnp.float32)
+    kept = onward(jnp.concatenate([own_part, combine, spare], axis=1), lambda z: z)
+    answers = []
+    for i, shift in enumerate(SHIFTS):
+        part = slice(i * CAP, (i + 1) * CAP)
+        if i:
+            answers.append(onward(sums[0][part], lambda z, by=shift: z - by))
+        answers.append(onward(sums[1][part], lambda z, by=shift: (z ^ 1) - by))
+    return finished(kept, answers)
 
 
 def local(
@@ -443,7 +474,7 @@
     residual = mixer_block(
         stream[0], mixer_gain[0], ssm_weight[0], decay_rate[0], skip_gain[0], mixed_gain[0]
     )
-    finished = expert_layer(
+    result = expert_layer(
         residual,
         ffn_gain[0],
         router_weight[0],
@@ -452,7 +483,7 @@
         up_weight[0],
         down_weight[0],
     )
-    return finished[None]
+    return result[None]
 
 
 def solution(mesh):

time: 225 us -> 204 us (0.907)
  the two profiles are of different devices: /device:TPU:24 before, /device:TPU:65 now
where the time goes in v1:
time: 204 us
  starting transfers between devices  92.2 us (45%)
  waiting for transfers between devices  67 us (33%)
  Pallas kernels  34 us (17%)
  other arithmetic  4.87 us (2%)
  local copies, waits for them, and re-layouts  2.76 us (1%)
  matrix products  2.65 us (1%)
    ppermute x8, starting transfers between devices, onward(): return lax.ppermute(value, ('section', 'wide_0'), pairs)  48.6 us
    ppermute x16, waiting for transfers between devices, along_y(): lax.ppermute(value, 'wide_1', [(y, (y + by) % NY) for y in range(NY)])  27.5 us
    pallas_call x2, Pallas kernels, expert_rows(): pl.pallas_call(functools.partial(expert_kernel, sizes, tile, out_tile), o...  21.5 us
    ppermute x16, starting transfers between devices, along_y(): lax.ppermute(value, 'wide_1', [(y, (y + by) % NY) for y in range(NY)])  21.4 us
    ppermute x8, waiting for transfers between devices, onward(): return lax.ppermute(value, ('section', 'wide_0'), pairs)  16.1 us
    all_to_all x1, waiting for transfers between devices, carried_states(): lax.all_to_all(payload, WIDE, split_axis=0, concat_axis=0, tiled=True)  11.2 us
    all_to_all x1, starting transfers between devices, carried_states(): lax.all_to_all(payload, WIDE, split_axis=0, concat_axis=0, tiled=True)  10.5 us
    ppermute x4, waiting for transfers between devices, along_z(): lax.ppermute(value, 'wide_0', [(z, target(z) % NZ) for z in range(NZ)])  8.71 us
  transfers between devices with their start and end apart: 30, of which 14 were waited for; matrix products, arithmetic and copies ran while one was open for 4% of the time, Pallas kernels for 13%

profile of v1, /device:TPU:65, one launch (start us, length us, event | category | flops | bytes accessed | tf_op | source)
XLA Modules:
  0.0 203.9 jit_solution(13148625730068184357)
XLA Ops:
  0.0 3.7 %front.1 = (bf16[32,40,128]{2,1,0:T(8,128)(2,1)}, bf16[64,2048]{1,0:T(8,128)(2,1)}, f32[64,128]{1,0:T(8,128)}, f32[64,32]{1,0:T(8,128)}, f32[64,32]{1,0:T(8,128)}) custom-call(bf16[64,2048]{1,0:T(8,128)(2,1)} %bitcast.38, f32[1,2048]{1,0:T(1,128)} %gain_ref.1, bf16[160,2048]{1,0:T(8,128)(2,1)} %bitcast.41, f32[1,32]{1,0:T(1,128)} %rate_ref.1), custom_call_target="tpu_custom_call" | custom-call | tf_op jit(solution)/shard_map/front/pallas_call | solution.py:178
  3.7 10.5 %all-to-all-start = ((bf16[32,40,128]{2,1,0:T(8,128)(2,1)}), bf16[32,40,128]{2,1,0:T(8,128)(2,1)S(1)}, u32[]{:S(2)}, u32[]{:S(2)}) async-start(bf16[32,40,128]{2,1,0:T(8,128)(2,1)} %get-tuple-element.24), calls=%async_computation | async-start | bytes 655360 | tf_op jit(solution)/shard_map/all_to_all | solution.py:69
  15.1 11.2 %all-to-all-done.arrived_ref = bf16[32,40,128]{2,1,0:T(8,128)(2,1)S(1)} async-done(((bf16[32,40,128]{2,1,0:T(8,128)(2,1)}), bf16[32,40,128]{2,1,0:T(8,128)(2,1)S(1)}, u32[]{:S(2)}, u32[]{:S(2)}) %all-to-all-start) | async-done | bytes 327712 | tf_op jit(solution)/shard_map/all_to_all | solution.py:69
  26.2 0.8 prefix_states.1
  27.1 5.5 %all-to-all-start.1 = ((bf16[32,32,128]{2,1,0:T(8,128)(2,1)}), bf16[32,32,128]{2,1,0:T(8,128)(2,1)S(1)}, u32[]{:S(2)}, u32[]{:S(2)}) async-start(bf16[32,32,128]{2,1,0:T(8,128)(2,1)} %prefix_states.1), calls=%async_computation.1 | async-start | bytes 524288 | tf_op jit(solution)/shard_map/all_to_all | solution.py:70
  33.6 5.6 %within.1 = f32[64,2048]{1,0:T(8,128)} custom-call(bf16[64,2048]{1,0:T(8,128)(2,1)} %get-tuple-element.20.normed_ref, f32[64,128]{1,0:T(8,128)} %get-tuple-element.21.maps_ref, f32[64,32]{1,0:T(8,128)} %get-tuple-element.22.step_ref, f32[64,32]{1,0:T(8,128)} %get-tuple-element.23.cum_ref, f32[1,32]{1,0:T(1,128)} %skip_ref.1), custom_call_target="tpu_custom_call" | custom-call | flops 83886080 | bytes 1048576 | tf_op jit(solution)/shard_map/within/pallas_call | solution.py:192
  39.2 3.5 %all-to-all-done.1 = bf16[32,32,128]{2,1,0:T(8,128)(2,1)S(1)} async-done(((bf16[32,32,128]{2,1,0:T(8,128)(2,1)}), bf16[32,32,128]{2,1,0:T(8,128)(2,1)S(1)}, u32[]{:S(2)}, u32[]{:S(2)}) %all-to-all-start.1) | async-done | bytes 262176 | tf_op jit(solution)/shard_map/all_to_all | solution.py:70
  42.8 1.4 multiply_reduce_fusion.1
  44.6 0.5 convolution_convert_fusion
  45.1 0.6 collective-permute-start
  45.7 1.9 collective-permute-start.1
  47.6 2.4 %collective-permute-start.2 = (bf16[40,2048]{1,0:T(8,128)(2,1)S(1)}, bf16[40,2048]{1,0:T(8,128)(2,1)S(1)}, u32[]{:S(2)}, u32[]{:S(2)}) collective-permute-start(bf16[40,2048]{1,0:T(8,128)(2,1)S(1)} %get-tuple-element.46), channel_id=1, source_target_pairs={{0,16},{4,20},{8,24},{12,28},{16,0},{20,4},{24,8},{28,12},{1,17},{... | collective-permute-start | bytes 491528 | tf_op jit(solution)/shard_map/ppermute | solution.py:30
  49.9 1.7 collective-permute-done.refs_1_
  51.6 1.9 collective-permute-done.1.refs_2_
  53.5 5.1 %collective-permute-done.2.refs_3_ = bf16[40,2048]{1,0:T(8,128)(2,1)S(1)} collective-permute-done((bf16[40,2048]{1,0:T(8,128)(2,1)S(1)}, bf16[40,2048]{1,0:T(8,128)(2,1)S(1)}, u32[]{:S(2)}, u32[]{:S(2)}) %collective-permute-start.2) | collective-permute-done | bytes 163872 | tf_op jit(solution)/shard_map/ppermute | solution.py:30
  58.6 1.0 join.1.refs_0_
  59.6 2.7 %collective-permute-start.4 = (bf16[160,2048]{1,0:T(8,128)(2,1)}, bf16[160,2048]{1,0:T(8,128)(2,1)S(1)}, u32[]{:S(2)}, u32[]{:S(2)}) collective-permute-start(bf16[160,2048]{1,0:T(8,128)(2,1)} %join.1.refs_0_), channel_id=1, source_target_pairs={{0,3},{1,0},{2,1},{3,2},{4,7},{5,4},{6,5},{7,6},{8,11},{9,8},{10,9... | collective-permute-start | bytes 1966088 | tf_op jit(solution)/shard_map/ppermute | solution.py:26
  62.3 1.4 collective-permute-start.12
  63.6 9.3 %collective-permute-done.3.refs_1_ = bf16[160,2048]{1,0:T(8,128)(2,1)S(1)} collective-permute-done((bf16[160,2048]{1,0:T(8,128)(2,1)}, bf16[160,2048]{1,0:T(8,128)(2,1)S(1)}, u32[]{:S(2)}, u32[]{:S(2)}) %collective-permute-start.3) | collective-permute-done | bytes 655392 | tf_op jit(solution)/shard_map/ppermute | solution.py:26
  73.1 2.7 %collective-permute-start.6 = (bf16[80,2048]{1,0:T(8,128)(2,1)S(1)}, bf16[80,2048]{1,0:T(8,128)(2,1)S(1)}, u32[]{:S(2)}, u32[]{:S(2)}) collective-permute-start(bf16[80,2048]{1,0:T(8,128)(2,1)S(1)} %slice.124), channel_id=1, source_target_pairs={{0,3},{1,0},{2,1},{3,2},{4,7},{5,4},{6,5},{7,6},{8,11},{9,8},{10,9... | collective-permute-start | bytes 983048 | tf_op jit(solution)/shard_map/ppermute | solution.py:26
  76.2 2.7 %collective-permute-start.14 = (bf16[160,2048]{1,0:T(8,128)(2,1)S(1)}, bf16[160,2048]{1,0:T(8,128)(2,1)S(1)}, u32[]{:S(2)}, u32[]{:S(2)}) collective-permute-start(bf16[160,2048]{1,0:T(8,128)(2,1)S(1)} %collective-permute-done.12.refs_0_), channel_id=1, source_target_pairs={{0,3},{1,0},{2,1},{3,2},{4,7},{5,4},{6,5},{7,6},{8,11},{9,8},{10,9... | collective-permute-start | bytes 1966088 | tf_op jit(solution)/shard_map/ppermute | solution.py:26
  78.9 2.1 %collective-permute-done.5.refs_3_ = bf16[80,2048]{1,0:T(8,128)(2,1)S(1)} collective-permute-done((bf16[80,2048]{1,0:T(8,128)(2,1)S(1)}, bf16[80,2048]{1,0:T(8,128)(2,1)S(1)}, u32[]{:S(2)}, u32[]{:S(2)}) %collective-permute-start.5) | collective-permute-done | bytes 327712 | tf_op jit(solution)/shard_map/ppermute | solution.py:26
  81.0 10.8 %expert_rows.2 = (bf16[160,2048]{1,0:T(8,128)(2,1)S(1)}, bf16[160,2048]{1,0:T(8,128)(2,1)S(1)}, bf16[160,2048]{1,0:T(8,128)(2,1)S(1)}, bf16[80,2048]{1,0:T(8,128)(2,1)S(1)}, bf16[80,2048]{1,0:T(8,128)(2,1)S(1)}) custom-call(bf16[160,2048]{1,0:T(8,128)(2,1)S(1)} %copy-done.1, bf16[160,2048]{1,0:T(8,128)(2,1)S(1)} %collective-permute-done.3.refs_1_, ...), custom_call_target="tpu_custom_call" | custom-call | flops 7046430720 | bytes 16252928 | tf_op jit(solution)/shard_map/expert_rows/pallas_call | solution.py:288
  92.1 2.7 %collective-permute-start.7 = (bf16[80,2048]{1,0:T(8,128)(2,1)S(1)}, bf16[80,2048]{1,0:T(8,128)(2,1)S(1)}, u32[]{:S(2)}, u32[]{:S(2)}) collective-permute-start(bf16[80,2048]{1,0:T(8,128)(2,1)S(1)} %get-tuple-element.27), channel_id=1, source_target_pairs={{0,3},{1,0},{2,1},{3,2},{4,7},{5,4},{6,5},{7,6},{8,11},{9,8},{10,9... | collective-permute-start | bytes 983048 | tf_op jit(solution)/shard_map/ppermute | solution.py:26
  95.0 2.7 %collective-permute-start.16 = (bf16[80,2048]{1,0:T(8,128)(2,1)S(1)}, bf16[80,2048]{1,0:T(8,128)(2,1)S(1)}, u32[]{:S(2)}, u32[]{:S(2)}) collective-permute-start(bf16[80,2048]{1,0:T(8,128)(2,1)S(1)} %slice.127), channel_id=1, source_target_pairs={{0,3},{1,0},{2,1},{3,2},{4,7},{5,4},{6,5},{7,6},{8,11},{9,8},{10,9... | collective-permute-start | bytes 983048 | tf_op jit(solution)/shard_map/ppermute | solution.py:26
  97.7 4.4 %collective-permute-done.9 = bf16[80,2048]{1,0:T(8,128)(2,1)S(1)} collective-permute-done((bf16[80,2048]{1,0:T(8,128)(2,1)S(1)}, bf16[80,2048]{1,0:T(8,128)(2,1)S(1)}, u32[]{:S(2)}, u32[]{:S(2)}) %collective-permute-start.9) | collective-permute-done | bytes 327712 | tf_op jit(solution)/shard_map/ppermute | solution.py:26
  102.3 3.3 %collective-permute-done.15.refs_3_ = bf16[80,2048]{1,0:T(8,128)(2,1)S(1)} collective-permute-done((bf16[80,2048]{1,0:T(8,128)(2,1)S(1)}, bf16[80,2048]{1,0:T(8,128)(2,1)S(1)}, u32[]{:S(2)}, u32[]{:S(2)}) %collective-permute-start.15) | collective-permute-done | bytes 327712 | tf_op jit(solution)/shard_map/ppermute | solution.py:26
  105.6 10.8 %expert_rows.3 = (bf16[160,2048]{1,0:T(8,128)(2,1)S(1)}, bf16[160,2048]{1,0:T(8,128)(2,1)S(1)}, bf16[160,2048]{1,0:T(8,128)(2,1)S(1)}, bf16[80,2048]{1,0:T(8,128)(2,1)S(1)}, bf16[80,2048]{1,0:T(8,128)(2,1)S(1)}) custom-call(bf16[160,2048]{1,0:T(8,128)(2,1)S(1)} %collective-permute-done.12.refs_0_, bf16[160,2048]{1,0:T(8,128)(2,1)S(1)} %collective-permute-done.13.refs_1_, ...), custom_call_target="tpu_custom_call" | custom-call | flops 7046430720 | bytes 16252928 | tf_op jit(solution)/shard_map/expert_rows/pallas_call | solution.py:288
  116.6 2.7 %collective-permute-start.8 = (bf16[160,2048]{1,0:T(8,128)(2,1)S(1)}, bf16[160,2048]{1,0:T(8,128)(2,1)S(1)}, u32[]{:S(2)}, u32[]{:S(2)}) collective-permute-start(bf16[160,2048]{1,0:T(8,128)(2,1)S(1)} %pad_maximum_fusion), channel_id=1, source_target_pairs={{0,3},{1,0},{2,1},{3,2},{4,7},{5,4},{6,5},{7,6},{8,11},{9,8},{10,9... | collective-permute-start | bytes 1966088 | tf_op jit(solution)/shard_map/ppermute | solution.py:26
  119.4 1.5 collective-permute-start.17
  120.9 6.4 %collective-permute-done.19 = bf16[80,2048]{1,0:T(8,128)(2,1)S(1)} collective-permute-done((bf16[80,2048]{1,0:T(8,128)(2,1)S(1)}, bf16[80,2048]{1,0:T(8,128)(2,1)S(1)}, u32[]{:S(2)}, u32[]{:S(2)}) %collective-permute-start.19) | collective-permute-done | bytes 327712 | tf_op jit(solution)/shard_map/ppermute | solution.py:26
  127.4 0.9 pad_maximum_fusion.3
  128.3 2.0 collective-permute-done.17
  130.5 1.0 pad_maximum_fusion.2
  131.4 3.1 %collective-permute-start.18 = (bf16[160,2048]{1,0:T(8,128)(2,1)}, bf16[160,2048]{1,0:T(8,128)(2,1)}, u32[]{:S(2)}, u32[]{:S(2)}) collective-permute-start(bf16[160,2048]{1,0:T(8,128)(2,1)} %pad_maximum_fusion.2), channel_id=1, source_target_pairs={{0,3},{1,0},{2,1},{3,2},{4,7},{5,4},{6,5},{7,6},{8,11},{9,8},{10,9... | collective-permute-start | bytes 1966088 | tf_op jit(solution)/shard_map/ppermute | solution.py:26
  135.3 0.9 concatenate.17
  136.2 24.5 %collective-permute-start.11 = (f32[64,2304]{1,0:T(8,128)}, f32[64,2304]{1,0:T(8,128)S(1)}, u32[]{:S(2)}, u32[]{:S(2)}) collective-permute-start(f32[64,2304]{1,0:T(8,128)} %concatenate.17), channel_id=1, source_target_pairs={{0,32},{4,36},{8,40},{12,44},{16,48},{20,52},{24,56},{28,60},{32,6... | collective-permute-start | bytes 1769480 | tf_op jit(solution)/shard_map/ppermute | solution.py:346
  160.8 3.1 %collective-permute-start.22 = (bf16[40,2048]{1,0:T(8,128)(2,1)S(1)}, bf16[40,2048]{1,0:T(8,128)(2,1)S(1)}, u32[]{:S(2)}, u32[]{:S(2)}) collective-permute-start(bf16[40,2048]{1,0:T(8,128)(2,1)S(1)} %get-tuple-element.45), channel_id=1, source_target_pairs={{0,56},{4,60},{8,32},{12,36},{16,40},{20,44},{24,48},{28,52},{32,8... | collective-permute-start | bytes 491528 | tf_op jit(solution)/shard_map/ppermute | solution.py:346
  163.8 1.8 collective-permute-start.24
  165.6 3.4 %collective-permute-start.26 = (bf16[40,2048]{1,0:T(8,128)(2,1)S(1)}, bf16[40,2048]{1,0:T(8,128)(2,1)S(1)}, u32[]{:S(2)}, u32[]{:S(2)}) collective-permute-start(bf16[40,2048]{1,0:T(8,128)(2,1)S(1)} %get-tuple-element.43), channel_id=1, source_target_pairs={{0,48},{4,52},{8,56},{12,60},{16,32},{20,36},{24,40},{28,44},{32,8... | collective-permute-start | bytes 491528 | tf_op jit(solution)/shard_map/ppermute | solution.py:346
  169.0 1.4 add_convert_fusion
  170.5 2.5 %collective-permute-start.21 = (bf16[40,2048]{1,0:T(8,128)(2,1)S(1)}, bf16[40,2048]{1,0:T(8,128)(2,1)S(1)}, u32[]{:S(2)}, u32[]{:S(2)}) collective-permute-start(bf16[40,2048]{1,0:T(8,128)(2,1)S(1)} %get-tuple-element.42), channel_id=1, source_target_pairs={{0,36},{4,32},{8,44},{12,40},{16,52},{20,48},{24,60},{28,56},{32,6... | collective-permute-start | bytes 491528 | tf_op jit(solution)/shard_map/ppermute | solution.py:346
  173.0 2.5 %collective-permute-start.23 = (bf16[40,2048]{1,0:T(8,128)(2,1)S(1)}, bf16[40,2048]{1,0:T(8,128)(2,1)S(1)}, u32[]{:S(2)}, u32[]{:S(2)}) collective-permute-start(bf16[40,2048]{1,0:T(8,128)(2,1)S(1)} %get-tuple-element.41), channel_id=1, source_target_pairs={{0,60},{4,56},{8,36},{12,32},{16,44},{20,40},{24,52},{28,48},{32,9... | collective-permute-start | bytes 491528 | tf_op jit(solution)/shard_map/ppermute | solution.py:346
  175.5 10.9 %collective-permute-start.25 = (bf16[40,2048]{1,0:T(8,128)(2,1)S(1)}, bf16[40,2048]{1,0:T(8,128)(2,1)S(1)}, u32[]{:S(2)}, u32[]{:S(2)}) collective-permute-start(bf16[40,2048]{1,0:T(8,128)(2,1)S(1)} %get-tuple-element.40), channel_id=1, source_target_pairs={{0,44},{4,40},{8,52},{12,48},{16,60},{20,56},{24,36},{28,32},{32,7... | collective-permute-start | bytes 491528 | tf_op jit(solution)/shard_map/ppermute | solution.py:346
  186.4 9.4 %collective-permute-done.23.refs_2_ = bf16[40,2048]{1,0:T(8,128)(2,1)S(1)} collective-permute-done((bf16[40,2048]{1,0:T(8,128)(2,1)S(1)}, bf16[40,2048]{1,0:T(8,128)(2,1)S(1)}, u32[]{:S(2)}, u32[]{:S(2)}) %collective-permute-start.23) | collective-permute-done | bytes 163872 | tf_op jit(solution)/shard_map/ppermute | solution.py:346
  195.8 1.1 collective-permute-done.25.refs_4_
  196.9 5.6 %collective-permute-done.27.refs_6_ = bf16[40,2048]{1,0:T(8,128)(2,1)S(1)} collective-permute-done((bf16[40,2048]{1,0:T(8,128)(2,1)S(1)}, bf16[40,2048]{1,0:T(8,128)(2,1)S(1)}, u32[]{:S(2)}, u32[]{:S(2)}) %collective-permute-start.27) | collective-permute-done | bytes 163872 | tf_op jit(solution)/shard_map/ppermute | solution.py:346
  202.5 1.4 finish.1
  (85 shorter events, 4.8 us)
Async XLA Ops:
  0.0 75.8 %copy-start = (bf16[1,2048,4]{1,2,0:T(4,128)(2,1)S(1)}, bf16[1,2048,4]{1,2,0:T(4,128)(2,1)}, u32[]{:S(2)}) copy-start(bf16[1,2048,4]{1,2,0:T(4,128)(2,1)} %param.19) | copy-start | bytes 49156
  0.0 14.2 %copy-start.7 = (s32[1,64,2]{1,2,0:T(2,128)S(1)}, s32[1,64,2]{1,2,0:T(2,128)}, u32[]{:S(2)}) copy-start(s32[1,64,2]{1,2,0:T(2,128)} %param.20) | copy-start | bytes 1540
  3.7 29.1 %copy-start.4 = (f32[64,32]{1,0:T(8,128)S(1)}, f32[64,32]{1,0:T(8,128)}, u32[]{:S(2)}) copy-start(f32[64,32]{1,0:T(8,128)} %get-tuple-element.23.cum_ref) | copy-start | bytes 24580
  3.7 22.5 %all-to-all-start = ((bf16[32,40,128]{2,1,0:T(8,128)(2,1)}), bf16[32,40,128]{2,1,0:T(8,128)(2,1)S(1)}, u32[]{:S(2)}, u32[]{:S(2)}) async-start(bf16[32,40,128]{2,1,0:T(8,128)(2,1)} %get-tuple-element.24), calls=%async_computation | async-start | bytes 655360 | tf_op jit(solution)/shard_map/all_to_all | solution.py:69
  27.1 15.6 %all-to-all-start.1 = ((bf16[32,32,128]{2,1,0:T(8,128)(2,1)}), bf16[32,32,128]{2,1,0:T(8,128)(2,1)S(1)}, u32[]{:S(2)}, u32[]{:S(2)}) async-start(bf16[32,32,128]{2,1,0:T(8,128)(2,1)} %prefix_states.1), calls=%async_computation.1 | async-start | bytes 524288 | tf_op jit(solution)/shard_map/all_to_all | solution.py:70
  33.2 5.9 %copy-start.8 = (s32[160]{0:T(256)S(1)}, s32[160]{0:T(256)}, u32[]{:S(2)}) copy-start(s32[160]{0:T(256)} %constant.54.clone.1) | copy-start | bytes 1924
  33.2 9.6 %copy-start.3 = (f32[64,128]{1,0:T(8,128)S(1)}, f32[64,128]{1,0:T(8,128)}, u32[]{:S(2)}) copy-start(f32[64,128]{1,0:T(8,128)} %get-tuple-element.21.maps_ref) | copy-start | bytes 98308
  39.1 5.1 %copy-start.2 = (bf16[1,64,2048]{2,1,0:T(8,128)(2,1)S(1)}, bf16[1,64,2048]{2,1,0:T(8,128)(2,1)}, u32[]{:S(2)}) copy-start(bf16[1,64,2048]{2,1,0:T(8,128)(2,1)} %param.12) | copy-start | bytes 786436
  39.1 5.2 %copy-start.5 = (f32[1,2048]{1,0:T(1,128)S(1)}, f32[1,2048]{1,0:T(1,128)}, u32[]{:S(2)}) copy-start(f32[1,2048]{1,0:T(1,128)} %param.17) | copy-start | bytes 24580
  42.8 1.8 copy-start.6
  45.1 6.5 %collective-permute-start = (bf16[40,2048]{1,0:T(8,128)(2,1)S(1)}, bf16[40,2048]{1,0:T(8,128)(2,1)S(1)}, u32[]{:S(2)}, u32[]{:S(2)}) collective-permute-start(bf16[40,2048]{1,0:T(8,128)(2,1)S(1)} %get-tuple-element.48), channel_id=1, source_target_pairs={{0,8},{4,12},{8,16},{12,20},{16,24},{20,28},{24,0},{28,4},{1,9},{5... | collective-permute-start | bytes 491528 | tf_op jit(solution)/shard_map/ppermute | solution.py:30
  45.7 7.8 %collective-permute-start.1 = (bf16[40,2048]{1,0:T(8,128)(2,1)S(1)}, bf16[40,2048]{1,0:T(8,128)(2,1)S(1)}, u32[]{:S(2)}, u32[]{:S(2)}) collective-permute-start(bf16[40,2048]{1,0:T(8,128)(2,1)S(1)} %get-tuple-element.47), channel_id=1, source_target_pairs={{0,24},{4,28},{8,0},{12,4},{16,8},{20,12},{24,16},{28,20},{1,25},{... | collective-permute-start | bytes 491528 | tf_op jit(solution)/shard_map/ppermute | solution.py:30
  47.6 11.1 %collective-permute-start.2 = (bf16[40,2048]{1,0:T(8,128)(2,1)S(1)}, bf16[40,2048]{1,0:T(8,128)(2,1)S(1)}, u32[]{:S(2)}, u32[]{:S(2)}) collective-permute-start(bf16[40,2048]{1,0:T(8,128)(2,1)S(1)} %get-tuple-element.46), channel_id=1, source_target_pairs={{0,16},{4,20},{8,24},{12,28},{16,0},{20,4},{24,8},{28,12},{1,17},{... | collective-permute-start | bytes 491528 | tf_op jit(solution)/shard_map/ppermute | solution.py:30
  59.6 21.4 %copy-start.1 = (bf16[160,2048]{1,0:T(8,128)(2,1)S(1)}, bf16[160,2048]{1,0:T(8,128)(2,1)}, u32[]{:S(2)}) copy-start(bf16[160,2048]{1,0:T(8,128)(2,1)} %join.1.refs_0_) | copy-start | bytes 1966084
  59.6 13.3 %collective-permute-start.3 = (bf16[160,2048]{1,0:T(8,128)(2,1)}, bf16[160,2048]{1,0:T(8,128)(2,1)S(1)}, u32[]{:S(2)}, u32[]{:S(2)}) collective-permute-start(bf16[160,2048]{1,0:T(8,128)(2,1)} %join.1.refs_0_), channel_id=1, source_target_pairs={{0,1},{1,2},{2,3},{3,0},{4,5},{5,6},{6,7},{7,4},{8,9},{9,10},{10,1... | collective-permute-start | bytes 1966088 | tf_op jit(solution)/shard_map/ppermute | solution.py:26
  59.6 13.4 %collective-permute-start.4 = (bf16[160,2048]{1,0:T(8,128)(2,1)}, bf16[160,2048]{1,0:T(8,128)(2,1)S(1)}, u32[]{:S(2)}, u32[]{:S(2)}) collective-permute-start(bf16[160,2048]{1,0:T(8,128)(2,1)} %join.1.refs_0_), channel_id=1, source_target_pairs={{0,3},{1,0},{2,1},{3,2},{4,7},{5,4},{6,5},{7,6},{8,11},{9,8},{10,9... | collective-permute-start | bytes 1966088 | tf_op jit(solution)/shard_map/ppermute | solution.py:26
  62.3 13.9 %collective-permute-start.12 = (bf16[160,2048]{1,0:T(8,128)(2,1)}, bf16[160,2048]{1,0:T(8,128)(2,1)S(1)}, u32[]{:S(2)}, u32[]{:S(2)}) collective-permute-start(bf16[160,2048]{1,0:T(8,128)(2,1)} %join.1.refs_0_), channel_id=1, source_target_pairs={{0,4},{4,0},{8,12},{12,8},{16,20},{20,16},{24,28},{28,24},{1,5},{5... | collective-permute-start | bytes 1966088 | tf_op jit(solution)/shard_map/ppermute | solution.py:30
  72.9 8.0 %collective-permute-start.5 = (bf16[80,2048]{1,0:T(8,128)(2,1)S(1)}, bf16[80,2048]{1,0:T(8,128)(2,1)S(1)}, u32[]{:S(2)}, u32[]{:S(2)}) collective-permute-start(bf16[80,2048]{1,0:T(8,128)(2,1)S(1)} %slice.123), channel_id=1, source_target_pairs={{0,1},{1,2},{2,3},{3,0},{4,5},{5,6},{6,7},{7,4},{8,9},{9,10},{10,1... | collective-permute-start | bytes 983048 | tf_op jit(solution)/shard_map/ppermute | solution.py:26
  73.1 7.9 %collective-permute-start.6 = (bf16[80,2048]{1,0:T(8,128)(2,1)S(1)}, bf16[80,2048]{1,0:T(8,128)(2,1)S(1)}, u32[]{:S(2)}, u32[]{:S(2)}) collective-permute-start(bf16[80,2048]{1,0:T(8,128)(2,1)S(1)} %slice.124), channel_id=1, source_target_pairs={{0,3},{1,0},{2,1},{3,2},{4,7},{5,4},{6,5},{7,6},{8,11},{9,8},{10,9... | collective-permute-start | bytes 983048 | tf_op jit(solution)/shard_map/ppermute | solution.py:26
  76.1 18.7 %collective-permute-start.13 = (bf16[160,2048]{1,0:T(8,128)(2,1)S(1)}, bf16[160,2048]{1,0:T(8,128)(2,1)S(1)}, u32[]{:S(2)}, u32[]{:S(2)}) collective-permute-start(bf16[160,2048]{1,0:T(8,128)(2,1)S(1)} %collective-permute-done.12.refs_0_), channel_id=1, source_target_pairs={{0,1},{1,2},{2,3},{3,0},{4,5},{5,6},{6,7},{7,4},{8,9},{9,10},{10,1... | collective-permute-start | bytes 1966088 | tf_op jit(solution)/shard_map/ppermute | solution.py:26
  76.2 18.7 %collective-permute-start.14 = (bf16[160,2048]{1,0:T(8,128)(2,1)S(1)}, bf16[160,2048]{1,0:T(8,128)(2,1)S(1)}, u32[]{:S(2)}, u32[]{:S(2)}) collective-permute-start(bf16[160,2048]{1,0:T(8,128)(2,1)S(1)} %collective-permute-done.12.refs_0_), channel_id=1, source_target_pairs={{0,3},{1,0},{2,1},{3,2},{4,7},{5,4},{6,5},{7,6},{8,11},{9,8},{10,9... | collective-permute-start | bytes 1966088 | tf_op jit(solution)/shard_map/ppermute | solution.py:26
  91.8 10.3 %collective-permute-start.9 = (bf16[80,2048]{1,0:T(8,128)(2,1)S(1)}, bf16[80,2048]{1,0:T(8,128)(2,1)S(1)}, u32[]{:S(2)}, u32[]{:S(2)}) collective-permute-start(bf16[80,2048]{1,0:T(8,128)(2,1)S(1)} %get-tuple-element.29), channel_id=1, source_target_pairs={{0,1},{1,2},{2,3},{3,0},{4,5},{5,6},{6,7},{7,4},{8,9},{9,10},{10,1... | collective-permute-start | bytes 983048 | tf_op jit(solution)/shard_map/ppermute | solution.py:26
  92.1 24.4 %collective-permute-start.7 = (bf16[80,2048]{1,0:T(8,128)(2,1)S(1)}, bf16[80,2048]{1,0:T(8,128)(2,1)S(1)}, u32[]{:S(2)}, u32[]{:S(2)}) collective-permute-start(bf16[80,2048]{1,0:T(8,128)(2,1)S(1)} %get-tuple-element.27), channel_id=1, source_target_pairs={{0,3},{1,0},{2,1},{3,2},{4,7},{5,4},{6,5},{7,6},{8,11},{9,8},{10,9... | collective-permute-start | bytes 983048 | tf_op jit(solution)/shard_map/ppermute | solution.py:26
  94.8 10.7 %collective-permute-start.15 = (bf16[80,2048]{1,0:T(8,128)(2,1)S(1)}, bf16[80,2048]{1,0:T(8,128)(2,1)S(1)}, u32[]{:S(2)}, u32[]{:S(2)}) collective-permute-start(bf16[80,2048]{1,0:T(8,128)(2,1)S(1)} %slice.126), channel_id=1, source_target_pairs={{0,1},{1,2},{2,3},{3,0},{4,5},{5,6},{6,7},{7,4},{8,9},{9,10},{10,1... | collective-permute-start | bytes 983048 | tf_op jit(solution)/shard_map/ppermute | solution.py:26
  95.0 10.6 %collective-permute-start.16 = (bf16[80,2048]{1,0:T(8,128)(2,1)S(1)}, bf16[80,2048]{1,0:T(8,128)(2,1)S(1)}, u32[]{:S(2)}, u32[]{:S(2)}) collective-permute-start(bf16[80,2048]{1,0:T(8,128)(2,1)S(1)} %slice.127), channel_id=1, source_target_pairs={{0,3},{1,0},{2,1},{3,2},{4,7},{5,4},{6,5},{7,6},{8,11},{9,8},{10,9... | collective-permute-start | bytes 983048 | tf_op jit(solution)/shard_map/ppermute | solution.py:26
  102.2 32.3 %collective-permute-start.10 = (bf16[160,2048]{1,0:T(8,128)(2,1)S(1)}, bf16[160,2048]{1,0:T(8,128)(2,1)S(1)}, u32[]{:S(2)}, u32[]{:S(2)}) collective-permute-start(bf16[160,2048]{1,0:T(8,128)(2,1)S(1)} %pad_maximum_fusion.1), channel_id=1, source_target_pairs={{0,1},{1,2},{2,3},{3,0},{4,5},{5,6},{6,7},{7,4},{8,9},{9,10},{10,1... | collective-permute-start | bytes 1966088 | tf_op jit(solution)/shard_map/ppermute | solution.py:26
  116.3 11.0 %collective-permute-start.19 = (bf16[80,2048]{1,0:T(8,128)(2,1)S(1)}, bf16[80,2048]{1,0:T(8,128)(2,1)S(1)}, u32[]{:S(2)}, u32[]{:S(2)}) collective-permute-start(bf16[80,2048]{1,0:T(8,128)(2,1)S(1)} %get-tuple-element.34), channel_id=1, source_target_pairs={{0,1},{1,2},{2,3},{3,0},{4,5},{5,6},{6,7},{7,4},{8,9},{9,10},{10,1... | collective-permute-start | bytes 983048 | tf_op jit(solution)/shard_map/ppermute | solution.py:26
  116.6 17.9 %collective-permute-start.8 = (bf16[160,2048]{1,0:T(8,128)(2,1)S(1)}, bf16[160,2048]{1,0:T(8,128)(2,1)S(1)}, u32[]{:S(2)}, u32[]{:S(2)}) collective-permute-start(bf16[160,2048]{1,0:T(8,128)(2,1)S(1)} %pad_maximum_fusion), channel_id=1, source_target_pairs={{0,3},{1,0},{2,1},{3,2},{4,7},{5,4},{6,5},{7,6},{8,11},{9,8},{10,9... | collective-permute-start | bytes 1966088 | tf_op jit(solution)/shard_map/ppermute | solution.py:26
  119.4 11.0 %collective-permute-start.17 = (bf16[80,2048]{1,0:T(8,128)(2,1)S(1)}, bf16[80,2048]{1,0:T(8,128)(2,1)S(1)}, u32[]{:S(2)}, u32[]{:S(2)}) collective-permute-start(bf16[80,2048]{1,0:T(8,128)(2,1)S(1)} %get-tuple-element.32), channel_id=1, source_target_pairs={{0,3},{1,0},{2,1},{3,2},{4,7},{5,4},{6,5},{7,6},{8,11},{9,8},{10,9... | collective-permute-start | bytes 983048 | tf_op jit(solution)/shard_map/ppermute | solution.py:26
  128.3 37.3 %collective-permute-start.20 = (bf16[160,2048]{1,0:T(8,128)(2,1)}, bf16[160,2048]{1,0:T(8,128)(2,1)S(1)}, u32[]{:S(2)}, u32[]{:S(2)}) collective-permute-start(bf16[160,2048]{1,0:T(8,128)(2,1)} %pad_maximum_fusion.3), channel_id=1, source_target_pairs={{0,1},{1,2},{2,3},{3,0},{4,5},{5,6},{6,7},{7,4},{8,9},{9,10},{10,1... | collective-permute-start | bytes 1966088 | tf_op jit(solution)/shard_map/ppermute | solution.py:26
  131.4 37.6 %collective-permute-start.18 = (bf16[160,2048]{1,0:T(8,128)(2,1)}, bf16[160,2048]{1,0:T(8,128)(2,1)}, u32[]{:S(2)}, u32[]{:S(2)}) collective-permute-start(bf16[160,2048]{1,0:T(8,128)(2,1)} %pad_maximum_fusion.2), channel_id=1, source_target_pairs={{0,3},{1,0},{2,1},{3,2},{4,7},{5,4},{6,5},{7,6},{8,11},{9,8},{10,9... | collective-permute-start | bytes 1966088 | tf_op jit(solution)/shard_map/ppermute | solution.py:26
  136.2 50.2 %collective-permute-start.11 = (f32[64,2304]{1,0:T(8,128)}, f32[64,2304]{1,0:T(8,128)S(1)}, u32[]{:S(2)}, u32[]{:S(2)}) collective-permute-start(f32[64,2304]{1,0:T(8,128)} %concatenate.17), channel_id=1, source_target_pairs={{0,32},{4,36},{8,40},{12,44},{16,48},{20,52},{24,56},{28,60},{32,6... | collective-permute-start | bytes 1769480 | tf_op jit(solution)/shard_map/ppermute | solution.py:346
  160.8 12.2 %collective-permute-start.22 = (bf16[40,2048]{1,0:T(8,128)(2,1)S(1)}, bf16[40,2048]{1,0:T(8,128)(2,1)S(1)}, u32[]{:S(2)}, u32[]{:S(2)}) collective-permute-start(bf16[40,2048]{1,0:T(8,128)(2,1)S(1)} %get-tuple-element.45), channel_id=1, source_target_pairs={{0,56},{4,60},{8,32},{12,36},{16,40},{20,44},{24,48},{28,52},{32,8... | collective-permute-start | bytes 491528 | tf_op jit(solution)/shard_map/ppermute | solution.py:346
  163.8 11.6 %collective-permute-start.24 = (bf16[40,2048]{1,0:T(8,128)(2,1)S(1)}, bf16[40,2048]{1,0:T(8,128)(2,1)S(1)}, u32[]{:S(2)}, u32[]{:S(2)}) collective-permute-start(bf16[40,2048]{1,0:T(8,128)(2,1)S(1)} %get-tuple-element.44), channel_id=1, source_target_pairs={{0,40},{4,44},{8,48},{12,52},{16,56},{20,60},{24,32},{28,36},{32,7... | collective-permute-start | bytes 491528 | tf_op jit(solution)/shard_map/ppermute | solution.py:346
  165.6 20.8 %collective-permute-start.26 = (bf16[40,2048]{1,0:T(8,128)(2,1)S(1)}, bf16[40,2048]{1,0:T(8,128)(2,1)S(1)}, u32[]{:S(2)}, u32[]{:S(2)}) collective-permute-start(bf16[40,2048]{1,0:T(8,128)(2,1)S(1)} %get-tuple-element.43), channel_id=1, source_target_pairs={{0,48},{4,52},{8,56},{12,60},{16,32},{20,36},{24,40},{28,44},{32,8... | collective-permute-start | bytes 491528 | tf_op jit(solution)/shard_map/ppermute | solution.py:346
  170.5 15.9 %collective-permute-start.21 = (bf16[40,2048]{1,0:T(8,128)(2,1)S(1)}, bf16[40,2048]{1,0:T(8,128)(2,1)S(1)}, u32[]{:S(2)}, u32[]{:S(2)}) collective-permute-start(bf16[40,2048]{1,0:T(8,128)(2,1)S(1)} %get-tuple-element.42), channel_id=1, source_target_pairs={{0,36},{4,32},{8,44},{12,40},{16,52},{20,48},{24,60},{28,56},{32,6... | collective-permute-start | bytes 491528 | tf_op jit(solution)/shard_map/ppermute | solution.py:346
  173.0 22.8 %collective-permute-start.23 = (bf16[40,2048]{1,0:T(8,128)(2,1)S(1)}, bf16[40,2048]{1,0:T(8,128)(2,1)S(1)}, u32[]{:S(2)}, u32[]{:S(2)}) collective-permute-start(bf16[40,2048]{1,0:T(8,128)(2,1)S(1)} %get-tuple-element.41), channel_id=1, source_target_pairs={{0,60},{4,56},{8,36},{12,32},{16,44},{20,40},{24,52},{28,48},{32,9... | collective-permute-start | bytes 491528 | tf_op jit(solution)/shard_map/ppermute | solution.py:346
  175.5 21.4 %collective-permute-start.25 = (bf16[40,2048]{1,0:T(8,128)(2,1)S(1)}, bf16[40,2048]{1,0:T(8,128)(2,1)S(1)}, u32[]{:S(2)}, u32[]{:S(2)}) collective-permute-start(bf16[40,2048]{1,0:T(8,128)(2,1)S(1)} %get-tuple-element.40), channel_id=1, source_target_pairs={{0,44},{4,40},{8,52},{12,48},{16,60},{20,56},{24,36},{28,32},{32,7... | collective-permute-start | bytes 491528 | tf_op jit(solution)/shard_map/ppermute | solution.py:346
  186.4 16.1 %collective-permute-start.27 = (bf16[40,2048]{1,0:T(8,128)(2,1)S(1)}, bf16[40,2048]{1,0:T(8,128)(2,1)S(1)}, u32[]{:S(2)}, u32[]{:S(2)}) collective-permute-start(bf16[40,2048]{1,0:T(8,128)(2,1)S(1)} %get-tuple-element.39), channel_id=1, source_target_pairs={{0,52},{4,48},{8,60},{12,56},{16,36},{20,32},{24,44},{28,40},{32,8... | collective-permute-start | bytes 491528 | tf_op jit(solution)/shard_map/ppermute | solution.py:346

commit v2 on v1

--- a/solution.py
+++ b/solution.py
@@ -61,6 +61,7 @@
         out_shape=jax.ShapeDtypeStruct((NZ * NY, 32, 128), jnp.bfloat16),
         in_specs=[pl.BlockSpec(memory_space=pltpu.VMEM)],
         out_specs=pl.BlockSpec(memory_space=pltpu.VMEM),
+        compiler_params=pltpu.CompilerParams(vmem_limit_bytes=4 * 2**20),
         name="prefix_states",
     )(pltpu.with_memory_space_constraint(arrived, pltpu.VMEM))
 
@@ -203,6 +204,7 @@
             transcendentals=seq_len * seq_len * HEADS,
             bytes_accessed=8 * seq_len * features,
         ),
+        compiler_params=pltpu.CompilerParams(vmem_limit_bytes=10 * 2**20),
         name="within",
     )(normed, maps, step_size, cumulative, skip_gain[None])
     c_rows = maps[:, STATE:] / math.sqrt(STATE)
@@ -236,11 +238,10 @@
             sem_down.at[j],
         )
 
-    for i in range(tiles):
+    ahead = 3
+    for i in range(ahead):
         for copy in copies(i):
             copy.start()
-    for j in range(out_tiles):
-        down_copy(j).start()
     at = 0
     for piece, size in zip(pieces, sizes):
 
@@ -256,6 +257,16 @@
     def first(i, carry):
         for copy in copies(i):
             copy.wait()
+
+        @pl.when(i + ahead < tiles)
+        def _():
+            for copy in copies(i + ahead):
+                copy.start()
+
+        @pl.when(i + out_tiles >= tiles)
+        def _():
+            down_copy(i + out_tiles - tiles).start()
+
         both = jnp.dot(rows[...], gate_up[i], preferred_element_type=jnp.float32)
         gate_pre, up_pre = both[:, :tile], both[:, tile:]
         hidden[:, pl.ds(pl.multiple_of(i * tile, tile), tile)] = (
@@ -328,12 +339,37 @@
         out_shape=jax.ShapeDtypeStruct((rows * len(blocks), features), blocks[0].dtype),
         in_specs=[here] * len(blocks),
         out_specs=here,
+        compiler_params=pltpu.CompilerParams(vmem_limit_bytes=6 * 2**20),
         name="join",
     )(*(pltpu.with_memory_space_constraint(block, pltpu.VMEM) for block in blocks))
 
 
-def added(one, other):
-    return (one.astype(jnp.float32) + other.astype(jnp.float32)).astype(jnp.bfloat16)
+def merge_kernel(at, whole_ref, part_ref, out_ref):
+    rows = part_ref.shape[0]
+    for start in range(0, whole_ref.shape[0], rows):
+
+        def copy(i, carry, start=start):
+            here = pl.ds(pl.multiple_of(start + i * 16, 16), 16)
+            value = whole_ref[here]
+            if start == at:
+                part = part_ref[pl.ds(pl.multiple_of(i * 16, 16), 16)].astype(jnp.float32)
+                value = (value.astype(jnp.float32) + part).astype(jnp.bfloat16)
+            out_ref[here] = value
+            return carry
+
+        lax.fori_loop(0, rows // 16, copy, 0)
+
+
+def merged(whole, part, at):
+    here = pl.BlockSpec(memory_space=pltpu.VMEM)
+    return pl.pallas_call(
+        functools.partial(merge_kernel, at),
+        out_shape=jax.ShapeDtypeStruct(whole.shape, whole.dtype),
+        in_specs=[here] * 2,
+        out_specs=here,
+        compiler_params=pltpu.CompilerParams(vmem_limit_bytes=6 * 2**20),
+        name="merge",
+    )(whole, part)
 
 
 def onward(value, target):
@@ -383,6 +419,7 @@
         in_specs=[here] * (1 + len(answers)),
         out_specs=here,
         scratch_shapes=[pltpu.VMEM((len(answers) * CAP, features), jnp.bfloat16)],
+        compiler_params=pltpu.CompilerParams(vmem_limit_bytes=10 * 2**20),
         name="finish",
     )(*(pltpu.with_memory_space_constraint(value, pltpu.VMEM) for value in (kept, *answers)))
 
@@ -438,8 +475,8 @@
         )
         mid_a = along_y(o_far_a, -1)
         mid_b = along_y(o_far_b, 1)
-        to_left = jnp.concatenate([added(o_left[:half], mid_a), o_left[half:]], axis=0)
-        to_right = jnp.concatenate([o_right[:half], added(o_right[half:], mid_b)], axis=0)
+        to_left = merged(o_left, mid_a, 0)
+        to_right = merged(o_right, mid_b, half)
         from_left = along_y(to_left, -1)
         from_right = along_y(to_right, 1)
         total = o_own.astype(jnp.float32) + from_left.astype(jnp.float32)

time: 204 us -> 192 us (0.941)
  the two profiles are of different devices: /device:TPU:65 before, /device:TPU:64 now
where the time goes in v2:
time: 192 us; the launch traced here: 191 us
  waiting for transfers between devices  82.3 us (43%)
  starting transfers between devices  69.5 us (36%)
  Pallas kernels  31.9 us (17%)
  local copies, waits for them, and re-layouts  2.91 us (2%)
  other arithmetic  2.79 us (1%)
    ppermute x16, waiting for transfers between devices, along_y(): lax.ppermute(value, 'wide_1', [(y, (y + by) % NY) for y in range(NY)])  31 us
    ppermute x16, starting transfers between devices, along_y(): lax.ppermute(value, 'wide_1', [(y, (y + by) % NY) for y in range(NY)])  26.9 us
    ppermute x8, waiting for transfers between devices, onward(): return lax.ppermute(value, ('section', 'wide_0'), pairs)  23.9 us
    pallas_call x2, Pallas kernels, expert_rows(): pl.pallas_call(functools.partial(expert_kernel, sizes, tile, out_tile), o...  21.6 us
    ppermute x8, starting transfers between devices, onward(): return lax.ppermute(value, ('section', 'wide_0'), pairs)  19.2 us
    all_to_all x1, waiting for transfers between devices, carried_states(): lax.all_to_all(payload, WIDE, split_axis=0, concat_axis=0, tiled=True)  11.9 us
    all_to_all x1, starting transfers between devices, carried_states(): lax.all_to_all(payload, WIDE, split_axis=0, concat_axis=0, tiled=True)  11 us
    ppermute x4, waiting for transfers between devices, along_z(): lax.ppermute(value, 'wide_0', [(z, target(z) % NZ) for z in range(NZ)])  9.87 us
  transfers between devices with their start and end apart: 30, of which 14 were waited for; matrix products, arithmetic and copies ran while one was open for 3% of the time, Pallas kernels for 13%

profile of v2, /device:TPU:64, one launch (start us, length us, event | category | flops | bytes accessed | tf_op | source)
XLA Modules:
  0.0 191.3 jit_solution(9476005602316726935)
XLA Ops:
  0.0 3.7 %front.1 = (bf16[32,40,128]{2,1,0:T(8,128)(2,1)}, bf16[64,2048]{1,0:T(8,128)(2,1)}, f32[64,128]{1,0:T(8,128)}, f32[64,32]{1,0:T(8,128)}, f32[64,32]{1,0:T(8,128)}) custom-call(bf16[64,2048]{1,0:T(8,128)(2,1)} %bitcast.38, f32[1,2048]{1,0:T(1,128)} %gain_ref.1, bf16[160,2048]{1,0:T(8,128)(2,1)} %bitcast.41, f32[1,32]{1,0:T(1,128)} %rate_ref.1), custom_call_target="tpu_custom_call" | custom-call | tf_op jit(solution)/shard_map/front/pallas_call | solution.py:179
  3.7 11.0 %all-to-all-start = ((bf16[32,40,128]{2,1,0:T(8,128)(2,1)}), bf16[32,40,128]{2,1,0:T(8,128)(2,1)S(1)}, u32[]{:S(2)}, u32[]{:S(2)}) async-start(bf16[32,40,128]{2,1,0:T(8,128)(2,1)} %get-tuple-element.24), calls=%async_computation | async-start | bytes 655360 | tf_op jit(solution)/shard_map/all_to_all | solution.py:70
  15.6 11.9 %all-to-all-done.arrived_ref = bf16[32,40,128]{2,1,0:T(8,128)(2,1)S(1)} async-done(((bf16[32,40,128]{2,1,0:T(8,128)(2,1)}), bf16[32,40,128]{2,1,0:T(8,128)(2,1)S(1)}, u32[]{:S(2)}, u32[]{:S(2)}) %all-to-all-start) | async-done | bytes 327712 | tf_op jit(solution)/shard_map/all_to_all | solution.py:70
  27.5 0.8 prefix_states.1
  28.3 5.4 %all-to-all-start.1 = ((bf16[32,32,128]{2,1,0:T(8,128)(2,1)}), bf16[32,32,128]{2,1,0:T(8,128)(2,1)S(1)}, u32[]{:S(2)}, u32[]{:S(2)}) async-start(bf16[32,32,128]{2,1,0:T(8,128)(2,1)} %prefix_states.1), calls=%async_computation.1 | async-start | bytes 524288 | tf_op jit(solution)/shard_map/all_to_all | solution.py:71
  34.1 0.3 broadcast_in_dim.31
  34.4 0.4 reshape.78
  35.0 3.7 %within.1 = f32[64,2048]{1,0:T(8,128)S(1)} custom-call(bf16[64,2048]{1,0:T(8,128)(2,1)S(1)} %copy-done.1, f32[64,128]{1,0:T(8,128)S(1)} %copy-done.2, f32[64,32]{1,0:T(8,128)S(1)} %copy-done.4, f32[64,32]{1,0:T(8,128)S(1)} %copy-done.3, f32[1,32]{1,0:T(1,128)S(1)} %copy-done.5), custom_call_target="tpu_custom_call" | custom-call | flops 83886080 | bytes 1048576 | tf_op jit(solution)/shard_map/within/pallas_call | solution.py:193
  38.8 5.7 %all-to-all-done.1 = bf16[32,32,128]{2,1,0:T(8,128)(2,1)S(1)} async-done(((bf16[32,32,128]{2,1,0:T(8,128)(2,1)}), bf16[32,32,128]{2,1,0:T(8,128)(2,1)S(1)}, u32[]{:S(2)}, u32[]{:S(2)}) %all-to-all-start.1) | async-done | bytes 262176 | tf_op jit(solution)/shard_map/all_to_all | solution.py:71
  44.7 0.4 multiply_reduce_fusion.1
  45.4 0.5 convolution_convert_fusion
  45.9 0.7 collective-permute-start
  46.6 2.3 %collective-permute-start.1 = (bf16[40,2048]{1,0:T(8,128)(2,1)S(1)}, bf16[40,2048]{1,0:T(8,128)(2,1)S(1)}, u32[]{:S(2)}, u32[]{:S(2)}) collective-permute-start(bf16[40,2048]{1,0:T(8,128)(2,1)S(1)} %get-tuple-element.47), channel_id=1, source_target_pairs={{0,24},{4,28},{8,0},{12,4},{16,8},{20,12},{24,16},{28,20},{1,25},{... | collective-permute-start | bytes 491528 | tf_op jit(solution)/shard_map/ppermute | solution.py:30
  48.9 2.5 %collective-permute-start.2 = (bf16[40,2048]{1,0:T(8,128)(2,1)S(1)}, bf16[40,2048]{1,0:T(8,128)(2,1)S(1)}, u32[]{:S(2)}, u32[]{:S(2)}) collective-permute-start(bf16[40,2048]{1,0:T(8,128)(2,1)S(1)} %get-tuple-element.46), channel_id=1, source_target_pairs={{0,16},{4,20},{8,24},{12,28},{16,0},{20,4},{24,8},{28,12},{1,17},{... | collective-permute-start | bytes 491528 | tf_op jit(solution)/shard_map/ppermute | solution.py:30
  51.4 4.7 %collective-permute-done.refs_1_ = bf16[40,2048]{1,0:T(8,128)(2,1)S(1)} collective-permute-done((bf16[40,2048]{1,0:T(8,128)(2,1)S(1)}, bf16[40,2048]{1,0:T(8,128)(2,1)S(1)}, u32[]{:S(2)}, u32[]{:S(2)}) %collective-permute-start) | collective-permute-done | bytes 163872 | tf_op jit(solution)/shard_map/ppermute | solution.py:30
  56.1 0.6 collective-permute-done.1.refs_2_
  56.7 4.6 %collective-permute-done.2.refs_3_ = bf16[40,2048]{1,0:T(8,128)(2,1)S(1)} collective-permute-done((bf16[40,2048]{1,0:T(8,128)(2,1)S(1)}, bf16[40,2048]{1,0:T(8,128)(2,1)S(1)}, u32[]{:S(2)}, u32[]{:S(2)}) %collective-permute-start.2) | collective-permute-done | bytes 163872 | tf_op jit(solution)/shard_map/ppermute | solution.py:30
  61.4 0.3 collective-permute-start.3
  61.7 3.0 %collective-permute-start.4 = (bf16[160,2048]{1,0:T(8,128)(2,1)S(1)}, bf16[160,2048]{1,0:T(8,128)(2,1)S(1)}, u32[]{:S(2)}, u32[]{:S(2)}) collective-permute-start(bf16[160,2048]{1,0:T(8,128)(2,1)S(1)} %join.1.refs_0_), channel_id=1, source_target_pairs={{0,3},{1,0},{2,1},{3,2},{4,7},{5,4},{6,5},{7,6},{8,11},{9,8},{10,9... | collective-permute-start | bytes 1966088 | tf_op jit(solution)/shard_map/ppermute | solution.py:26
  64.7 1.4 collective-permute-start.12
  66.2 10.1 %collective-permute-done.3.refs_1_ = bf16[160,2048]{1,0:T(8,128)(2,1)S(1)} collective-permute-done((bf16[160,2048]{1,0:T(8,128)(2,1)S(1)}, bf16[160,2048]{1,0:T(8,128)(2,1)S(1)}, u32[]{:S(2)}, u32[]{:S(2)}) %collective-permute-start.3) | collective-permute-done | bytes 655392 | tf_op jit(solution)/shard_map/ppermute | solution.py:26
  76.4 3.3 %collective-permute-start.6 = (bf16[80,2048]{1,0:T(8,128)(2,1)S(1)}, bf16[80,2048]{1,0:T(8,128)(2,1)S(1)}, u32[]{:S(2)}, u32[]{:S(2)}) collective-permute-start(bf16[80,2048]{1,0:T(8,128)(2,1)S(1)} %slice.92), channel_id=1, source_target_pairs={{0,3},{1,0},{2,1},{3,2},{4,7},{5,4},{6,5},{7,6},{8,11},{9,8},{10,9... | collective-permute-start | bytes 983048 | tf_op jit(solution)/shard_map/ppermute | solution.py:26
  79.7 3.2 %collective-permute-start.14 = (bf16[160,2048]{1,0:T(8,128)(2,1)S(1)}, bf16[160,2048]{1,0:T(8,128)(2,1)S(1)}, u32[]{:S(2)}, u32[]{:S(2)}) collective-permute-start(bf16[160,2048]{1,0:T(8,128)(2,1)S(1)} %collective-permute-done.12.refs_0_), channel_id=1, source_target_pairs={{0,3},{1,0},{2,1},{3,2},{4,7},{5,4},{6,5},{7,6},{8,11},{9,8},{10,9... | collective-permute-start | bytes 1966088 | tf_op jit(solution)/shard_map/ppermute | solution.py:26
  83.0 5.2 %collective-permute-done.5.refs_3_ = bf16[80,2048]{1,0:T(8,128)(2,1)S(1)} collective-permute-done((bf16[80,2048]{1,0:T(8,128)(2,1)S(1)}, bf16[80,2048]{1,0:T(8,128)(2,1)S(1)}, u32[]{:S(2)}, u32[]{:S(2)}) %collective-permute-start.5) | collective-permute-done | bytes 327712 | tf_op jit(solution)/shard_map/ppermute | solution.py:26
  88.2 10.8 %expert_rows.2 = (bf16[160,2048]{1,0:T(8,128)(2,1)S(1)}, bf16[160,2048]{1,0:T(8,128)(2,1)S(1)}, bf16[160,2048]{1,0:T(8,128)(2,1)S(1)}, bf16[80,2048]{1,0:T(8,128)(2,1)S(1)}, bf16[80,2048]{1,0:T(8,128)(2,1)S(1)}) custom-call(bf16[160,2048]{1,0:T(8,128)(2,1)S(1)} %join.1.refs_0_, bf16[160,2048]{1,0:T(8,128)(2,1)S(1)} %collective-permute-done.3.refs_1_, ...), custom_call_target="tpu_custom_call" | custom-call | flops 7046430720 | bytes 16252928 | tf_op jit(solution)/shard_map/expert_rows/pallas_call | solution.py:299
  99.1 3.4 %collective-permute-start.7 = (bf16[80,2048]{1,0:T(8,128)(2,1)S(1)}, bf16[80,2048]{1,0:T(8,128)(2,1)S(1)}, u32[]{:S(2)}, u32[]{:S(2)}) collective-permute-start(bf16[80,2048]{1,0:T(8,128)(2,1)S(1)} %get-tuple-element.27), channel_id=1, source_target_pairs={{0,3},{1,0},{2,1},{3,2},{4,7},{5,4},{6,5},{7,6},{8,11},{9,8},{10,9... | collective-permute-start | bytes 983048 | tf_op jit(solution)/shard_map/ppermute | solution.py:26
  102.6 3.3 %collective-permute-start.16 = (bf16[80,2048]{1,0:T(8,128)(2,1)S(1)}, bf16[80,2048]{1,0:T(8,128)(2,1)S(1)}, u32[]{:S(2)}, u32[]{:S(2)}) collective-permute-start(bf16[80,2048]{1,0:T(8,128)(2,1)S(1)} %slice.95), channel_id=1, source_target_pairs={{0,3},{1,0},{2,1},{3,2},{4,7},{5,4},{6,5},{7,6},{8,11},{9,8},{10,9... | collective-permute-start | bytes 983048 | tf_op jit(solution)/shard_map/ppermute | solution.py:26
  105.9 0.3 fusion.2
  106.2 4.7 %collective-permute-done.9.part_ref = bf16[80,2048]{1,0:T(8,128)(2,1)S(1)} collective-permute-done((bf16[80,2048]{1,0:T(8,128)(2,1)S(1)}, bf16[80,2048]{1,0:T(8,128)(2,1)S(1)}, u32[]{:S(2)}, u32[]{:S(2)}) %collective-permute-start.9) | collective-permute-done | bytes 327712 | tf_op jit(solution)/shard_map/ppermute | solution.py:26
  111.3 3.3 %collective-permute-start.8 = (bf16[160,2048]{1,0:T(8,128)(2,1)S(1)}, bf16[160,2048]{1,0:T(8,128)(2,1)S(1)}, u32[]{:S(2)}, u32[]{:S(2)}) collective-permute-start(bf16[160,2048]{1,0:T(8,128)(2,1)S(1)} %merge.4), channel_id=1, source_target_pairs={{0,3},{1,0},{2,1},{3,2},{4,7},{5,4},{6,5},{7,6},{8,11},{9,8},{10,9... | collective-permute-start | bytes 1966088 | tf_op jit(solution)/shard_map/ppermute | solution.py:26
  114.6 3.3 %collective-permute-done.15.refs_3_ = bf16[80,2048]{1,0:T(8,128)(2,1)S(1)} collective-permute-done((bf16[80,2048]{1,0:T(8,128)(2,1)S(1)}, bf16[80,2048]{1,0:T(8,128)(2,1)S(1)}, u32[]{:S(2)}, u32[]{:S(2)}) %collective-permute-start.15) | collective-permute-done | bytes 327712 | tf_op jit(solution)/shard_map/ppermute | solution.py:26
  117.9 10.8 %expert_rows.3 = (bf16[160,2048]{1,0:T(8,128)(2,1)S(1)}, bf16[160,2048]{1,0:T(8,128)(2,1)S(1)}, bf16[160,2048]{1,0:T(8,128)(2,1)S(1)}, bf16[80,2048]{1,0:T(8,128)(2,1)S(1)}, bf16[80,2048]{1,0:T(8,128)(2,1)S(1)}) custom-call(bf16[160,2048]{1,0:T(8,128)(2,1)S(1)} %collective-permute-done.12.refs_0_, bf16[160,2048]{1,0:T(8,128)(2,1)S(1)} %collective-permute-done.13.refs_1_, ...), custom_call_target="tpu_custom_call" | custom-call | flops 7046430720 | bytes 16252928 | tf_op jit(solution)/shard_map/expert_rows/pallas_call | solution.py:299
  128.8 3.3 %collective-permute-start.17 = (bf16[80,2048]{1,0:T(8,128)(2,1)S(1)}, bf16[80,2048]{1,0:T(8,128)(2,1)S(1)}, u32[]{:S(2)}, u32[]{:S(2)}) collective-permute-start(bf16[80,2048]{1,0:T(8,128)(2,1)S(1)} %get-tuple-element.32), channel_id=1, source_target_pairs={{0,3},{1,0},{2,1},{3,2},{4,7},{5,4},{6,5},{7,6},{8,11},{9,8},{10,9... | collective-permute-start | bytes 983048 | tf_op jit(solution)/shard_map/ppermute | solution.py:26
  132.2 7.5 %collective-permute-done.19.part_ref = bf16[80,2048]{1,0:T(8,128)(2,1)S(1)} collective-permute-done((bf16[80,2048]{1,0:T(8,128)(2,1)S(1)}, bf16[80,2048]{1,0:T(8,128)(2,1)S(1)}, u32[]{:S(2)}, u32[]{:S(2)}) %collective-permute-start.19) | collective-permute-done | bytes 327712 | tf_op jit(solution)/shard_map/ppermute | solution.py:26
  140.1 3.3 %collective-permute-start.18 = (bf16[160,2048]{1,0:T(8,128)(2,1)S(1)}, bf16[160,2048]{1,0:T(8,128)(2,1)}, u32[]{:S(2)}, u32[]{:S(2)}) collective-permute-start(bf16[160,2048]{1,0:T(8,128)(2,1)S(1)} %merge.6), channel_id=1, source_target_pairs={{0,3},{1,0},{2,1},{3,2},{4,7},{5,4},{6,5},{7,6},{8,11},{9,8},{10,9... | collective-permute-start | bytes 1966088 | tf_op jit(solution)/shard_map/ppermute | solution.py:26
  143.4 0.3 add_convert_fusion.1
  144.2 0.9 concatenate.3
  145.1 5.8 %collective-permute-start.22 = (bf16[40,2048]{1,0:T(8,128)(2,1)S(1)}, bf16[40,2048]{1,0:T(8,128)(2,1)S(1)}, u32[]{:S(2)}, u32[]{:S(2)}) collective-permute-start(bf16[40,2048]{1,0:T(8,128)(2,1)S(1)} %get-tuple-element.45), channel_id=1, source_target_pairs={{0,56},{4,60},{8,32},{12,36},{16,40},{20,44},{24,48},{28,52},{32,8... | collective-permute-start | bytes 491528 | tf_op jit(solution)/shard_map/ppermute | solution.py:382
  150.9 0.8 collective-permute-start.24
  151.8 6.5 %collective-permute-start.26 = (bf16[40,2048]{1,0:T(8,128)(2,1)S(1)}, bf16[40,2048]{1,0:T(8,128)(2,1)S(1)}, u32[]{:S(2)}, u32[]{:S(2)}) collective-permute-start(bf16[40,2048]{1,0:T(8,128)(2,1)S(1)} %get-tuple-element.43), channel_id=1, source_target_pairs={{0,48},{4,52},{8,56},{12,60},{16,32},{20,36},{24,40},{28,44},{32,8... | collective-permute-start | bytes 491528 | tf_op jit(solution)/shard_map/ppermute | solution.py:382
  158.4 1.6 add_convert_fusion
  160.0 0.6 collective-permute-start.21
  160.7 3.3 %collective-permute-start.23 = (bf16[40,2048]{1,0:T(8,128)(2,1)S(1)}, bf16[40,2048]{1,0:T(8,128)(2,1)S(1)}, u32[]{:S(2)}, u32[]{:S(2)}) collective-permute-start(bf16[40,2048]{1,0:T(8,128)(2,1)S(1)} %get-tuple-element.41), channel_id=1, source_target_pairs={{0,60},{4,56},{8,36},{12,32},{16,44},{20,40},{24,52},{28,48},{32,9... | collective-permute-start | bytes 491528 | tf_op jit(solution)/shard_map/ppermute | solution.py:382
  164.0 2.1 %collective-permute-start.25 = (bf16[40,2048]{1,0:T(8,128)(2,1)S(1)}, bf16[40,2048]{1,0:T(8,128)(2,1)S(1)}, u32[]{:S(2)}, u32[]{:S(2)}) collective-permute-start(bf16[40,2048]{1,0:T(8,128)(2,1)S(1)} %get-tuple-element.40), channel_id=1, source_target_pairs={{0,44},{4,40},{8,52},{12,48},{16,60},{20,56},{24,36},{28,32},{32,7... | collective-permute-start | bytes 491528 | tf_op jit(solution)/shard_map/ppermute | solution.py:382
  166.1 8.7 %collective-permute-done.26.refs_5_ = bf16[40,2048]{1,0:T(8,128)(2,1)S(1)} collective-permute-done((bf16[40,2048]{1,0:T(8,128)(2,1)S(1)}, bf16[40,2048]{1,0:T(8,128)(2,1)S(1)}, u32[]{:S(2)}, u32[]{:S(2)}) %collective-permute-start.26) | collective-permute-done | bytes 163872 | tf_op jit(solution)/shard_map/ppermute | solution.py:382
  174.8 6.0 %collective-permute-done.23.refs_2_ = bf16[40,2048]{1,0:T(8,128)(2,1)S(1)} collective-permute-done((bf16[40,2048]{1,0:T(8,128)(2,1)S(1)}, bf16[40,2048]{1,0:T(8,128)(2,1)S(1)}, u32[]{:S(2)}, u32[]{:S(2)}) %collective-permute-start.23) | collective-permute-done | bytes 163872 | tf_op jit(solution)/shard_map/ppermute | solution.py:382
  180.7 9.2 %collective-permute-done.27.refs_6_ = bf16[40,2048]{1,0:T(8,128)(2,1)S(1)} collective-permute-done((bf16[40,2048]{1,0:T(8,128)(2,1)S(1)}, bf16[40,2048]{1,0:T(8,128)(2,1)S(1)}, u32[]{:S(2)}, u32[]{:S(2)}) %collective-permute-start.27) | collective-permute-done | bytes 163872 | tf_op jit(solution)/shard_map/ppermute | solution.py:382
  189.9 1.4 finish.1
  (81 shorter events, 3.9 us)
Async XLA Ops:
  0.0 105.9 %copy-start = (bf16[1,2048,4]{1,2,0:T(4,128)(2,1)S(1)}, bf16[1,2048,4]{1,2,0:T(4,128)(2,1)}, u32[]{:S(2)}) copy-start(bf16[1,2048,4]{1,2,0:T(4,128)(2,1)} %param.19) | copy-start | bytes 49156
  0.0 14.8 %copy-start.9 = (s32[1,64,2]{1,2,0:T(2,128)S(1)}, s32[1,64,2]{1,2,0:T(2,128)}, u32[]{:S(2)}) copy-start(s32[1,64,2]{1,2,0:T(2,128)} %param.20) | copy-start | bytes 1540
  3.7 30.3 %copy-start.3 = (f32[64,32]{1,0:T(8,128)S(1)}, f32[64,32]{1,0:T(8,128)}, u32[]{:S(2)}) copy-start(f32[64,32]{1,0:T(8,128)} %get-tuple-element.23.cum_ref) | copy-start | bytes 24580
  3.7 23.8 %all-to-all-start = ((bf16[32,40,128]{2,1,0:T(8,128)(2,1)}), bf16[32,40,128]{2,1,0:T(8,128)(2,1)S(1)}, u32[]{:S(2)}, u32[]{:S(2)}) async-start(bf16[32,40,128]{2,1,0:T(8,128)(2,1)} %get-tuple-element.24), calls=%async_computation | async-start | bytes 655360 | tf_op jit(solution)/shard_map/all_to_all | solution.py:70
  28.3 16.2 %all-to-all-start.1 = ((bf16[32,32,128]{2,1,0:T(8,128)(2,1)}), bf16[32,32,128]{2,1,0:T(8,128)(2,1)S(1)}, u32[]{:S(2)}, u32[]{:S(2)}) async-start(bf16[32,32,128]{2,1,0:T(8,128)(2,1)} %prefix_states.1), calls=%async_computation.1 | async-start | bytes 524288 | tf_op jit(solution)/shard_map/all_to_all | solution.py:71
  34.1 1.0 copy-start.1
  34.1 0.9 copy-start.2
  34.1 0.9 copy-start.4
  34.1 0.9 copy-start.5
  34.4 4.4 %copy-start.10 = (s32[160]{0:T(256)S(1)}, s32[160]{0:T(256)}, u32[]{:S(2)}) copy-start(s32[160]{0:T(256)} %constant.54.clone.1) | copy-start | bytes 1924
  38.8 6.3 %copy-start.6 = (bf16[1,64,2048]{2,1,0:T(8,128)(2,1)S(1)}, bf16[1,64,2048]{2,1,0:T(8,128)(2,1)}, u32[]{:S(2)}) copy-start(bf16[1,64,2048]{2,1,0:T(8,128)(2,1)} %param.12) | copy-start | bytes 786436
  38.8 6.3 %copy-start.7 = (f32[1,2048]{1,0:T(1,128)S(1)}, f32[1,2048]{1,0:T(1,128)}, u32[]{:S(2)}) copy-start(f32[1,2048]{1,0:T(1,128)} %param.17) | copy-start | bytes 24580
  44.7 0.7 copy-start.8
  45.9 10.2 %collective-permute-start = (bf16[40,2048]{1,0:T(8,128)(2,1)S(1)}, bf16[40,2048]{1,0:T(8,128)(2,1)S(1)}, u32[]{:S(2)}, u32[]{:S(2)}) collective-permute-start(bf16[40,2048]{1,0:T(8,128)(2,1)S(1)} %get-tuple-element.48), channel_id=1, source_target_pairs={{0,8},{4,12},{8,16},{12,20},{16,24},{20,28},{24,0},{28,4},{1,9},{5... | collective-permute-start | bytes 491528 | tf_op jit(solution)/shard_map/ppermute | solution.py:30
  46.6 10.1 %collective-permute-start.1 = (bf16[40,2048]{1,0:T(8,128)(2,1)S(1)}, bf16[40,2048]{1,0:T(8,128)(2,1)S(1)}, u32[]{:S(2)}, u32[]{:S(2)}) collective-permute-start(bf16[40,2048]{1,0:T(8,128)(2,1)S(1)} %get-tuple-element.47), channel_id=1, source_target_pairs={{0,24},{4,28},{8,0},{12,4},{16,8},{20,12},{24,16},{28,20},{1,25},{... | collective-permute-start | bytes 491528 | tf_op jit(solution)/shard_map/ppermute | solution.py:30
  48.9 12.4 %collective-permute-start.2 = (bf16[40,2048]{1,0:T(8,128)(2,1)S(1)}, bf16[40,2048]{1,0:T(8,128)(2,1)S(1)}, u32[]{:S(2)}, u32[]{:S(2)}) collective-permute-start(bf16[40,2048]{1,0:T(8,128)(2,1)S(1)} %get-tuple-element.46), channel_id=1, source_target_pairs={{0,16},{4,20},{8,24},{12,28},{16,0},{20,4},{24,8},{28,12},{1,17},{... | collective-permute-start | bytes 491528 | tf_op jit(solution)/shard_map/ppermute | solution.py:30
  61.4 14.9 %collective-permute-start.3 = (bf16[160,2048]{1,0:T(8,128)(2,1)S(1)}, bf16[160,2048]{1,0:T(8,128)(2,1)S(1)}, u32[]{:S(2)}, u32[]{:S(2)}) collective-permute-start(bf16[160,2048]{1,0:T(8,128)(2,1)S(1)} %join.1.refs_0_), channel_id=1, source_target_pairs={{0,1},{1,2},{2,3},{3,0},{4,5},{5,6},{6,7},{7,4},{8,9},{9,10},{10,1... | collective-permute-start | bytes 1966088 | tf_op jit(solution)/shard_map/ppermute | solution.py:26
  61.7 14.7 %collective-permute-start.4 = (bf16[160,2048]{1,0:T(8,128)(2,1)S(1)}, bf16[160,2048]{1,0:T(8,128)(2,1)S(1)}, u32[]{:S(2)}, u32[]{:S(2)}) collective-permute-start(bf16[160,2048]{1,0:T(8,128)(2,1)S(1)} %join.1.refs_0_), channel_id=1, source_target_pairs={{0,3},{1,0},{2,1},{3,2},{4,7},{5,4},{6,5},{7,6},{8,11},{9,8},{10,9... | collective-permute-start | bytes 1966088 | tf_op jit(solution)/shard_map/ppermute | solution.py:26
  64.7 15.0 %collective-permute-start.12 = (bf16[160,2048]{1,0:T(8,128)(2,1)S(1)}, bf16[160,2048]{1,0:T(8,128)(2,1)S(1)}, u32[]{:S(2)}, u32[]{:S(2)}) collective-permute-start(bf16[160,2048]{1,0:T(8,128)(2,1)S(1)} %join.1.refs_0_), channel_id=1, source_target_pairs={{0,4},{4,0},{8,12},{12,8},{16,20},{20,16},{24,28},{28,24},{1,5},{5... | collective-permute-start | bytes 1966088 | tf_op jit(solution)/shard_map/ppermute | solution.py:30
  76.3 11.9 %collective-permute-start.5 = (bf16[80,2048]{1,0:T(8,128)(2,1)S(1)}, bf16[80,2048]{1,0:T(8,128)(2,1)S(1)}, u32[]{:S(2)}, u32[]{:S(2)}) collective-permute-start(bf16[80,2048]{1,0:T(8,128)(2,1)S(1)} %slice.91), channel_id=1, source_target_pairs={{0,1},{1,2},{2,3},{3,0},{4,5},{5,6},{6,7},{7,4},{8,9},{9,10},{10,1... | collective-permute-start | bytes 983048 | tf_op jit(solution)/shard_map/ppermute | solution.py:26
  76.4 11.7 %collective-permute-start.6 = (bf16[80,2048]{1,0:T(8,128)(2,1)S(1)}, bf16[80,2048]{1,0:T(8,128)(2,1)S(1)}, u32[]{:S(2)}, u32[]{:S(2)}) collective-permute-start(bf16[80,2048]{1,0:T(8,128)(2,1)S(1)} %slice.92), channel_id=1, source_target_pairs={{0,3},{1,0},{2,1},{3,2},{4,7},{5,4},{6,5},{7,6},{8,11},{9,8},{10,9... | collective-permute-start | bytes 983048 | tf_op jit(solution)/shard_map/ppermute | solution.py:26
  79.7 22.7 %collective-permute-start.13 = (bf16[160,2048]{1,0:T(8,128)(2,1)S(1)}, bf16[160,2048]{1,0:T(8,128)(2,1)S(1)}, u32[]{:S(2)}, u32[]{:S(2)}) collective-permute-start(bf16[160,2048]{1,0:T(8,128)(2,1)S(1)} %collective-permute-done.12.refs_0_), channel_id=1, source_target_pairs={{0,1},{1,2},{2,3},{3,0},{4,5},{5,6},{6,7},{7,4},{8,9},{9,10},{10,1... | collective-permute-start | bytes 1966088 | tf_op jit(solution)/shard_map/ppermute | solution.py:26
  79.7 22.9 %collective-permute-start.14 = (bf16[160,2048]{1,0:T(8,128)(2,1)S(1)}, bf16[160,2048]{1,0:T(8,128)(2,1)S(1)}, u32[]{:S(2)}, u32[]{:S(2)}) collective-permute-start(bf16[160,2048]{1,0:T(8,128)(2,1)S(1)} %collective-permute-done.12.refs_0_), channel_id=1, source_target_pairs={{0,3},{1,0},{2,1},{3,2},{4,7},{5,4},{6,5},{7,6},{8,11},{9,8},{10,9... | collective-permute-start | bytes 1966088 | tf_op jit(solution)/shard_map/ppermute | solution.py:26
  99.0 12.0 %collective-permute-start.9 = (bf16[80,2048]{1,0:T(8,128)(2,1)S(1)}, bf16[80,2048]{1,0:T(8,128)(2,1)S(1)}, u32[]{:S(2)}, u32[]{:S(2)}) collective-permute-start(bf16[80,2048]{1,0:T(8,128)(2,1)S(1)} %get-tuple-element.29), channel_id=1, source_target_pairs={{0,1},{1,2},{2,3},{3,0},{4,5},{5,6},{6,7},{7,4},{8,9},{9,10},{10,1... | collective-permute-start | bytes 983048 | tf_op jit(solution)/shard_map/ppermute | solution.py:26
  99.1 12.1 %collective-permute-start.7 = (bf16[80,2048]{1,0:T(8,128)(2,1)S(1)}, bf16[80,2048]{1,0:T(8,128)(2,1)S(1)}, u32[]{:S(2)}, u32[]{:S(2)}) collective-permute-start(bf16[80,2048]{1,0:T(8,128)(2,1)S(1)} %get-tuple-element.27), channel_id=1, source_target_pairs={{0,3},{1,0},{2,1},{3,2},{4,7},{5,4},{6,5},{7,6},{8,11},{9,8},{10,9... | collective-permute-start | bytes 983048 | tf_op jit(solution)/shard_map/ppermute | solution.py:26
  102.5 15.4 %collective-permute-start.15 = (bf16[80,2048]{1,0:T(8,128)(2,1)S(1)}, bf16[80,2048]{1,0:T(8,128)(2,1)S(1)}, u32[]{:S(2)}, u32[]{:S(2)}) collective-permute-start(bf16[80,2048]{1,0:T(8,128)(2,1)S(1)} %slice.94), channel_id=1, source_target_pairs={{0,1},{1,2},{2,3},{3,0},{4,5},{5,6},{6,7},{7,4},{8,9},{9,10},{10,1... | collective-permute-start | bytes 983048 | tf_op jit(solution)/shard_map/ppermute | solution.py:26
  102.6 15.3 %collective-permute-start.16 = (bf16[80,2048]{1,0:T(8,128)(2,1)S(1)}, bf16[80,2048]{1,0:T(8,128)(2,1)S(1)}, u32[]{:S(2)}, u32[]{:S(2)}) collective-permute-start(bf16[80,2048]{1,0:T(8,128)(2,1)S(1)} %slice.95), channel_id=1, source_target_pairs={{0,3},{1,0},{2,1},{3,2},{4,7},{5,4},{6,5},{7,6},{8,11},{9,8},{10,9... | collective-permute-start | bytes 983048 | tf_op jit(solution)/shard_map/ppermute | solution.py:26
  111.1 32.3 %collective-permute-start.10 = (bf16[160,2048]{1,0:T(8,128)(2,1)S(1)}, bf16[160,2048]{1,0:T(8,128)(2,1)S(1)}, u32[]{:S(2)}, u32[]{:S(2)}) collective-permute-start(bf16[160,2048]{1,0:T(8,128)(2,1)S(1)} %merge.5), channel_id=1, source_target_pairs={{0,1},{1,2},{2,3},{3,0},{4,5},{5,6},{6,7},{7,4},{8,9},{9,10},{10,1... | collective-permute-start | bytes 1966088 | tf_op jit(solution)/shard_map/ppermute | solution.py:26
  111.3 32.1 %collective-permute-start.8 = (bf16[160,2048]{1,0:T(8,128)(2,1)S(1)}, bf16[160,2048]{1,0:T(8,128)(2,1)S(1)}, u32[]{:S(2)}, u32[]{:S(2)}) collective-permute-start(bf16[160,2048]{1,0:T(8,128)(2,1)S(1)} %merge.4), channel_id=1, source_target_pairs={{0,3},{1,0},{2,1},{3,2},{4,7},{5,4},{6,5},{7,6},{8,11},{9,8},{10,9... | collective-permute-start | bytes 1966088 | tf_op jit(solution)/shard_map/ppermute | solution.py:26
  128.7 11.0 %collective-permute-start.19 = (bf16[80,2048]{1,0:T(8,128)(2,1)S(1)}, bf16[80,2048]{1,0:T(8,128)(2,1)S(1)}, u32[]{:S(2)}, u32[]{:S(2)}) collective-permute-start(bf16[80,2048]{1,0:T(8,128)(2,1)S(1)} %get-tuple-element.34), channel_id=1, source_target_pairs={{0,1},{1,2},{2,3},{3,0},{4,5},{5,6},{6,7},{7,4},{8,9},{9,10},{10,1... | collective-permute-start | bytes 983048 | tf_op jit(solution)/shard_map/ppermute | solution.py:26
  128.8 11.2 %collective-permute-start.17 = (bf16[80,2048]{1,0:T(8,128)(2,1)S(1)}, bf16[80,2048]{1,0:T(8,128)(2,1)S(1)}, u32[]{:S(2)}, u32[]{:S(2)}) collective-permute-start(bf16[80,2048]{1,0:T(8,128)(2,1)S(1)} %get-tuple-element.32), channel_id=1, source_target_pairs={{0,3},{1,0},{2,1},{3,2},{4,7},{5,4},{6,5},{7,6},{8,11},{9,8},{10,9... | collective-permute-start | bytes 983048 | tf_op jit(solution)/shard_map/ppermute | solution.py:26
  139.8 12.0 %collective-permute-start.20 = (bf16[160,2048]{1,0:T(8,128)(2,1)S(1)}, bf16[160,2048]{1,0:T(8,128)(2,1)}, u32[]{:S(2)}, u32[]{:S(2)}) collective-permute-start(bf16[160,2048]{1,0:T(8,128)(2,1)S(1)} %merge.7), channel_id=1, source_target_pairs={{0,1},{1,2},{2,3},{3,0},{4,5},{5,6},{6,7},{7,4},{8,9},{9,10},{10,1... | collective-permute-start | bytes 1966088 | tf_op jit(solution)/shard_map/ppermute | solution.py:26
  140.1 18.3 %collective-permute-start.18 = (bf16[160,2048]{1,0:T(8,128)(2,1)S(1)}, bf16[160,2048]{1,0:T(8,128)(2,1)}, u32[]{:S(2)}, u32[]{:S(2)}) collective-permute-start(bf16[160,2048]{1,0:T(8,128)(2,1)S(1)} %merge.6), channel_id=1, source_target_pairs={{0,3},{1,0},{2,1},{3,2},{4,7},{5,4},{6,5},{7,6},{8,11},{9,8},{10,9... | collective-permute-start | bytes 1966088 | tf_op jit(solution)/shard_map/ppermute | solution.py:26
  145.1 29.7 %collective-permute-start.11 = (f32[64,2304]{1,0:T(8,128)}, f32[64,2304]{1,0:T(8,128)S(1)}, u32[]{:S(2)}, u32[]{:S(2)}) collective-permute-start(f32[64,2304]{1,0:T(8,128)} %concatenate.3), channel_id=1, source_target_pairs={{0,32},{4,36},{8,40},{12,44},{16,48},{20,52},{24,56},{28,60},{32,6... | collective-permute-start | bytes 1769480 | tf_op jit(solution)/shard_map/ppermute | solution.py:382
  145.1 15.6 %collective-permute-start.22 = (bf16[40,2048]{1,0:T(8,128)(2,1)S(1)}, bf16[40,2048]{1,0:T(8,128)(2,1)S(1)}, u32[]{:S(2)}, u32[]{:S(2)}) collective-permute-start(bf16[40,2048]{1,0:T(8,128)(2,1)S(1)} %get-tuple-element.45), channel_id=1, source_target_pairs={{0,56},{4,60},{8,32},{12,36},{16,40},{20,44},{24,48},{28,52},{32,8... | collective-permute-start | bytes 491528 | tf_op jit(solution)/shard_map/ppermute | solution.py:382
  150.9 13.0 %collective-permute-start.24 = (bf16[40,2048]{1,0:T(8,128)(2,1)S(1)}, bf16[40,2048]{1,0:T(8,128)(2,1)S(1)}, u32[]{:S(2)}, u32[]{:S(2)}) collective-permute-start(bf16[40,2048]{1,0:T(8,128)(2,1)S(1)} %get-tuple-element.44), channel_id=1, source_target_pairs={{0,40},{4,44},{8,48},{12,52},{16,56},{20,60},{24,32},{28,36},{32,7... | collective-permute-start | bytes 491528 | tf_op jit(solution)/shard_map/ppermute | solution.py:382
  151.8 22.9 %collective-permute-start.26 = (bf16[40,2048]{1,0:T(8,128)(2,1)S(1)}, bf16[40,2048]{1,0:T(8,128)(2,1)S(1)}, u32[]{:S(2)}, u32[]{:S(2)}) collective-permute-start(bf16[40,2048]{1,0:T(8,128)(2,1)S(1)} %get-tuple-element.43), channel_id=1, source_target_pairs={{0,48},{4,52},{8,56},{12,60},{16,32},{20,36},{24,40},{28,44},{32,8... | collective-permute-start | bytes 491528 | tf_op jit(solution)/shard_map/ppermute | solution.py:382
  160.0 14.7 %collective-permute-start.21 = (bf16[40,2048]{1,0:T(8,128)(2,1)S(1)}, bf16[40,2048]{1,0:T(8,128)(2,1)S(1)}, u32[]{:S(2)}, u32[]{:S(2)}) collective-permute-start(bf16[40,2048]{1,0:T(8,128)(2,1)S(1)} %get-tuple-element.42), channel_id=1, source_target_pairs={{0,36},{4,32},{8,44},{12,40},{16,52},{20,48},{24,60},{28,56},{32,6... | collective-permute-start | bytes 491528 | tf_op jit(solution)/shard_map/ppermute | solution.py:382
  160.7 20.0 %collective-permute-start.23 = (bf16[40,2048]{1,0:T(8,128)(2,1)S(1)}, bf16[40,2048]{1,0:T(8,128)(2,1)S(1)}, u32[]{:S(2)}, u32[]{:S(2)}) collective-permute-start(bf16[40,2048]{1,0:T(8,128)(2,1)S(1)} %get-tuple-element.41), channel_id=1, source_target_pairs={{0,60},{4,56},{8,36},{12,32},{16,44},{20,40},{24,52},{28,48},{32,9... | collective-permute-start | bytes 491528 | tf_op jit(solution)/shard_map/ppermute | solution.py:382
  164.0 16.8 %collective-permute-start.25 = (bf16[40,2048]{1,0:T(8,128)(2,1)S(1)}, bf16[40,2048]{1,0:T(8,128)(2,1)S(1)}, u32[]{:S(2)}, u32[]{:S(2)}) collective-permute-start(bf16[40,2048]{1,0:T(8,128)(2,1)S(1)} %get-tuple-element.40), channel_id=1, source_target_pairs={{0,44},{4,40},{8,52},{12,48},{16,60},{20,56},{24,36},{28,32},{32,7... | collective-permute-start | bytes 491528 | tf_op jit(solution)/shard_map/ppermute | solution.py:382
  174.8 15.2 %collective-permute-start.27 = (bf16[40,2048]{1,0:T(8,128)(2,1)S(1)}, bf16[40,2048]{1,0:T(8,128)(2,1)S(1)}, u32[]{:S(2)}, u32[]{:S(2)}) collective-permute-start(bf16[40,2048]{1,0:T(8,128)(2,1)S(1)} %get-tuple-element.39), channel_id=1, source_target_pairs={{0,52},{4,48},{8,60},{12,56},{16,36},{20,32},{24,44},{28,40},{32,8... | collective-permute-start | bytes 491528 | tf_op jit(solution)/shard_map/ppermute | solution.py:382

commit v3 on v1

--- a/solution.py
+++ b/solution.py
@@ -61,6 +61,7 @@
         out_shape=jax.ShapeDtypeStruct((NZ * NY, 32, 128), jnp.bfloat16),
         in_specs=[pl.BlockSpec(memory_space=pltpu.VMEM)],
         out_specs=pl.BlockSpec(memory_space=pltpu.VMEM),
+        compiler_params=pltpu.CompilerParams(vmem_limit_bytes=4 * 2**20),
         name="prefix_states",
     )(pltpu.with_memory_space_constraint(arrived, pltpu.VMEM))
 
@@ -203,6 +204,7 @@
             transcendentals=seq_len * seq_len * HEADS,
             bytes_accessed=8 * seq_len * features,
         ),
+        compiler_params=pltpu.CompilerParams(vmem_limit_bytes=10 * 2**20),
         name="within",
     )(normed, maps, step_size, cumulative, skip_gain[None])
     c_rows = maps[:, STATE:] / math.sqrt(STATE)
@@ -212,10 +214,10 @@
     return inputs.astype(jnp.float32) + rms_scale(within + carried_part, mixed_gain)
 
 
-def expert_kernel(sizes, tile, out_tile, *refs):
-    n = len(sizes)
-    pieces, (gate, up, down), outs = refs[:n], refs[n : n + 3], refs[n + 3 : 2 * n + 3]
-    rows, gate_up, downs, hidden, sem_in, sem_down = refs[2 * n + 3 :]
+def expert_kernel(sizes, out_sizes, tile, out_tile, *refs):
+    n, scratch = len(sizes), len(refs) - 6
+    pieces, (gate, up, down), outs = refs[:n], refs[n : n + 3], refs[n + 3 : scratch]
+    rows, gate_up, downs, hidden, sem_in, sem_down = refs[scratch:]
     tiles, out_tiles = gate_up.shape[0], downs.shape[0]
 
     def copies(i):
@@ -236,11 +238,10 @@
             sem_down.at[j],
         )
 
-    for i in range(tiles):
+    ahead = 3
+    for i in range(ahead):
         for copy in copies(i):
             copy.start()
-    for j in range(out_tiles):
-        down_copy(j).start()
     at = 0
     for piece, size in zip(pieces, sizes):
 
@@ -256,6 +257,16 @@
     def first(i, carry):
         for copy in copies(i):
             copy.wait()
+
+        @pl.when(i + ahead < tiles)
+        def _():
+            for copy in copies(i + ahead):
+                copy.start()
+
+        @pl.when(i + out_tiles >= tiles)
+        def _():
+            down_copy(i + out_tiles - tiles).start()
+
         both = jnp.dot(rows[...], gate_up[i], preferred_element_type=jnp.float32)
         gate_pre, up_pre = both[:, :tile], both[:, tile:]
         hidden[:, pl.ds(pl.multiple_of(i * tile, tile), tile)] = (
@@ -270,7 +281,7 @@
         result = jnp.dot(hidden[...], downs[j], preferred_element_type=jnp.float32)
         result = result.astype(jnp.bfloat16)
         at = 0
-        for out, size in zip(outs, sizes):
+        for out, size in zip(outs, out_sizes):
             out[:, pl.ds(pl.multiple_of(j * out_tile, out_tile), out_tile)] = result[at : at + size]
             at += size
         return carry
@@ -283,13 +294,14 @@
     tile, out_tile = 128, 512
     sizes = tuple(piece.shape[0] for piece in pieces)
     total = sum(sizes)
+    out_sizes = (sizes[0] // 2,) * (2 * total // sizes[0])
     here = pl.BlockSpec(memory_space=pltpu.VMEM)
     away = pl.BlockSpec(memory_space=pltpu.HBM)
     return pl.pallas_call(
-        functools.partial(expert_kernel, sizes, tile, out_tile),
-        out_shape=[jax.ShapeDtypeStruct((size, features), jnp.bfloat16) for size in sizes],
+        functools.partial(expert_kernel, sizes, out_sizes, tile, out_tile),
+        out_shape=[jax.ShapeDtypeStruct((size, features), jnp.bfloat16) for size in out_sizes],
         in_specs=[here] * len(sizes) + [away] * 3,
-        out_specs=[here] * len(sizes),
+        out_specs=[here] * len(out_sizes),
         scratch_shapes=[
             pltpu.VMEM((total, features), jnp.bfloat16),
             pltpu.VMEM((width // tile, features, 2 * tile), jnp.bfloat16),
@@ -328,12 +340,13 @@
         out_shape=jax.ShapeDtypeStruct((rows * len(blocks), features), blocks[0].dtype),
         in_specs=[here] * len(blocks),
         out_specs=here,
+        compiler_params=pltpu.CompilerParams(vmem_limit_bytes=6 * 2**20),
         name="join",
     )(*(pltpu.with_memory_space_constraint(block, pltpu.VMEM) for block in blocks))
 
 
-def added(one, other):
-    return (one.astype(jnp.float32) + other.astype(jnp.float32)).astype(jnp.bfloat16)
+def added(*parts):
+    return sum(part.astype(jnp.float32) for part in parts).astype(jnp.bfloat16)
 
 
 def onward(value, target):
@@ -383,6 +396,7 @@
         in_specs=[here] * (1 + len(answers)),
         out_specs=here,
         scratch_shapes=[pltpu.VMEM((len(answers) * CAP, features), jnp.bfloat16)],
+        compiler_params=pltpu.CompilerParams(vmem_limit_bytes=10 * 2**20),
         name="finish",
     )(*(pltpu.with_memory_space_constraint(value, pltpu.VMEM) for value in (kept, *answers)))
 
@@ -426,34 +440,41 @@
     even = joined(blocks)
     odd = along_z(even, lambda z: z ^ 1)
 
-    sums = []
+    sums, fars = [], None
     for own in (even, odd):
         half = own.shape[0] // 2
         left = along_y(own, 1)
         right = along_y(own, -1)
-        far_a = along_y(left[:half], 1)
-        far_b = along_y(right[half:], -1)
-        o_own, o_left, o_right, o_far_a, o_far_b = expert_rows(
+        if fars is None:
+            far_a = along_y(left[:half], 1)
+            far_b = along_y(right[half:], -1)
+            fars = (far_a, far_b)
+        else:
+            far_a = along_z(fars[0], lambda z: z ^ 1)
+            far_b = along_z(fars[1], lambda z: z ^ 1)
+        own_a, own_b, left_a, left_b, right_a, right_b, far_a, far_b = expert_rows(
             (own, left, right, far_a, far_b), gate_part, up_part, down_part
         )
-        mid_a = along_y(o_far_a, -1)
-        mid_b = along_y(o_far_b, 1)
-        to_left = jnp.concatenate([added(o_left[:half], mid_a), o_left[half:]], axis=0)
-        to_right = jnp.concatenate([o_right[:half], added(o_right[half:], mid_b)], axis=0)
-        from_left = along_y(to_left, -1)
-        from_right = along_y(to_right, 1)
-        total = o_own.astype(jnp.float32) + from_left.astype(jnp.float32)
-        sums.append((total + from_right.astype(jnp.float32)).astype(jnp.bfloat16))
-
-    own_part = residual + weighted_rows(combine[:, :CAP], sums[0][:CAP])
+        mid_a = along_y(far_a, -1)
+        mid_b = along_y(far_b, 1)
+        early_left = along_y(left_b, -1)
+        early_right = along_y(right_a, 1)
+        left_a = added(left_a, mid_a)
+        right_b = added(right_b, mid_b)
+        back_left = along_y(left_a, -1)
+        back_right = along_y(right_b, 1)
+        sums.append((added(own_a, back_left, early_right), added(own_b, early_left, back_right)))
+
+    own_part = residual + weighted_rows(combine[:, :CAP], sums[0][0][:CAP])
     spare = jnp.zeros((tok_rows, 96), jnp.float32)
     kept = onward(jnp.concatenate([own_part, combine, spare], axis=1), lambda z: z)
     answers = []
     for i, shift in enumerate(SHIFTS):
-        part = slice(i * CAP, (i + 1) * CAP)
+        part = slice(i % 2 * CAP, (i % 2 + 1) * CAP)
+        even, odd = sums[0][i // 2][part], sums[1][i // 2][part]
         if i:
-            answers.append(onward(sums[0][part], lambda z, by=shift: z - by))
-        answers.append(onward(sums[1][part], lambda z, by=shift: (z ^ 1) - by))
+            answers.append(onward(even, lambda z, by=shift: z - by))
+        answers.append(onward(odd, lambda z, by=shift: (z ^ 1) - by))
     return finished(kept, answers)
 
 

time: 204 us -> 206 us (level)
  the two profiles are of different devices: /device:TPU:65 before, /device:TPU:1 now
where the time goes in v3:
time: 206 us; the launch traced here: 205 us
  starting transfers between devices  85.9 us (42%)
  waiting for transfers between devices  72.8 us (35%)
  Pallas kernels  31.3 us (15%)
  other arithmetic  6.4 us (3%)
  local copies, waits for them, and re-layouts  5.79 us (3%)
  matrix products  2.4 us (1%)
    ppermute x8, starting transfers between devices, onward(): return lax.ppermute(value, ('section', 'wide_0'), pairs)  32.7 us
    ppermute x18, waiting for transfers between devices, along_y(): lax.ppermute(value, 'wide_1', [(y, (y + by) % NY) for y in range(NY)])  31.2 us
    pallas_call x2, Pallas kernels, expert_rows(): pl.pallas_call(functools.partial(expert_kernel, sizes, out_sizes, tile, o...  21.6 us
    ppermute x18, starting transfers between devices, along_y(): lax.ppermute(value, 'wide_1', [(y, (y + by) % NY) for y in range(NY)])  20.7 us
    ppermute x6, starting transfers between devices, along_z(): lax.ppermute(value, 'wide_0', [(z, target(z) % NZ) for z in range(NZ)])  15.4 us
    ppermute x8, waiting for transfers between devices, onward(): return lax.ppermute(value, ('section', 'wide_0'), pairs)  14.2 us
    all_to_all x1, starting transfers between devices, carried_states(): lax.all_to_all(payload, WIDE, split_axis=0, concat_axis=0, tiled=True)  12.2 us
    ppermute x6, waiting for transfers between devices, along_z(): lax.ppermute(value, 'wide_0', [(z, target(z) % NZ) for z in range(NZ)])  11.3 us
  transfers between devices with their start and end apart: 34, of which 14 were waited for; matrix products, arithmetic and copies ran while one was open for 6% of the time, Pallas kernels for 12%

profile of v3, /device:TPU:1, one launch (start us, length us, event | category | flops | bytes accessed | tf_op | source)
XLA Modules:
  0.0 205.2 jit_solution(14160608331489571042)
XLA Ops:
  0.0 3.7 %front.1 = (bf16[32,40,128]{2,1,0:T(8,128)(2,1)}, bf16[64,2048]{1,0:T(8,128)(2,1)}, f32[64,128]{1,0:T(8,128)}, f32[64,32]{1,0:T(8,128)}, f32[64,32]{1,0:T(8,128)}) custom-call(bf16[64,2048]{1,0:T(8,128)(2,1)} %bitcast.38, f32[1,2048]{1,0:T(1,128)} %gain_ref.1, bf16[160,2048]{1,0:T(8,128)(2,1)} %bitcast.41, f32[1,32]{1,0:T(1,128)} %rate_ref.1), custom_call_target="tpu_custom_call" | custom-call | tf_op jit(solution)/shard_map/front/pallas_call | solution.py:179
  3.8 12.2 %all-to-all-start = ((bf16[32,40,128]{2,1,0:T(8,128)(2,1)}), bf16[32,40,128]{2,1,0:T(8,128)(2,1)S(1)}, u32[]{:S(2)}, u32[]{:S(2)}) async-start(bf16[32,40,128]{2,1,0:T(8,128)(2,1)} %get-tuple-element.30), calls=%async_computation | async-start | bytes 655360 | tf_op jit(solution)/shard_map/all_to_all | solution.py:70
  17.5 11.2 %all-to-all-done.arrived_ref = bf16[32,40,128]{2,1,0:T(8,128)(2,1)S(1)} async-done(((bf16[32,40,128]{2,1,0:T(8,128)(2,1)}), bf16[32,40,128]{2,1,0:T(8,128)(2,1)S(1)}, u32[]{:S(2)}, u32[]{:S(2)}) %all-to-all-start) | async-done | bytes 327712 | tf_op jit(solution)/shard_map/all_to_all | solution.py:70
  28.7 0.8 prefix_states.1
  29.5 4.9 %all-to-all-start.1 = ((bf16[32,32,128]{2,1,0:T(8,128)(2,1)}), bf16[32,32,128]{2,1,0:T(8,128)(2,1)S(1)}, u32[]{:S(2)}, u32[]{:S(2)}) async-start(bf16[32,32,128]{2,1,0:T(8,128)(2,1)} %prefix_states.1), calls=%async_computation.1 | async-start | bytes 524288 | tf_op jit(solution)/shard_map/all_to_all | solution.py:71
  34.7 0.8 exp.13
  36.2 3.7 %within.1 = f32[64,2048]{1,0:T(8,128)S(1)} custom-call(bf16[64,2048]{1,0:T(8,128)(2,1)S(1)} %copy-done.1, f32[64,128]{1,0:T(8,128)S(1)} %copy-done.2, f32[64,32]{1,0:T(8,128)S(1)} %copy-done.4, f32[64,32]{1,0:T(8,128)S(1)} %copy-done.3, f32[1,32]{1,0:T(1,128)S(1)} %copy-done.5), custom_call_target="tpu_custom_call" | custom-call | flops 83886080 | bytes 1048576 | tf_op jit(solution)/shard_map/within/pallas_call | solution.py:193
  40.0 4.9 %all-to-all-done.1 = bf16[32,32,128]{2,1,0:T(8,128)(2,1)S(1)} async-done(((bf16[32,32,128]{2,1,0:T(8,128)(2,1)}), bf16[32,32,128]{2,1,0:T(8,128)(2,1)S(1)}, u32[]{:S(2)}, u32[]{:S(2)}) %all-to-all-start.1) | async-done | bytes 262176 | tf_op jit(solution)/shard_map/all_to_all | solution.py:71
  46.3 1.8 collective-permute-start
  48.1 1.8 collective-permute-start.1
  50.0 2.0 collective-permute-start.2
  51.9 1.5 collective-permute-done.refs_1_
  53.4 3.8 %collective-permute-done.1.refs_2_ = bf16[40,2048]{1,0:T(8,128)(2,1)S(1)} collective-permute-done((bf16[40,2048]{1,0:T(8,128)(2,1)S(1)}, bf16[40,2048]{1,0:T(8,128)(2,1)S(1)}, u32[]{:S(2)}, u32[]{:S(2)}) %collective-permute-start.1) | collective-permute-done | bytes 163872 | tf_op jit(solution)/shard_map/ppermute | solution.py:30
  57.2 6.1 %collective-permute-done.2.refs_3_ = bf16[40,2048]{1,0:T(8,128)(2,1)S(1)} collective-permute-done((bf16[40,2048]{1,0:T(8,128)(2,1)S(1)}, bf16[40,2048]{1,0:T(8,128)(2,1)S(1)}, u32[]{:S(2)}, u32[]{:S(2)}) %collective-permute-start.2) | collective-permute-done | bytes 163872 | tf_op jit(solution)/shard_map/ppermute | solution.py:30
  63.4 0.9 collective-permute-start.3
  64.3 1.8 collective-permute-start.4
  66.1 12.3 %collective-permute-done.3.refs_1_ = bf16[160,2048]{1,0:T(8,128)(2,1)S(1)} collective-permute-done((bf16[160,2048]{1,0:T(8,128)(2,1)S(1)}, bf16[160,2048]{1,0:T(8,128)(2,1)S(1)}, u32[]{:S(2)}, u32[]{:S(2)}) %collective-permute-start.3) | collective-permute-done | bytes 655392 | tf_op jit(solution)/shard_map/ppermute | solution.py:26
  78.6 2.7 %collective-permute-start.6 = (bf16[80,2048]{1,0:T(8,128)(2,1)S(1)}, bf16[80,2048]{1,0:T(8,128)(2,1)S(1)}, u32[]{:S(2)}, u32[]{:S(2)}) collective-permute-start(bf16[80,2048]{1,0:T(8,128)(2,1)S(1)} %slice.84), channel_id=1, source_target_pairs={{0,3},{1,0},{2,1},{3,2},{4,7},{5,4},{6,5},{7,6},{8,11},{9,8},{10,9... | collective-permute-start | bytes 983048 | tf_op jit(solution)/shard_map/ppermute | solution.py:26
  81.7 4.3 %collective-permute-start.11 = (bf16[160,2048]{1,0:T(8,128)(2,1)S(1)}, bf16[160,2048]{1,0:T(8,128)(2,1)S(1)}, u32[]{:S(2)}, u32[]{:S(2)}) collective-permute-start(bf16[160,2048]{1,0:T(8,128)(2,1)S(1)} %join.1.refs_0_), channel_id=1, source_target_pairs={{0,4},{4,0},{8,12},{12,8},{16,20},{20,16},{24,28},{28,24},{1,5},{5... | collective-permute-start | bytes 1966088 | tf_op jit(solution)/shard_map/ppermute | solution.py:30
  86.0 10.8 %expert_rows.2 = (bf16[80,2048]{1,0:T(8,128)(2,1)S(1)}, bf16[80,2048]{1,0:T(8,128)(2,1)S(1)}, bf16[80,2048]{1,0:T(8,128)(2,1)S(1)}, bf16[80,2048]{1,0:T(8,128)(2...) custom-call(bf16[160,2048]{1,0:T(8,128)(2,1)S(1)} %join.1.refs_0_, ...), custom_call_target="tpu_custom_call" | custom-call | flops 7046430720 | bytes 16252928 | tf_op jit(solution)/shard_map/expert_rows/pallas_call | solution.py:300
  96.8 2.6 %collective-permute-start.7 = (bf16[80,2048]{1,0:T(8,128)(2,1)S(1)}, bf16[80,2048]{1,0:T(8,128)(2,1)S(1)}, u32[]{:S(2)}, u32[]{:S(2)}) collective-permute-start(bf16[80,2048]{1,0:T(8,128)(2,1)S(1)} %get-tuple-element.33), channel_id=1, source_target_pairs={{0,3},{1,0},{2,1},{3,2},{4,7},{5,4},{6,5},{7,6},{8,11},{9,8},{10,9... | collective-permute-start | bytes 983048 | tf_op jit(solution)/shard_map/ppermute | solution.py:26
  99.6 2.7 %collective-permute-start.13 = (bf16[160,2048]{1,0:T(8,128)(2,1)S(1)}, bf16[160,2048]{1,0:T(8,128)(2,1)S(1)}, u32[]{:S(2)}, u32[]{:S(2)}) collective-permute-start(bf16[160,2048]{1,0:T(8,128)(2,1)S(1)} %collective-permute-done.11.refs_0_), channel_id=1, source_target_pairs={{0,3},{1,0},{2,1},{3,2},{4,7},{5,4},{6,5},{7,6},{8,11},{9,8},{10,9... | collective-permute-start | bytes 1966088 | tf_op jit(solution)/shard_map/ppermute | solution.py:26
  102.5 4.8 %collective-permute-start.14 = (bf16[80,2048]{1,0:T(8,128)(2,1)S(1)}, bf16[80,2048]{1,0:T(8,128)(2,1)S(1)}, u32[]{:S(2)}, u32[]{:S(2)}) collective-permute-start(bf16[80,2048]{1,0:T(8,128)(2,1)S(1)} %collective-permute-done.5.refs_3_), channel_id=1, source_target_pairs={{0,4},{4,0},{8,12},{12,8},{16,20},{20,16},{24,28},{28,24},{1,5},{5... | collective-permute-start | bytes 983048 | tf_op jit(solution)/shard_map/ppermute | solution.py:30
  108.1 3.9 %collective-permute-done.12.refs_1_ = bf16[160,2048]{1,0:T(8,128)(2,1)S(1)} collective-permute-done((bf16[160,2048]{1,0:T(8,128)(2,1)S(1)}, bf16[160,2048]{1,0:T(8,128)(2,1)S(1)}, u32[]{:S(2)}, u32[]{:S(2)}) %collective-permute-start.12) | collective-permute-done | bytes 655392 | tf_op jit(solution)/shard_map/ppermute | solution.py:26
  112.0 3.9 %collective-permute-done.13.refs_2_ = bf16[160,2048]{1,0:T(8,128)(2,1)S(1)} collective-permute-done((bf16[160,2048]{1,0:T(8,128)(2,1)S(1)}, bf16[160,2048]{1,0:T(8,128)(2,1)S(1)}, u32[]{:S(2)}, u32[]{:S(2)}) %collective-permute-start.13) | collective-permute-done | bytes 655392 | tf_op jit(solution)/shard_map/ppermute | solution.py:26
  115.9 3.1 %collective-permute-start.22 = (bf16[80,2048]{1,0:T(8,128)(2,1)S(1)}, bf16[80,2048]{1,0:T(8,128)(2,1)}, u32[]{:S(2)}, u32[]{:S(2)}) collective-permute-start(bf16[80,2048]{1,0:T(8,128)(2,1)S(1)} %get-tuple-element.40), channel_id=1, source_target_pairs={{0,3},{1,0},{2,1},{3,2},{4,7},{5,4},{6,5},{7,6},{8,11},{9,8},{10,9... | collective-permute-start | bytes 983048 | tf_op jit(solution)/shard_map/ppermute | solution.py:26
  119.2 10.8 %expert_rows.3 = (bf16[80,2048]{1,0:T(8,128)(2,1)S(1)}, bf16[80,2048]{1,0:T(8,128)(2,1)S(1)}, bf16[80,2048]{1,0:T(8,128)(2,1)S(1)}, bf16[80,2048]{1,0:T(8,128)(2...) custom-call(bf16[160,2048]{1,0:T(8,128)(2,1)S(1)} %collective-permut, ...), custom_call_target="tpu_custom_call" | custom-call | flops 7046430720 | bytes 16252928 | tf_op jit(solution)/shard_map/expert_rows/pallas_call | solution.py:300
  129.9 1.5 collective-permute-start.18
  131.4 1.3 collective-permute-start.16
  132.7 0.8 add_convert_fusion.3
  134.8 1.0 fusion.1
  135.9 1.9 concatenate.3
  138.5 3.2 %collective-permute-start.26 = (bf16[80,2048]{1,0:T(8,128)(2,1)S(1)}, bf16[80,2048]{1,0:T(8,128)(2,1)S(1)}, u32[]{:S(2)}, u32[]{:S(2)}) collective-permute-start(bf16[80,2048]{1,0:T(8,128)(2,1)S(1)} %get-tuple-element.44), channel_id=1, source_target_pairs={{0,3},{1,0},{2,1},{3,2},{4,7},{5,4},{6,5},{7,6},{8,11},{9,8},{10,9... | collective-permute-start | bytes 983048 | tf_op jit(solution)/shard_map/ppermute | solution.py:26
  141.7 1.1 add_convert_fusion.5
  142.7 4.6 %collective-permute-done.27 = bf16[80,2048]{1,0:T(8,128)(2,1)} collective-permute-done((bf16[80,2048]{1,0:T(8,128)(2,1)S(1)}, bf16[80,2048]{1,0:T(8,128)(2,1)}, u32[]{:S(2)}, u32[]{:S(2)}) %collective-permute-start.27) | collective-permute-done | bytes 327712 | tf_op jit(solution)/shard_map/ppermute | solution.py:26
  147.4 9.5 %collective-permute-start.10 = (f32[64,2304]{1,0:T(8,128)}, f32[64,2304]{1,0:T(8,128)S(1)}, u32[]{:S(2)}, u32[]{:S(2)}) collective-permute-start(f32[64,2304]{1,0:T(8,128)} %concatenate.3), channel_id=1, source_target_pairs={{0,32},{4,36},{8,40},{12,44},{16,48},{20,52},{24,56},{28,60},{32,6... | collective-permute-start | bytes 1769480 | tf_op jit(solution)/shard_map/ppermute | solution.py:359
  156.9 1.1 add_convert_fusion.1
  158.1 4.1 %collective-permute-start.20 = (bf16[40,2048]{1,0:T(8,128)(2,1)}, bf16[40,2048]{1,0:T(8,128)(2,1)S(1)}, u32[]{:S(2)}, u32[]{:S(2)}) collective-permute-start(bf16[40,2048]{1,0:T(8,128)(2,1)} %slice.87), channel_id=1, source_target_pairs={{0,56},{4,60},{8,32},{12,36},{16,40},{20,44},{24,48},{28,52},{32,8... | collective-permute-start | bytes 491528 | tf_op jit(solution)/shard_map/ppermute | solution.py:359
  162.2 1.2 add_convert_fusion.2
  163.5 3.5 %collective-permute-done.17 = bf16[80,2048]{1,0:T(8,128)(2,1)S(1)} collective-permute-done((bf16[80,2048]{1,0:T(8,128)(2,1)S(1)}, bf16[80,2048]{1,0:T(8,128)(2,1)S(1)}, u32[]{:S(2)}, u32[]{:S(2)}) %collective-permute-start.17) | collective-permute-done | bytes 327712 | tf_op jit(solution)/shard_map/ppermute | solution.py:26
  167.1 1.1 add_convert_fusion.4
  168.2 7.4 %collective-permute-start.30 = (bf16[40,2048]{1,0:T(8,128)(2,1)S(1)}, bf16[40,2048]{1,0:T(8,128)(2,1)S(1)}, u32[]{:S(2)}, u32[]{:S(2)}) collective-permute-start(bf16[40,2048]{1,0:T(8,128)(2,1)S(1)} %get-tuple-element.57), channel_id=1, source_target_pairs={{0,48},{4,52},{8,56},{12,60},{16,32},{20,36},{24,40},{28,44},{32,8... | collective-permute-start | bytes 491528 | tf_op jit(solution)/shard_map/ppermute | solution.py:359
  175.6 2.2 %collective-permute-done.28 = bf16[80,2048]{1,0:T(8,128)(2,1)S(1)} collective-permute-done((bf16[80,2048]{1,0:T(8,128)(2,1)S(1)}, bf16[80,2048]{1,0:T(8,128)(2,1)S(1)}, u32[]{:S(2)}, u32[]{:S(2)}) %collective-permute-start.28) | collective-permute-done | bytes 327712 | tf_op jit(solution)/shard_map/ppermute | solution.py:26
  177.9 7.1 %collective-permute-start.19 = (bf16[40,2048]{1,0:T(8,128)(2,1)S(1)}, bf16[40,2048]{1,0:T(8,128)(2,1)S(1)}, u32[]{:S(2)}, u32[]{:S(2)}) collective-permute-start(bf16[40,2048]{1,0:T(8,128)(2,1)S(1)} %get-tuple-element.60), channel_id=1, source_target_pairs={{0,36},{4,32},{8,44},{12,40},{16,52},{20,48},{24,60},{28,56},{32,6... | collective-permute-start | bytes 491528 | tf_op jit(solution)/shard_map/ppermute | solution.py:359
  185.2 4.4 %collective-permute-start.29 = (bf16[40,2048]{1,0:T(8,128)(2,1)S(1)}, bf16[40,2048]{1,0:T(8,128)(2,1)S(1)}, u32[]{:S(2)}, u32[]{:S(2)}) collective-permute-start(bf16[40,2048]{1,0:T(8,128)(2,1)S(1)} %get-tuple-element.56), channel_id=1, source_target_pairs={{0,44},{4,40},{8,52},{12,48},{16,60},{20,56},{24,36},{28,32},{32,7... | collective-permute-start | bytes 491528 | tf_op jit(solution)/shard_map/ppermute | solution.py:359
  189.6 9.0 %collective-permute-done.21.refs_2_ = bf16[40,2048]{1,0:T(8,128)(2,1)S(1)} collective-permute-done((bf16[40,2048]{1,0:T(8,128)(2,1)S(1)}, bf16[40,2048]{1,0:T(8,128)(2,1)S(1)}, u32[]{:S(2)}, u32[]{:S(2)}) %collective-permute-start.21) | collective-permute-done | bytes 163872 | tf_op jit(solution)/shard_map/ppermute | solution.py:359
  198.7 5.1 %collective-permute-done.31.refs_6_ = bf16[40,2048]{1,0:T(8,128)(2,1)S(1)} collective-permute-done((bf16[40,2048]{1,0:T(8,128)(2,1)S(1)}, bf16[40,2048]{1,0:T(8,128)(2,1)S(1)}, u32[]{:S(2)}, u32[]{:S(2)}) %collective-permute-start.31) | collective-permute-done | bytes 163872 | tf_op jit(solution)/shard_map/ppermute | solution.py:359
  203.8 1.4 finish.1
  (95 shorter events, 8.3 us)
Async XLA Ops:
  0.0 81.3 %copy-start = (bf16[1,2048,4]{1,2,0:T(4,128)(2,1)S(1)}, bf16[1,2048,4]{1,2,0:T(4,128)(2,1)}, u32[]{:S(2)}) copy-start(bf16[1,2048,4]{1,2,0:T(4,128)(2,1)} %param.19) | copy-start | bytes 49156
  0.0 40.0 %copy-start.12 = (s32[160]{0:T(256)S(1)}, s32[160]{0:T(256)}, u32[]{:S(2)}) copy-start(s32[160]{0:T(256)} %constant.54.clone.1) | copy-start | bytes 1924
  0.0 40.0 %copy-start.11 = (s32[1,64,2]{1,2,0:T(2,128)S(1)}, s32[1,64,2]{1,2,0:T(2,128)}, u32[]{:S(2)}) copy-start(s32[1,64,2]{1,2,0:T(2,128)} %param.20) | copy-start | bytes 1540
  0.0 36.2 %copy-start.5 = (f32[1,32]{1,0:T(1,128)S(1)}, f32[1,32]{1,0:T(1,128)}, u32[]{:S(2)}) copy-start(f32[1,32]{1,0:T(1,128)} %skip_ref.1) | copy-start | bytes 388
  3.8 32.4 %copy-start.1 = (bf16[64,2048]{1,0:T(8,128)(2,1)S(1)}, bf16[64,2048]{1,0:T(8,128)(2,1)}, u32[]{:S(2)}) copy-start(bf16[64,2048]{1,0:T(8,128)(2,1)} %get-tuple-element.26.normed_ref) | copy-start | bytes 786436
  3.8 32.4 %copy-start.2 = (f32[64,128]{1,0:T(8,128)S(1)}, f32[64,128]{1,0:T(8,128)}, u32[]{:S(2)}) copy-start(f32[64,128]{1,0:T(8,128)} %get-tuple-element.27.maps_ref) | copy-start | bytes 98308
  3.8 32.4 %copy-start.3 = (f32[64,32]{1,0:T(8,128)S(1)}, f32[64,32]{1,0:T(8,128)}, u32[]{:S(2)}) copy-start(f32[64,32]{1,0:T(8,128)} %get-tuple-element.29.cum_ref) | copy-start | bytes 24580
  3.8 32.4 %copy-start.4 = (f32[64,32]{1,0:T(8,128)S(1)}, f32[64,32]{1,0:T(8,128)}, u32[]{:S(2)}) copy-start(f32[64,32]{1,0:T(8,128)} %get-tuple-element.28.step_ref) | copy-start | bytes 24580
  3.8 24.9 %all-to-all-start = ((bf16[32,40,128]{2,1,0:T(8,128)(2,1)}), bf16[32,40,128]{2,1,0:T(8,128)(2,1)S(1)}, u32[]{:S(2)}, u32[]{:S(2)}) async-start(bf16[32,40,128]{2,1,0:T(8,128)(2,1)} %get-tuple-element.30), calls=%async_computation | async-start | bytes 655360 | tf_op jit(solution)/shard_map/all_to_all | solution.py:70
  17.1 28.3 %copy-start.6 = (bf16[1,64,2048]{2,1,0:T(8,128)(2,1)S(1)}, bf16[1,64,2048]{2,1,0:T(8,128)(2,1)}, u32[]{:S(2)}) copy-start(bf16[1,64,2048]{2,1,0:T(8,128)(2,1)} %param.12) | copy-start | bytes 786436
  17.1 28.3 %copy-start.8 = (f32[1,2048]{1,0:T(1,128)S(1)}, f32[1,2048]{1,0:T(1,128)}, u32[]{:S(2)}) copy-start(f32[1,2048]{1,0:T(1,128)} %param.17) | copy-start | bytes 24580
  29.5 16.3 %copy-start.10 = (f32[1,2048]{1,0:T(1,128)S(1)}, f32[1,2048]{1,0:T(1,128)}, u32[]{:S(2)}) copy-start(f32[1,2048]{1,0:T(1,128)} %param.18) | copy-start | bytes 24580
  29.5 15.4 %all-to-all-start.1 = ((bf16[32,32,128]{2,1,0:T(8,128)(2,1)}), bf16[32,32,128]{2,1,0:T(8,128)(2,1)S(1)}, u32[]{:S(2)}, u32[]{:S(2)}) async-start(bf16[32,32,128]{2,1,0:T(8,128)(2,1)} %prefix_states.1), calls=%async_computation.1 | async-start | bytes 524288 | tf_op jit(solution)/shard_map/all_to_all | solution.py:71
  46.3 7.1 %collective-permute-start = (bf16[40,2048]{1,0:T(8,128)(2,1)S(1)}, bf16[40,2048]{1,0:T(8,128)(2,1)S(1)}, u32[]{:S(2)}, u32[]{:S(2)}) collective-permute-start(bf16[40,2048]{1,0:T(8,128)(2,1)S(1)} %get-tuple-element.53), channel_id=1, source_target_pairs={{0,8},{4,12},{8,16},{12,20},{16,24},{20,28},{24,0},{28,4},{1,9},{5... | collective-permute-start | bytes 491528 | tf_op jit(solution)/shard_map/ppermute | solution.py:30
  48.1 9.1 %collective-permute-start.1 = (bf16[40,2048]{1,0:T(8,128)(2,1)S(1)}, bf16[40,2048]{1,0:T(8,128)(2,1)S(1)}, u32[]{:S(2)}, u32[]{:S(2)}) collective-permute-start(bf16[40,2048]{1,0:T(8,128)(2,1)S(1)} %get-tuple-element.52), channel_id=1, source_target_pairs={{0,24},{4,28},{8,0},{12,4},{16,8},{20,12},{24,16},{28,20},{1,25},{... | collective-permute-start | bytes 491528 | tf_op jit(solution)/shard_map/ppermute | solution.py:30
  50.0 13.3 %collective-permute-start.2 = (bf16[40,2048]{1,0:T(8,128)(2,1)S(1)}, bf16[40,2048]{1,0:T(8,128)(2,1)S(1)}, u32[]{:S(2)}, u32[]{:S(2)}) collective-permute-start(bf16[40,2048]{1,0:T(8,128)(2,1)S(1)} %get-tuple-element.51), channel_id=1, source_target_pairs={{0,16},{4,20},{8,24},{12,28},{16,0},{20,4},{24,8},{28,12},{1,17},{... | collective-permute-start | bytes 491528 | tf_op jit(solution)/shard_map/ppermute | solution.py:30
  63.4 15.1 %collective-permute-start.3 = (bf16[160,2048]{1,0:T(8,128)(2,1)S(1)}, bf16[160,2048]{1,0:T(8,128)(2,1)S(1)}, u32[]{:S(2)}, u32[]{:S(2)}) collective-permute-start(bf16[160,2048]{1,0:T(8,128)(2,1)S(1)} %join.1.refs_0_), channel_id=1, source_target_pairs={{0,1},{1,2},{2,3},{3,0},{4,5},{5,6},{6,7},{7,4},{8,9},{9,10},{10,1... | collective-permute-start | bytes 1966088 | tf_op jit(solution)/shard_map/ppermute | solution.py:26
  64.3 14.3 %collective-permute-start.4 = (bf16[160,2048]{1,0:T(8,128)(2,1)S(1)}, bf16[160,2048]{1,0:T(8,128)(2,1)S(1)}, u32[]{:S(2)}, u32[]{:S(2)}) collective-permute-start(bf16[160,2048]{1,0:T(8,128)(2,1)S(1)} %join.1.refs_0_), channel_id=1, source_target_pairs={{0,3},{1,0},{2,1},{3,2},{4,7},{5,4},{6,5},{7,6},{8,11},{9,8},{10,9... | collective-permute-start | bytes 1966088 | tf_op jit(solution)/shard_map/ppermute | solution.py:26
  78.5 7.5 %collective-permute-start.5 = (bf16[80,2048]{1,0:T(8,128)(2,1)S(1)}, bf16[80,2048]{1,0:T(8,128)(2,1)S(1)}, u32[]{:S(2)}, u32[]{:S(2)}) collective-permute-start(bf16[80,2048]{1,0:T(8,128)(2,1)S(1)} %slice.83), channel_id=1, source_target_pairs={{0,1},{1,2},{2,3},{3,0},{4,5},{5,6},{6,7},{7,4},{8,9},{9,10},{10,1... | collective-permute-start | bytes 983048 | tf_op jit(solution)/shard_map/ppermute | solution.py:26
  78.6 7.4 %collective-permute-start.6 = (bf16[80,2048]{1,0:T(8,128)(2,1)S(1)}, bf16[80,2048]{1,0:T(8,128)(2,1)S(1)}, u32[]{:S(2)}, u32[]{:S(2)}) collective-permute-start(bf16[80,2048]{1,0:T(8,128)(2,1)S(1)} %slice.84), channel_id=1, source_target_pairs={{0,3},{1,0},{2,1},{3,2},{4,7},{5,4},{6,5},{7,6},{8,11},{9,8},{10,9... | collective-permute-start | bytes 983048 | tf_op jit(solution)/shard_map/ppermute | solution.py:26
  81.7 17.7 %collective-permute-start.11 = (bf16[160,2048]{1,0:T(8,128)(2,1)S(1)}, bf16[160,2048]{1,0:T(8,128)(2,1)S(1)}, u32[]{:S(2)}, u32[]{:S(2)}) collective-permute-start(bf16[160,2048]{1,0:T(8,128)(2,1)S(1)} %join.1.refs_0_), channel_id=1, source_target_pairs={{0,4},{4,0},{8,12},{12,8},{16,20},{20,16},{24,28},{28,24},{1,5},{5... | collective-permute-start | bytes 1966088 | tf_op jit(solution)/shard_map/ppermute | solution.py:30
  96.8 10.5 %collective-permute-start.7 = (bf16[80,2048]{1,0:T(8,128)(2,1)S(1)}, bf16[80,2048]{1,0:T(8,128)(2,1)S(1)}, u32[]{:S(2)}, u32[]{:S(2)}) collective-permute-start(bf16[80,2048]{1,0:T(8,128)(2,1)S(1)} %get-tuple-element.33), channel_id=1, source_target_pairs={{0,3},{1,0},{2,1},{3,2},{4,7},{5,4},{6,5},{7,6},{8,11},{9,8},{10,9... | collective-permute-start | bytes 983048 | tf_op jit(solution)/shard_map/ppermute | solution.py:26
  99.3 12.7 %collective-permute-start.12 = (bf16[160,2048]{1,0:T(8,128)(2,1)S(1)}, bf16[160,2048]{1,0:T(8,128)(2,1)S(1)}, u32[]{:S(2)}, u32[]{:S(2)}) collective-permute-start(bf16[160,2048]{1,0:T(8,128)(2,1)S(1)} %collective-permute-done.11.refs_0_), channel_id=1, source_target_pairs={{0,1},{1,2},{2,3},{3,0},{4,5},{5,6},{6,7},{7,4},{8,9},{9,10},{10,1... | collective-permute-start | bytes 1966088 | tf_op jit(solution)/shard_map/ppermute | solution.py:26
  99.6 16.3 %collective-permute-start.13 = (bf16[160,2048]{1,0:T(8,128)(2,1)S(1)}, bf16[160,2048]{1,0:T(8,128)(2,1)S(1)}, u32[]{:S(2)}, u32[]{:S(2)}) collective-permute-start(bf16[160,2048]{1,0:T(8,128)(2,1)S(1)} %collective-permute-done.11.refs_0_), channel_id=1, source_target_pairs={{0,3},{1,0},{2,1},{3,2},{4,7},{5,4},{6,5},{7,6},{8,11},{9,8},{10,9... | collective-permute-start | bytes 1966088 | tf_op jit(solution)/shard_map/ppermute | solution.py:26
  102.4 32.4 %copy-start.7 = (f32[64,160]{1,0:T(8,128)}, f32[64,160]{1,0:T(8,128)S(1)}, u32[]{:S(2)}) copy-start(f32[64,160]{1,0:T(8,128)S(1)} %select_add_fusion) | copy-start | bytes 122884
  102.4 31.1 %collective-permute-start.9 = (bf16[80,2048]{1,0:T(8,128)(2,1)S(1)}, bf16[80,2048]{1,0:T(8,128)(2,1)S(1)}, u32[]{:S(2)}, u32[]{:S(2)}) collective-permute-start(bf16[80,2048]{1,0:T(8,128)(2,1)S(1)} %get-tuple-element.34), channel_id=1, source_target_pairs={{0,1},{1,2},{2,3},{3,0},{4,5},{5,6},{6,7},{7,4},{8,9},{9,10},{10,1... | collective-permute-start | bytes 983048 | tf_op jit(solution)/shard_map/ppermute | solution.py:26
  102.5 16.6 %collective-permute-start.14 = (bf16[80,2048]{1,0:T(8,128)(2,1)S(1)}, bf16[80,2048]{1,0:T(8,128)(2,1)S(1)}, u32[]{:S(2)}, u32[]{:S(2)}) collective-permute-start(bf16[80,2048]{1,0:T(8,128)(2,1)S(1)} %collective-permute-done.5.refs_3_), channel_id=1, source_target_pairs={{0,4},{4,0},{8,12},{12,8},{16,20},{20,16},{24,28},{28,24},{1,5},{5... | collective-permute-start | bytes 983048 | tf_op jit(solution)/shard_map/ppermute | solution.py:30
  107.3 11.9 %collective-permute-start.15 = (bf16[80,2048]{1,0:T(8,128)(2,1)S(1)}, bf16[80,2048]{1,0:T(8,128)(2,1)S(1)}, u32[]{:S(2)}, u32[]{:S(2)}) collective-permute-start(bf16[80,2048]{1,0:T(8,128)(2,1)S(1)} %collective-permute-done.6.refs_4_), channel_id=1, source_target_pairs={{0,4},{4,0},{8,12},{12,8},{16,20},{20,16},{24,28},{28,24},{1,5},{5... | collective-permute-start | bytes 983048 | tf_op jit(solution)/shard_map/ppermute | solution.py:30
  112.0 19.4 %collective-permute-start.23 = (bf16[80,2048]{1,0:T(8,128)(2,1)S(1)}, bf16[80,2048]{1,0:T(8,128)(2,1)S(1)}, u32[]{:S(2)}, u32[]{:S(2)}) collective-permute-start(bf16[80,2048]{1,0:T(8,128)(2,1)S(1)} %get-tuple-element.42), channel_id=1, source_target_pairs={{0,1},{1,2},{2,3},{3,0},{4,5},{5,6},{6,7},{7,4},{8,9},{9,10},{10,1... | collective-permute-start | bytes 983048 | tf_op jit(solution)/shard_map/ppermute | solution.py:26
  115.9 18.9 %copy-start.9 = (f32[1,2048]{1,0:T(1,128)S(1)}, f32[1,2048]{1,0:T(1,128)}, u32[]{:S(2)}) copy-start(f32[1,2048]{1,0:T(1,128)} %param.17) | copy-start | bytes 24580
  115.9 42.0 %collective-permute-start.22 = (bf16[80,2048]{1,0:T(8,128)(2,1)S(1)}, bf16[80,2048]{1,0:T(8,128)(2,1)}, u32[]{:S(2)}, u32[]{:S(2)}) collective-permute-start(bf16[80,2048]{1,0:T(8,128)(2,1)S(1)} %get-tuple-element.40), channel_id=1, source_target_pairs={{0,3},{1,0},{2,1},{3,2},{4,7},{5,4},{6,5},{7,6},{8,11},{9,8},{10,9... | collective-permute-start | bytes 983048 | tf_op jit(solution)/shard_map/ppermute | solution.py:26
  119.1 14.6 %collective-permute-start.8 = (bf16[80,2048]{1,0:T(8,128)(2,1)S(1)}, bf16[80,2048]{1,0:T(8,128)(2,1)S(1)}, u32[]{:S(2)}, u32[]{:S(2)}) collective-permute-start(bf16[80,2048]{1,0:T(8,128)(2,1)S(1)} %add_convert_fusion.7), channel_id=1, source_target_pairs={{0,3},{1,0},{2,1},{3,2},{4,7},{5,4},{6,5},{7,6},{8,11},{9,8},{10,9... | collective-permute-start | bytes 983048 | tf_op jit(solution)/shard_map/ppermute | solution.py:26
  129.9 33.5 %collective-permute-start.18 = (bf16[80,2048]{1,0:T(8,128)(2,1)S(1)}, bf16[80,2048]{1,0:T(8,128)(2,1)}, u32[]{:S(2)}, u32[]{:S(2)}) collective-permute-start(bf16[80,2048]{1,0:T(8,128)(2,1)S(1)} %get-tuple-element.38), channel_id=1, source_target_pairs={{0,1},{1,2},{2,3},{3,0},{4,5},{5,6},{6,7},{7,4},{8,9},{9,10},{10,1... | collective-permute-start | bytes 983048 | tf_op jit(solution)/shard_map/ppermute | solution.py:26
  131.4 7.1 %collective-permute-start.16 = (bf16[80,2048]{1,0:T(8,128)(2,1)S(1)}, bf16[80,2048]{1,0:T(8,128)(2,1)}, u32[]{:S(2)}, u32[]{:S(2)}) collective-permute-start(bf16[80,2048]{1,0:T(8,128)(2,1)S(1)} %get-tuple-element.37), channel_id=1, source_target_pairs={{0,3},{1,0},{2,1},{3,2},{4,7},{5,4},{6,5},{7,6},{8,11},{9,8},{10,9... | collective-permute-start | bytes 983048 | tf_op jit(solution)/shard_map/ppermute | solution.py:26
  133.5 24.5 %collective-permute-start.24 = (bf16[80,2048]{1,0:T(8,128)(2,1)}, bf16[80,2048]{1,0:T(8,128)(2,1)}, u32[]{:S(2)}, u32[]{:S(2)}) collective-permute-start(bf16[80,2048]{1,0:T(8,128)(2,1)} %add_convert_fusion.3), channel_id=1, source_target_pairs={{0,1},{1,2},{2,3},{3,0},{4,5},{5,6},{6,7},{7,4},{8,9},{9,10},{10,1... | collective-permute-start | bytes 983048 | tf_op jit(solution)/shard_map/ppermute | solution.py:26
  133.7 13.7 %collective-permute-start.27 = (bf16[80,2048]{1,0:T(8,128)(2,1)S(1)}, bf16[80,2048]{1,0:T(8,128)(2,1)}, u32[]{:S(2)}, u32[]{:S(2)}) collective-permute-start(bf16[80,2048]{1,0:T(8,128)(2,1)S(1)} %get-tuple-element.46), channel_id=1, source_target_pairs={{0,1},{1,2},{2,3},{3,0},{4,5},{5,6},{6,7},{7,4},{8,9},{9,10},{10,1... | collective-permute-start | bytes 983048 | tf_op jit(solution)/shard_map/ppermute | solution.py:26
  138.5 29.7 %collective-permute-start.26 = (bf16[80,2048]{1,0:T(8,128)(2,1)S(1)}, bf16[80,2048]{1,0:T(8,128)(2,1)S(1)}, u32[]{:S(2)}, u32[]{:S(2)}) collective-permute-start(bf16[80,2048]{1,0:T(8,128)(2,1)S(1)} %get-tuple-element.44), channel_id=1, source_target_pairs={{0,3},{1,0},{2,1},{3,2},{4,7},{5,4},{6,5},{7,6},{8,11},{9,8},{10,9... | collective-permute-start | bytes 983048 | tf_op jit(solution)/shard_map/ppermute | solution.py:26
  147.4 56.4 %collective-permute-start.10 = (f32[64,2304]{1,0:T(8,128)}, f32[64,2304]{1,0:T(8,128)S(1)}, u32[]{:S(2)}, u32[]{:S(2)}) collective-permute-start(f32[64,2304]{1,0:T(8,128)} %concatenate.3), channel_id=1, source_target_pairs={{0,32},{4,36},{8,40},{12,44},{16,48},{20,52},{24,56},{28,60},{32,6... | collective-permute-start | bytes 1769480 | tf_op jit(solution)/shard_map/ppermute | solution.py:359
  158.0 9.1 %collective-permute-start.17 = (bf16[80,2048]{1,0:T(8,128)(2,1)S(1)}, bf16[80,2048]{1,0:T(8,128)(2,1)S(1)}, u32[]{:S(2)}, u32[]{:S(2)}) collective-permute-start(bf16[80,2048]{1,0:T(8,128)(2,1)S(1)} %add_convert_fusion.5), channel_id=1, source_target_pairs={{0,3},{1,0},{2,1},{3,2},{4,7},{5,4},{6,5},{7,6},{8,11},{9,8},{10,9... | collective-permute-start | bytes 983048 | tf_op jit(solution)/shard_map/ppermute | solution.py:26
  158.1 27.0 %collective-permute-start.20 = (bf16[40,2048]{1,0:T(8,128)(2,1)}, bf16[40,2048]{1,0:T(8,128)(2,1)S(1)}, u32[]{:S(2)}, u32[]{:S(2)}) collective-permute-start(bf16[40,2048]{1,0:T(8,128)(2,1)} %slice.87), channel_id=1, source_target_pairs={{0,56},{4,60},{8,32},{12,36},{16,40},{20,44},{24,48},{28,52},{32,8... | collective-permute-start | bytes 491528 | tf_op jit(solution)/shard_map/ppermute | solution.py:359
  163.4 21.8 %collective-permute-start.25 = (bf16[40,2048]{1,0:T(8,128)(2,1)S(1)}, bf16[40,2048]{1,0:T(8,128)(2,1)S(1)}, u32[]{:S(2)}, u32[]{:S(2)}) collective-permute-start(bf16[40,2048]{1,0:T(8,128)(2,1)S(1)} %get-tuple-element.58), channel_id=1, source_target_pairs={{0,40},{4,44},{8,48},{12,52},{16,56},{20,60},{24,32},{28,36},{32,7... | collective-permute-start | bytes 491528 | tf_op jit(solution)/shard_map/ppermute | solution.py:359
  167.1 10.8 %collective-permute-start.28 = (bf16[80,2048]{1,0:T(8,128)(2,1)S(1)}, bf16[80,2048]{1,0:T(8,128)(2,1)S(1)}, u32[]{:S(2)}, u32[]{:S(2)}) collective-permute-start(bf16[80,2048]{1,0:T(8,128)(2,1)S(1)} %add_convert_fusion.1), channel_id=1, source_target_pairs={{0,1},{1,2},{2,3},{3,0},{4,5},{5,6},{6,7},{7,4},{8,9},{9,10},{10,1... | collective-permute-start | bytes 983048 | tf_op jit(solution)/shard_map/ppermute | solution.py:26
  168.2 21.4 %collective-permute-start.30 = (bf16[40,2048]{1,0:T(8,128)(2,1)S(1)}, bf16[40,2048]{1,0:T(8,128)(2,1)S(1)}, u32[]{:S(2)}, u32[]{:S(2)}) collective-permute-start(bf16[40,2048]{1,0:T(8,128)(2,1)S(1)} %get-tuple-element.57), channel_id=1, source_target_pairs={{0,48},{4,52},{8,56},{12,60},{16,32},{20,36},{24,40},{28,44},{32,8... | collective-permute-start | bytes 491528 | tf_op jit(solution)/shard_map/ppermute | solution.py:359
  177.9 11.7 %collective-permute-start.19 = (bf16[40,2048]{1,0:T(8,128)(2,1)S(1)}, bf16[40,2048]{1,0:T(8,128)(2,1)S(1)}, u32[]{:S(2)}, u32[]{:S(2)}) collective-permute-start(bf16[40,2048]{1,0:T(8,128)(2,1)S(1)} %get-tuple-element.60), channel_id=1, source_target_pairs={{0,36},{4,32},{8,44},{12,40},{16,52},{20,48},{24,60},{28,56},{32,6... | collective-permute-start | bytes 491528 | tf_op jit(solution)/shard_map/ppermute | solution.py:359
  185.1 13.6 %collective-permute-start.21 = (bf16[40,2048]{1,0:T(8,128)(2,1)S(1)}, bf16[40,2048]{1,0:T(8,128)(2,1)S(1)}, u32[]{:S(2)}, u32[]{:S(2)}) collective-permute-start(bf16[40,2048]{1,0:T(8,128)(2,1)S(1)} %get-tuple-element.59), channel_id=1, source_target_pairs={{0,60},{4,56},{8,36},{12,32},{16,44},{20,40},{24,52},{28,48},{32,9... | collective-permute-start | bytes 491528 | tf_op jit(solution)/shard_map/ppermute | solution.py:359
  185.2 13.5 %collective-permute-start.29 = (bf16[40,2048]{1,0:T(8,128)(2,1)S(1)}, bf16[40,2048]{1,0:T(8,128)(2,1)S(1)}, u32[]{:S(2)}, u32[]{:S(2)}) collective-permute-start(bf16[40,2048]{1,0:T(8,128)(2,1)S(1)} %get-tuple-element.56), channel_id=1, source_target_pairs={{0,44},{4,40},{8,52},{12,48},{16,60},{20,56},{24,36},{28,32},{32,7... | collective-permute-start | bytes 491528 | tf_op jit(solution)/shard_map/ppermute | solution.py:359
  189.6 14.2 %collective-permute-start.31 = (bf16[40,2048]{1,0:T(8,128)(2,1)S(1)}, bf16[40,2048]{1,0:T(8,128)(2,1)S(1)}, u32[]{:S(2)}, u32[]{:S(2)}) collective-permute-start(bf16[40,2048]{1,0:T(8,128)(2,1)S(1)} %get-tuple-element.55), channel_id=1, source_target_pairs={{0,52},{4,48},{8,60},{12,56},{16,36},{20,32},{24,44},{28,40},{32,8... | collective-permute-start | bytes 491528 | tf_op jit(solution)/shard_map/ppermute | solution.py:359
